TPU v7x, 32 devices: a whole 2x2x4 slice. The times are simulated.
32 devices in a mesh: dp: 4 (over y, core), fsdp: 2 (over x), seq: 4 (over z).
Axes of the slice: x: 2, y: 2, z: 4, core: 2. Of those that a mesh axis runs over, the one named last changes fastest.
Arguments:
- frames_in: float32 [8, 1536, 768], P(('dp', 'fsdp'), 'seq'), may hold values from -8 to 8
- cotangent: float32 [8, 1536, 768], P(('dp', 'fsdp'), 'seq'), may hold values from -6 to 6
- attention_weight: float32 [4, 768, 768], P(None, 'fsdp'), may hold values from -16 to 16
- expand_weight: float32 [768, 3072], P('fsdp'), may hold values from -0.21875 to 0.21875
- contract_weight: float32 [3072, 768], P('fsdp'), may hold values from -0.109375 to 0.109375
- vectors: float32 [12, 768], P(None, 'fsdp'), may hold values from -2 to 2
- first_attention: float32 [4, 768, 768], P(None, 'fsdp'), may hold values from -32 to 32
- first_expand: float32 [768, 3072], P('fsdp'), may hold values from -32 to 32
- first_contract: float32 [3072, 768], P('fsdp'), may hold values from -32 to 32
- first_vectors: float32 [12, 768], P(None, 'fsdp'), may hold values from -32 to 32
- second_attention: float32 [4, 768, 768], P(None, 'fsdp'), may hold values from 0.24576 to 4.9152
- second_expand: float32 [768, 3072], P('fsdp'), may hold values from 0.24576 to 4.9152
- second_contract: float32 [3072, 768], P('fsdp'), may hold values from 0.24576 to 4.9152
- second_vectors: float32 [12, 768], P(None, 'fsdp'), may hold values from 0.24576 to 4.9152
Outputs:
- frames_out: float32 [8, 1536, 768], P(('dp', 'fsdp'), 'seq')
- input_gradient: float32 [8, 1536, 768], P(('dp', 'fsdp'), 'seq')
- gradient_attention: float32 [4, 768, 768], P(None, 'fsdp')
- gradient_expand: float32 [768, 3072], P('fsdp')
- gradient_contract: float32 [3072, 768], P('fsdp')
- gradient_vectors: float32 [12, 768], P(None, 'fsdp')
- updated_attention: float32 [4, 768, 768], P(None, 'fsdp')
- updated_expand: float32 [768, 3072], P('fsdp')
- updated_contract: float32 [3072, 768], P('fsdp')
- updated_vectors: float32 [12, 768], P(None, 'fsdp')
- average_attention: float32 [4, 768, 768], P(None, 'fsdp')
- average_expand: float32 [768, 3072], P('fsdp')
- average_contract: float32 [3072, 768], P('fsdp')
- average_vectors: float32 [12, 768], P(None, 'fsdp')
- variance_attention: float32 [4, 768, 768], P(None, 'fsdp')
- variance_expand: float32 [768, 3072], P('fsdp')
- variance_contract: float32 [3072, 768], P('fsdp')
- variance_vectors: float32 [12, 768], P(None, 'fsdp')
All inputs are finite; a program needn't handle non-finite values.
Results may differ from a plain program's by a relative error of at most 0.0095.
The roundings to bfloat16 on the way count: a program that leaves them out, or rounds other values in their place, can miss the bound.
Values may be sent and summed in bfloat16 or wider, within the bound.
A program may use at most 320 MiB of HBM per device.

v0:
```python
import jax
import jax.numpy as jnp
from jax import lax
from jax.sharding import PartitionSpec as P

HEADS = 12


norm_eps = 1e-05
beta_one = 0.9
beta_two = 0.999
adam_eps = 1e-08
adam_count = 5.0
rate_matrix = 0.02
rate_vector = 0.1
decay_matrix = 0.1
score_scale = 0.125


def layer_norm(values, gain, offset):
    center = values - jnp.mean(values, axis=-1, keepdims=True)
    inverse = lax.rsqrt(jnp.mean(center * center, axis=-1, keepdims=True) + norm_eps)
    normed = center * inverse
    return (normed * gain + offset, normed, inverse)


def norm_back(upstream, normed, inverse, gain):
    scaled = upstream * gain
    inner = (
        scaled
        - jnp.mean(scaled, axis=-1, keepdims=True)
        - normed * jnp.mean(scaled * normed, axis=-1, keepdims=True)
    )
    return (inverse * inner, jnp.sum(upstream * normed, axis=0), jnp.sum(upstream, axis=0))


def gelu_exact(values):
    return 0.5 * values * (1.0 + lax.erf(values * 0.7071067811865476))


def gelu_slope(values):
    return (
        0.5 * (1.0 + lax.erf(values * 0.7071067811865476))
        + values * jnp.exp(-0.5 * values * values) * 0.3989422804014327
    )


def product_nt(left, right):
    return lax.dot_general(
        left, right, (((1,), (1,)), ((), ())), preferred_element_type=jnp.float32
    )


def product_tn(left, right):
    return lax.dot_general(
        left, right, (((0,), (0,)), ((), ())), preferred_element_type=jnp.float32
    )


def split_heads(matrix):
    return jnp.transpose(matrix.reshape(matrix.shape[0], HEADS, -1), (1, 0, 2))


def join_heads(stacked):
    return jnp.transpose(stacked, (1, 0, 2)).reshape(stacked.shape[1], -1)


def head_forward(operands):
    queries, key_rows, value_rows = operands
    scores = product_nt(queries, key_rows) * score_scale
    largest = jnp.max(scores, axis=-1, keepdims=True)
    totals = jnp.sum(jnp.exp(scores - largest), axis=-1, keepdims=True)
    log_total = largest + jnp.log(totals)
    weights = jnp.exp(scores - log_total).astype(jnp.bfloat16)
    return (jnp.dot(weights, value_rows, preferred_element_type=jnp.float32), log_total[:, 0])


def head_backward(operands):
    queries, key_rows, value_rows, upstream, log_total = operands
    scores = product_nt(queries, key_rows) * score_scale
    probs = jnp.exp(scores - log_total[:, None])
    weights = probs.astype(jnp.bfloat16)
    slopes = product_nt(upstream, value_rows)
    value_grad = product_tn(weights, upstream)
    row_dot = jnp.sum(probs * slopes, axis=-1, keepdims=True)
    score_grad = (probs * (slopes - row_dot) * score_scale).astype(jnp.bfloat16)
    query_grad = jnp.dot(score_grad, key_rows, preferred_element_type=jnp.float32)
    key_grad = product_tn(score_grad, queries)
    return (query_grad, key_grad, value_grad)


def adam_update(weight, gradient, first, second, rate, decay):
    first_new = beta_one * first + (1.0 - beta_one) * gradient
    second_new = beta_two * second + (1.0 - beta_two) * gradient * gradient
    first_hat = first_new / (1.0 - beta_one**adam_count)
    second_hat = second_new / (1.0 - beta_two**adam_count)
    updated = weight - rate * (first_hat / (jnp.sqrt(second_hat) + adam_eps) + decay * weight)
    return (updated, first_new, second_new)


def on_device(
    frames_in,
    cotangent,
    attention_weight,
    expand_weight,
    contract_weight,
    vectors,
    first_attention,
    first_expand,
    first_contract,
    first_vectors,
    second_attention,
    second_expand,
    second_contract,
    second_vectors,
):
    shards = (
        attention_weight.astype(jnp.bfloat16),
        expand_weight.astype(jnp.bfloat16),
        contract_weight.astype(jnp.bfloat16),
        vectors.astype(jnp.bfloat16),
    )
    working = (
        lax.all_gather(shards[0], "fsdp", axis=1, tiled=True),
        lax.all_gather(shards[1], "fsdp", axis=0, tiled=True),
        lax.all_gather(shards[2], "fsdp", axis=0, tiled=True),
        lax.all_gather(shards[3], "fsdp", axis=1, tiled=True),
    )
    attention_bf, expand_bf, contract_bf, vector_bf = working
    vector_work = vector_bf.astype(jnp.float32)
    frames = frames_in[0]
    upstream = cotangent[0]
    width = frames.shape[1]
    bias_expand = vector_work[8:].reshape(-1)
    hidden_one, normed_one, inverse_one = layer_norm(frames, vector_work[0], vector_work[1])
    hidden_one = hidden_one.astype(jnp.bfloat16)
    queries = (
        jnp.dot(hidden_one, attention_bf[0], preferred_element_type=jnp.float32) + vector_work[2]
    ).astype(jnp.bfloat16)
    key_rows = jnp.dot(hidden_one, attention_bf[1], preferred_element_type=jnp.float32).astype(
        jnp.bfloat16
    )
    value_rows = (
        jnp.dot(hidden_one, attention_bf[2], preferred_element_type=jnp.float32) + vector_work[3]
    ).astype(jnp.bfloat16)
    all_keys = lax.all_gather(key_rows, "seq", axis=0, tiled=True)
    all_values = lax.all_gather(value_rows, "seq", axis=0, tiled=True)
    query_heads = split_heads(queries)
    key_heads = split_heads(all_keys)
    value_heads = split_heads(all_values)
    context_heads, log_total = lax.map(head_forward, (query_heads, key_heads, value_heads))
    context = join_heads(context_heads).astype(jnp.bfloat16)
    middle = (
        frames
        + jnp.dot(context, attention_bf[3], preferred_element_type=jnp.float32)
        + vector_work[4]
    )
    hidden_two, normed_two, inverse_two = layer_norm(middle, vector_work[5], vector_work[6])
    hidden_two = hidden_two.astype(jnp.bfloat16)
    expanded = jnp.dot(hidden_two, expand_bf, preferred_element_type=jnp.float32) + bias_expand
    activated = gelu_exact(expanded).astype(jnp.bfloat16)
    outputs = [
        middle
        + jnp.dot(activated, contract_bf, preferred_element_type=jnp.float32)
        + vector_work[7]
    ]
    working = (
        lax.all_gather(shards[0], "fsdp", axis=1, tiled=True),
        lax.all_gather(shards[1], "fsdp", axis=0, tiled=True),
        lax.all_gather(shards[2], "fsdp", axis=0, tiled=True),
        lax.all_gather(shards[3], "fsdp", axis=1, tiled=True),
    )
    attention_bf, expand_bf, contract_bf, vector_bf = working
    vector_work = vector_bf.astype(jnp.float32)
    upstream_bf = upstream.astype(jnp.bfloat16)
    grad_contract_w = product_tn(activated, upstream_bf)
    grad_expanded = product_nt(upstream_bf, contract_bf) * gelu_slope(expanded)
    grad_expanded_bf = grad_expanded.astype(jnp.bfloat16)
    grad_expand_w = product_tn(hidden_two, grad_expanded_bf)
    grad_hidden_two = product_nt(grad_expanded_bf, expand_bf)
    back_two, gain_two_grad, bias_two_grad = norm_back(
        grad_hidden_two, normed_two, inverse_two, vector_work[5]
    )
    grad_middle = upstream + back_two
    grad_middle_bf = grad_middle.astype(jnp.bfloat16)
    grad_output_w = product_tn(context, grad_middle_bf)
    grad_context = product_nt(grad_middle_bf, attention_bf[3]).astype(jnp.bfloat16)
    query_parts, key_parts, value_parts = lax.map(
        head_backward, (query_heads, key_heads, value_heads, split_heads(grad_context), log_total)
    )
    query_grad = join_heads(query_parts)
    key_grad = lax.psum_scatter(join_heads(key_parts), "seq", scatter_dimension=0, tiled=True)
    value_grad = lax.psum_scatter(join_heads(value_parts), "seq", scatter_dimension=0, tiled=True)
    query_grad_bf = query_grad.astype(jnp.bfloat16)
    key_grad_bf = key_grad.astype(jnp.bfloat16)
    value_grad_bf = value_grad.astype(jnp.bfloat16)
    grad_query_w = product_tn(hidden_one, query_grad_bf)
    grad_key_w = product_tn(hidden_one, key_grad_bf)
    grad_value_w = product_tn(hidden_one, value_grad_bf)
    grad_hidden_one = (
        product_nt(query_grad_bf, attention_bf[0])
        + product_nt(key_grad_bf, attention_bf[1])
        + product_nt(value_grad_bf, attention_bf[2])
    )
    back_one, gain_one_grad, bias_one_grad = norm_back(
        grad_hidden_one, normed_one, inverse_one, vector_work[0]
    )
    gradients_in = [grad_middle + back_one]
    small_rows = jnp.stack(
        [
            gain_one_grad,
            bias_one_grad,
            jnp.sum(query_grad, axis=0),
            jnp.sum(value_grad, axis=0),
            jnp.sum(grad_middle, axis=0),
            gain_two_grad,
            bias_two_grad,
            jnp.sum(upstream, axis=0),
        ]
    )
    grad_vectors = jnp.concatenate(
        [small_rows, jnp.sum(grad_expanded, axis=0).reshape(-1, width)], axis=0
    )
    grad_attention = jnp.stack([grad_query_w, grad_key_w, grad_value_w, grad_output_w])
    current = (grad_attention, grad_expand_w, grad_contract_w, grad_vectors)
    summed = lax.psum(current, ("dp", "seq"))
    owned = (
        lax.psum_scatter(summed[0], "fsdp", scatter_dimension=1, tiled=True),
        lax.psum_scatter(summed[1], "fsdp", scatter_dimension=0, tiled=True),
        lax.psum_scatter(summed[2], "fsdp", scatter_dimension=0, tiled=True),
        lax.psum_scatter(summed[3], "fsdp", scatter_dimension=1, tiled=True),
    )
    new_attention = adam_update(
        attention_weight, owned[0], first_attention, second_attention, rate_matrix, decay_matrix
    )
    new_expand = adam_update(
        expand_weight, owned[1], first_expand, second_expand, rate_matrix, decay_matrix
    )
    new_contract = adam_update(
        contract_weight, owned[2], first_contract, second_contract, rate_matrix, decay_matrix
    )
    new_vectors = adam_update(vectors, owned[3], first_vectors, second_vectors, rate_vector, 0.0)
    return (
        jnp.stack(outputs),
        jnp.stack(gradients_in),
        owned[0],
        owned[1],
        owned[2],
        owned[3],
        new_attention[0],
        new_expand[0],
        new_contract[0],
        new_vectors[0],
        new_attention[1],
        new_expand[1],
        new_contract[1],
        new_vectors[1],
        new_attention[2],
        new_expand[2],
        new_contract[2],
        new_vectors[2],
    )


def solution(mesh):
    in_specs = (
        P(("dp", "fsdp"), "seq", None),
        P(("dp", "fsdp"), "seq", None),
        P(None, "fsdp", None),
        P("fsdp", None),
        P("fsdp", None),
        P(None, "fsdp"),
        P(None, "fsdp", None),
        P("fsdp", None),
        P("fsdp", None),
        P(None, "fsdp"),
        P(None, "fsdp", None),
        P("fsdp", None),
        P("fsdp", None),
        P(None, "fsdp"),
    )
    out_specs = (
        P(("dp", "fsdp"), "seq", None),
        P(("dp", "fsdp"), "seq", None),
        P(None, "fsdp", None),
        P("fsdp", None),
        P("fsdp", None),
        P(None, "fsdp"),
        P(None, "fsdp", None),
        P("fsdp", None),
        P("fsdp", None),
        P(None, "fsdp"),
        P(None, "fsdp", None),
        P("fsdp", None),
        P("fsdp", None),
        P(None, "fsdp"),
        P(None, "fsdp", None),
        P("fsdp", None),
        P("fsdp", None),
        P(None, "fsdp"),
    )
    return jax.shard_map(
        on_device, mesh=mesh, in_specs=in_specs, out_specs=out_specs, check_vma=False
    )
```

profile of v0, /device:TPU:0, one launch (start us, length us, event | category | flops | bytes accessed | tf_op | source)
XLA Modules:
  0.0 1284.8 jit_solution(10163063939306772280)
XLA Ops:
  7.2 4.0 convert_element_type.91
  12.0 5.3 all_gather.22
  18.6 58.1 %all-gather.6.cloned.1.call-done = bf16[4,768,768]{2,1,0:T(8,128)(2,1)} async-done(((bf16[4,384,768]{2,1,0:T(8,128)(2,1)}), bf16[4,768,768]{2,1,0:T(8,128)(2,1)}) %all-gather.6.cloned.1.call-update) | async-done | bytes 4718608 | tf_op jit(solution)/shard_map/all_gather | solution.py:124
  76.7 2.7 convolution_convert_fusion.1
  79.5 2.7 fusion.51
  82.3 4.1 convert_element_type.99
  86.5 4.3 convert_element_type.101
  96.1 33.5 %all-gather.8.cloned.1.call-done = bf16[1536,768]{1,0:T(8,128)(2,1)} async-done(((bf16[384,768]{1,0:T(8,128)(2,1)}), bf16[1536,768]{1,0:T(8,128)(2,1)}) %all-gather.8.cloned.1.call-update) | async-done | bytes 2359312 | tf_op jit(solution)/shard_map/all_gather | solution.py:146
  129.6 2.8 copy.37
  132.5 3.9 copy.40
  136.4 44.2 %all-gather.10.cloned.1.call-done = bf16[1536,768]{1,0:T(8,128)(2,1)} async-done(((bf16[384,768]{1,0:T(8,128)(2,1)}), bf16[1536,768]{1,0:T(8,128)(2,1)}) %all-gather.10.cloned.1.call-update) | async-done | bytes 2359312 | tf_op jit(solution)/shard_map/all_gather | solution.py:147
  180.6 2.8 copy.38
  183.4 3.9 copy.41
  187.3 67.9 %while.28 = (s32[]{:T(128)}, bf16[12,384,64]{1,2,0:T(8,128)(2,1)}, f32[12,384]{1,0:T(8,128)}, bf16[12,384,64]{2,1,0:T(8,128)(2,1)}, bf16[12,1536,64]{2,1,0:T(8,128)(2,1)}, /*index=5*/bf16[12,1536,64]{2,1,0:T(8,128)(2,1)}) while((s32[]{:T(128)}, bf16[12,384,64]{1,2,0:T(8,128)(2,1)}, f32[12,384]{1,0:T(8,128)}, ...), condition=%wide.region_5.6_spmd.clone, body=%wide.region_2.5_spmd.sunk.clone | while | flops 154533504 | bytes 8079953 | solution.py:151
  189.5 2.3 fusion.138
  195.2 2.2 fusion.138
  200.8 2.2 fusion.138
  206.5 2.2 fusion.138
  212.1 2.2 fusion.138
  217.7 2.2 fusion.138
  223.4 2.2 fusion.138
  229.0 2.2 fusion.138
  234.6 2.2 fusion.138
  240.3 2.2 fusion.138
  245.9 2.2 fusion.138
  251.5 2.3 fusion.138
  255.2 2.4 fusion.75
  258.4 7.2 multiply_convert_fusion.1
  265.6 43.0 %all-gather.14.cloned.1.call-done = bf16[3072,768]{1,0:T(8,128)(2,1)} async-done(((bf16[1536,768]{1,0:T(8,128)(2,1)}), bf16[3072,768]{1,0:T(8,128)(2,1)}) %all-gather.14.cloned.1.call-update) | async-done | bytes 4718608 | tf_op jit(solution)/shard_map/all_gather | solution.py:126
  308.6 6.4 fusion.76
  315.0 2.9 multiply_reduce_fusion.1
  319.0 2.8 convolution_convert_fusion
  323.8 126.2 %while.29 = (s32[]{:T(128)}, f32[12,384,64]{1,2,0:T(8,128)}, f32[12,1536,64]{1,2,0:T(8,128)}, f32[12,1536,64]{1,2,0:T(8,128)}, bf16[12,384,64]{2,1,0:T(8,128)(2,...) while((s32[]{:T(128)}, f32[12,384,64]{1,2,0:T(8,128)}, ...), condition=%wide.region_12.13_spmd.clone, body=%wide.region_10.12_spmd.sunk.clone | while | flops 382795392 | bytes 20066920 | solution.py:188
  328.3 2.2 fusion.149
  338.8 2.2 fusion.149
  349.3 2.2 fusion.149
  359.8 2.2 fusion.149
  450.9 7.3 fusion.52
  458.3 8.3 fusion.77
  468.9 3.3 convolution_bitcast_fusion.6
  472.2 2.2 convolution_bitcast_fusion.3
  474.4 61.2 %reduce-scatter.9.cloned.1.call-done = f32[384,768]{0,1:T(8,128)} async-done(((f32[1536,768]{0,1:T(8,128)}), f32[384,768]{0,1:T(8,128)}) %reduce-scatter.9.cloned.1.call-update) | async-done | bytes 1179664 | tf_op jit(solution)/shard_map/reduce_scatter | solution.py:193
  535.5 3.7 convolution_bitcast_fusion.4
  539.2 85.0 %reduce-scatter.7.cloned.1.call-done = f32[384,768]{0,1:T(8,128)} async-done(((f32[1536,768]{0,1:T(8,128)}), f32[384,768]{0,1:T(8,128)}) %reduce-scatter.7.cloned.1.call-update) | async-done | bytes 1179664 | tf_op jit(solution)/shard_map/reduce_scatter | solution.py:192
  624.2 2.4 convolution_bitcast_fusion.5
  626.9 5.4 pad_maximum_fusion
  632.5 2.3 reduce_sum.186
  643.9 3.1 fusion.57
  649.1 2.9 convolution_add_fusion.2
  652.0 3.9 multiply_reduce_fusion.2
  657.0 2.8 concatenate.3
  660.1 77.6 %reduce-scatter.13.cloned.1.call-done = f32[384,3072]{1,0:T(8,128)} async-done(((f32[768,3072]{1,0:T(8,128)}), f32[384,3072]{1,0:T(8,128)}) %reduce-scatter.13.cloned.1.call-update) | async-done | bytes 4718608 | tf_op jit(solution)/shard_map/reduce_scatter | solution.py:229
  737.7 113.0 %reduce-scatter.15.cloned.1.call-done = f32[1536,768]{1,0:T(8,128)} async-done(((f32[3072,768]{1,0:T(8,128)}), f32[1536,768]{1,0:T(8,128)}) %reduce-scatter.15.cloned.1.call-update) | async-done | bytes 4718608 | tf_op jit(solution)/shard_map/reduce_scatter | solution.py:230
  850.7 112.8 %reduce-scatter.11.cloned.1.call-done = f32[4,384,768]{2,1,0:T(8,128)} async-done(((f32[4,768,768]{2,1,0:T(8,128)}), f32[4,384,768]{2,1,0:T(8,128)}) %reduce-scatter.11.cloned.1.call-update) | async-done | bytes 4718608 | tf_op jit(solution)/shard_map/reduce_scatter | solution.py:228
  963.6 6.2 fusion.49
  971.2 5.1 reduce-scatter.17.cloned.1.call-done
  976.3 64.6 %psum.35 = f32[12,384]{1,0:T(8,128)S(1)} all-reduce(f32[12,384]{1,0:T(8,128)} %reduce-scatter.17.cloned.1.call-done), channel_id=1, replica_groups=mesh['dp'=4,'fsdp'=2,'seq'=4] {'dp','seq'}, use_global_device_ids=true, to_apply=%region_32.33 | all-reduce | flops 4608 | bytes 36864 | tf_op jit(solution)/shard_map/psum | solution.py:226
  1041.6 197.4 %all-reduce.3.cloned.1.call-done = (f32[4,384,768]{2,1,0:T(8,128)}, f32[384,3072]{1,0:T(8,128)}, f32[1536,768]{1,0:T(8,128)}) async-done(((f32[4,384,768]{2,1,0:T(8,128)}, f32[384,3072]{1,0:T(8,128)}, f32[1536,768]{1,0:T(8,128)}), (f32[4,384,768]{2,1,0:T(8,128)}, f32[384,3072]{1,0:T(8,128)}, f32[1536,768]{1,0:T(8,128)})) %all-reduce.3.cloned.1.call-update) | async-done | bytes 14155792 | tf_op jit(solution)/shard_map/psum | solution.py:226
  1239.0 13.3 %multiply_subtract_fusion.2 = (f32[4,384,768]{2,1,0:T(8,128)}, f32[4,384,768]{2,1,0:T(8,128)}, f32[4,384,768]{2,1,0:T(8,128)}) fusion(f32[4,384,768]{2,1,0:T(8,128)} %param.20, f32[4,384,768]{2,1,0:T(8,128)} %get-tuple-element.385, f32[4,384,768]{2,1,0:T(8,128)} %param.24, f32[4,384,768]{2,1,0:T(8,128)} %param.28), kind=kLoop, calls=%fused_computation.67 | loop fusion | flops 17694720 | bytes 33030144 | tf_op jit(solution)/shard_map/sub | solution.py:97
  1252.7 9.7 multiply_subtract_fusion.1
  1262.6 8.9 multiply_subtract_fusion
  1271.4 2.2 copy.79
  1273.6 2.2 copy.80
  1275.8 2.2 copy.81
  (283 shorter events, 188.7 us)
Async XLA Ops:
  7.2 69.6 %all-gather.6.cloned.1.call-start = ((), (), s32[]{:S(2)}) async-start(), calls=%async_computation.6 | async-start | bytes 7077888 | tf_op jit(solution)/shard_map/all_gather | solution.py:124
  11.2 0.7 copy-start.12
  11.2 6.1 copy-start
  11.2 118.4 %all-gather.8.cloned.1.call-start = ((), (), s32[]{:S(2)}) async-start(), calls=%async_computation.7 | async-start | bytes 2949120 | tf_op jit(solution)/shard_map/all_gather | solution.py:146
  18.1 61.4 %copy-start.19 = (f32[768]{0:T(1024)}, f32[768]{0:T(1024)S(1)}, u32[]{:S(2)}) copy-start(f32[768]{0:T(1024)S(1)} %get-tuple-element.134) | copy-start | bytes 9220
  18.4 61.1 %copy-start.15 = (f32[384]{0:T(512)}, f32[384]{0:T(512)S(1)}, u32[]{:S(2)}) copy-start(f32[384]{0:T(512)S(1)} %add_rsqrt_fusion.1) | copy-start | bytes 4612
  18.6 73.7 %copy-start.10 = (bf16[384,768]{1,0:T(8,128)(2,1)}, bf16[384,768]{1,0:T(8,128)(2,1)S(1)}, u32[]{:S(2)}) copy-start(bf16[384,768]{1,0:T(8,128)(2,1)S(1)} %fusion.58) | copy-start | bytes 1769476
  79.5 101.1 %all-gather.10.cloned.1.call-start = ((), (), s32[]{:S(2)}) async-start(), calls=%async_computation.8 | async-start | bytes 2949120 | tf_op jit(solution)/shard_map/all_gather | solution.py:147
  82.3 176.1 %all-gather.12.cloned.1.call-start = ((), (), s32[]{:S(2)}) async-start(), calls=%async_computation.9 | async-start | bytes 7077888 | tf_op jit(solution)/shard_map/all_gather | solution.py:125
  86.4 222.2 %all-gather.14.cloned.1.call-start = ((), (), s32[]{:S(2)}) async-start(), calls=%async_computation.10 | async-start | bytes 7077888 | tf_op jit(solution)/shard_map/all_gather | solution.py:126
  90.8 444.7 %reduce-scatter.9.cloned.1.call-start = ((), (), s32[]{:S(2)}) async-start(), calls=%async_computation.12 | async-start | bytes 5898240 | tf_op jit(solution)/shard_map/reduce_scatter | solution.py:193
  187.3 67.9 %copy-start.25 = (f32[768]{0:T(1024)S(1)}, f32[768]{0:T(1024)}, u32[]{:S(2)}) copy-start(f32[768]{0:T(1024)} %get-tuple-element.131) | copy-start | bytes 9220
  257.5 0.9 copy-start.17
  258.4 50.2 %copy-start.3 = (f32[1,384,768]{2,1,0:T(8,128)S(1)}, f32[1,384,768]{2,1,0:T(8,128)}, u32[]{:S(2)}) copy-start(f32[1,384,768]{2,1,0:T(8,128)} %param.19) | copy-start | bytes 3538948
  308.6 6.4 copy-start.18
  308.6 6.4 copy-start.21
  308.6 6.4 copy-start.28
  315.0 2.9 copy-start.11
  315.0 2.9 copy-start.4
  450.1 174.2 %reduce-scatter.7.cloned.1.call-start = ((), (), s32[]{:S(2)}) async-start(), calls=%async_computation.11 | async-start | bytes 5898240 | tf_op jit(solution)/shard_map/reduce_scatter | solution.py:192
  450.8 286.9 %reduce-scatter.13.cloned.1.call-start = ((), (), s32[]{:S(2)}) async-start(), calls=%async_computation.14 | async-start | bytes 14155776 | tf_op jit(solution)/shard_map/reduce_scatter | solution.py:229
  458.2 392.5 %reduce-scatter.15.cloned.1.call-start = ((), (), s32[]{:S(2)}) async-start(), calls=%async_computation.15 | async-start | bytes 14155776 | tf_op jit(solution)/shard_map/reduce_scatter | solution.py:230
  466.6 496.9 %reduce-scatter.11.cloned.1.call-start = ((), (), s32[]{:S(2)}) async-start(), calls=%async_computation.13 | async-start | bytes 14155776 | tf_op jit(solution)/shard_map/reduce_scatter | solution.py:228
  466.6 5.5 copy-start.7
  468.1 0.8 copy-start.8
  472.2 63.4 %copy-start.16 = (f32[384]{0:T(512)S(1)}, f32[384]{0:T(512)}, u32[]{:S(2)}) copy-start(f32[384]{0:T(512)} %copy-done.15) | copy-start | bytes 4612
  472.2 63.4 %copy-start.20 = (f32[768]{0:T(1024)S(1)}, f32[768]{0:T(1024)}, u32[]{:S(2)}) copy-start(f32[768]{0:T(1024)} %copy-done.19) | copy-start | bytes 9220
  624.2 2.4 copy-start.5
  624.2 2.7 copy-start.6
  632.4 7.5 copy-start.24
  632.4 343.9 %reduce-scatter.17.cloned.1.call-start = ((), (), s32[]{:S(2)}) async-start(), calls=%async_computation.16 | async-start | bytes 73728 | tf_op jit(solution)/shard_map/reduce_scatter | solution.py:231
  649.1 2.9 copy-start.2
  659.8 579.2 %all-reduce.3.cloned.1.call-start = ((), (), s32[]{:S(2)}) async-start(), calls=%async_computation.17 | async-start | bytes 28311552 | tf_op jit(solution)/shard_map/psum | solution.py:226
  963.5 6.2 copy-start.27
  963.5 6.2 copy-start.26
  963.5 6.2 copy-start.9
  969.8 71.2 %copy-start.13 = (f32[12,384]{1,0:T(8,128)S(1)}, f32[12,384]{1,0:T(8,128)}, u32[]{:S(2)}) copy-start(f32[12,384]{1,0:T(8,128)} %param.23) | copy-start | bytes 55300
  969.8 71.2 %copy-start.22 = (f32[12,384]{1,0:T(8,128)S(1)}, f32[12,384]{1,0:T(8,128)}, u32[]{:S(2)}) copy-start(f32[12,384]{1,0:T(8,128)} %param.27) | copy-start | bytes 55300
  969.8 71.2 %copy-start.23 = (f32[12,384]{1,0:T(8,128)S(1)}, f32[12,384]{1,0:T(8,128)}, u32[]{:S(2)}) copy-start(f32[12,384]{1,0:T(8,128)} %param.31) | copy-start | bytes 55300
  969.8 282.6 %slice-start = ((s8[4718592]{0:T(1024)(128)(4,1)}), s8[524288]{0:T(1024)(128)(4,1)S(1)}, s32[]{:S(2)}) async-start(s8[4718592]{0:T(1024)(128)(4,1)} %bitcast.219), calls=%async_computation.18 | async-start | bytes 1048576
  1041.0 211.4 %copy-start.14 = (f32[12,384]{1,0:T(8,128)}, f32[12,384]{1,0:T(8,128)S(1)}, u32[]{:S(2)}) copy-start(f32[12,384]{1,0:T(8,128)S(1)} %psum.35) | copy-start | bytes 55300
  1239.0 13.4 %slice-start.1 = ((s8[4718592]{0:T(1024)(128)(4,1)}), s8[4194304]{0:T(1024)(128)(4,1)S(1)}, s32[]{:S(2)}) async-start(s8[4718592]{0:T(1024)(128)(4,1)} %bitcast.219), calls=%async_computation.19 | async-start | bytes 8388608
  1239.0 13.7 %copy-start.1 = (f32[384,3072]{1,0:T(8,128)S(1)}, f32[384,3072]{1,0:T(8,128)}, u32[]{:S(2)}) copy-start(f32[384,3072]{1,0:T(8,128)} %get-tuple-element.386) | copy-start | bytes 14155780
  1239.0 23.5 %slice-start.2 = ((s8[4718592]{0:T(1024)(128)(4,1)}), s8[4194304]{0:T(1024)(128)(4,1)S(1)}, s32[]{:S(2)}) async-start(s8[4718592]{0:T(1024)(128)(4,1)} %bitcast.221), calls=%async_computation.20 | async-start | bytes 8388608
  1239.0 23.5 %slice-start.4 = ((s8[4718592]{0:T(1024)(128)(4,1)}), s8[4194304]{0:T(1024)(128)(4,1)S(1)}, s32[]{:S(2)}) async-start(s8[4718592]{0:T(1024)(128)(4,1)} %bitcast.223), calls=%async_computation.22 | async-start | bytes 8388608
  1252.4 10.1 slice-start.3
  1252.4 10.2 slice-start.5
  1262.5 8.9 slice-start.6
  1262.5 8.9 slice-start.7
Sparse Core Ops, SparseCore 0:
  11.4 65.3 all-gather.5
  79.6 49.9 all-gather.7
  131.8 48.7 all-gather.9
  182.5 61.3 all-gather.11
  245.9 62.6 all-gather.13
  450.2 85.2 reduce-scatter.8
  538.4 85.7 reduce-scatter.6
  626.5 111.1 reduce-scatter.12
  740.0 110.6 reduce-scatter.14
  852.8 110.6 reduce-scatter.10
  966.3 9.9 reduce-scatter.16
  980.6 258.3 all-reduce.2
where the time goes:
time: 1290 us; the launch traced here: 1280 us
  waiting for transfers between devices  832 us (64%)
  matrix products  232 us (18%)
  other arithmetic  72.3 us (6%)
  blocking collectives  70 us (5%)
  local copies, waits for them, and re-layouts  63.7 us (5%)
  between operations  14.6 us (1%)
    psum x1, waiting for transfers between devices, on_device(): summed = lax.psum(current, ('dp', 'seq'))  197 us
    reduce_scatter x1, waiting for transfers between devices, on_device(): lax.psum_scatter(summed[2], 'fsdp', scatter_dimension=0, tiled=True)  113 us
    reduce_scatter x1, waiting for transfers between devices, on_device(): lax.psum_scatter(summed[0], 'fsdp', scatter_dimension=1, tiled=True)  113 us
    reduce_scatter x1, waiting for transfers between devices, on_device(): lax.psum_scatter(join_heads(key_parts), 'seq', scatter_dimension=0, tiled...  85 us
    dot_general x42, matrix products, product_nt(): lax.dot_general(left, right, (((1,), (1,)), ((), ())), preferred_element_...  81.8 us
    reduce_scatter x1, waiting for transfers between devices, on_device(): lax.psum_scatter(summed[1], 'fsdp', scatter_dimension=0, tiled=True)  77.6 us
    dot_general x30, matrix products, product_tn(): lax.dot_general(left, right, (((0,), (0,)), ((), ())), preferred_element_...  73.9 us
    psum x1, blocking collectives, on_device(): summed = lax.psum(current, ('dp', 'seq'))  64.6 us
  transfers between devices with their start and end apart: 12, of which 11 were waited for; matrix products, arithmetic and copies ran while one was open for 14% of the time, Pallas kernels for 0%

commit v1 on v0

v1 whole, which is shorter than its diff:
```python
import functools

import jax
import jax.numpy as jnp
from jax import lax
from jax.experimental import pallas as pl
from jax.experimental.pallas import tpu as pltpu
from jax.sharding import PartitionSpec as P

HEADS = 12
norm_eps = 1e-05
beta_one = 0.9
beta_two = 0.999
adam_eps = 1e-08
adam_count = 5.0
rate_matrix = 0.02
rate_vector = 0.1
decay_matrix = 0.1
score_scale = 0.125
VMEM_LIMIT = 60 << 20
MESH = pl.DeviceIdType.MESH
BF = jnp.bfloat16
F32 = jnp.float32


def nt(left, right):
    return lax.dot_general(left, right, (((1,), (1,)), ((), ())), preferred_element_type=F32)


def nn(left, right):
    return lax.dot_general(left, right, (((1,), (0,)), ((), ())), preferred_element_type=F32)


def tn(left, right):
    return lax.dot_general(left, right, (((0,), (0,)), ((), ())), preferred_element_type=F32)


def vmem():
    return pl.BlockSpec(memory_space=pltpu.VMEM)


def normalize(values):
    center = values - jnp.mean(values, axis=-1, keepdims=True)
    inverse = lax.rsqrt(jnp.mean(center * center, axis=-1, keepdims=True) + norm_eps)
    return center * inverse, inverse


def norm_back(upstream, normed, inverse, gain):
    scaled = upstream * gain
    inner = (
        scaled
        - jnp.mean(scaled, axis=-1, keepdims=True)
        - normed * jnp.mean(scaled * normed, axis=-1, keepdims=True)
    )
    return (inverse * inner, jnp.sum(upstream * normed, axis=0), jnp.sum(upstream, axis=0))


def gelu_exact(values):
    return 0.5 * values * (1.0 + lax.erf(values * 0.7071067811865476))


def gelu_slope(values):
    return (
        0.5 * (1.0 + lax.erf(values * 0.7071067811865476))
        + values * jnp.exp(-0.5 * values * values) * 0.3989422804014327
    )


def adam_update(weight, gradient, first, second, rate, decay):
    first_new = beta_one * first + (1.0 - beta_one) * gradient
    second_new = beta_two * second + (1.0 - beta_two) * gradient * gradient
    first_hat = first_new / (1.0 - beta_one**adam_count)
    second_hat = second_new / (1.0 - beta_two**adam_count)
    updated = weight - rate * (first_hat / (jnp.sqrt(second_hat) + adam_eps) + decay * weight)
    return (updated, first_new, second_new)


class Place:
    def __init__(self, sizes):
        self.nd, self.nf, self.ns = sizes
        self.nh = self.nd // 2
        self.dp = lax.axis_index("dp")
        self.x = lax.axis_index("fsdp")
        self.z = lax.axis_index("seq")
        self.core = lax.rem(self.dp, 2)
        self.hi = self.dp // 2

    def sibling(self):
        return {"dp": self.hi * 2 + 1 - self.core}

    def x_peer(self, k):
        return {"fsdp": lax.rem(self.x + k, self.nf)}

    def y_hi(self, k):
        return lax.rem(self.hi + k, self.nh)

    def y_peer(self, k):
        return {"dp": self.y_hi(k) * 2 + self.core}

    def z_at(self, k):
        return lax.rem(self.z + k + self.ns, self.ns)

    def z_peer(self, k):
        return {"seq": self.z_at(k)}

    def everyone(self):
        out = [self.sibling()]
        out += [self.x_peer(k) for k in range(1, self.nf)]
        out += [self.y_peer(k) for k in range(1, self.nh)]
        out += [self.z_peer(k) for k in range(1, self.ns)]
        return out

    def barrier(self):
        sem = pltpu.get_barrier_semaphore()
        peers = self.everyone()
        for peer in peers:
            pl.semaphore_signal(sem, inc=1, device_id=peer, device_id_type=MESH)
        pl.semaphore_wait(sem, len(peers))


def remote(src, dst, send, recv, peer):
    return pltpu.make_async_remote_copy(
        src_ref=src, dst_ref=dst, send_sem=send, recv_sem=recv, device_id=peer, device_id_type=MESH
    )


def gather_kernel(
    sizes, frames_ref, aw_ref, ew_ref, cw_ref, vec_ref,
    a_ref, e_ref, c_ref, v_ref, h_ref,
    xs, xr, ys, yr, s1s, s1r, s2s, s2r, vs, vr, rs, ls, hr,
):
    at = Place(sizes)
    nf, nh, ns = at.nf, at.nh, at.ns
    rows, width = frames_ref.shape
    shard = aw_ref.shape[1]
    half = shard // 2
    at.barrier()
    v_ref[at.x] = vec_ref[...].astype(BF)
    vec_copies = []
    for k in range(1, nf):
        copy = remote(v_ref.at[at.x], v_ref.at[at.x], vs.at[k], vr.at[k], at.x_peer(k))
        copy.start()
        vec_copies.append(copy)

    def view(chunk, j, hi, core):
        if chunk < 2:
            first, count = ((0, 3), (3, 1))[chunk]
            cols = width // nh
            return a_ref.at[
                pl.ds(first, count),
                pl.ds(pl.multiple_of(j * shard + core * half, 16), half),
                pl.ds(pl.multiple_of(hi * cols, 128), cols),
            ]
        if chunk == 2:
            cols = e_ref.shape[1] // nh
            return e_ref.at[
                pl.ds(pl.multiple_of(j * shard + core * half, 16), half),
                pl.ds(pl.multiple_of(hi * cols, 128), cols),
            ]
        cols = width // nh
        deep = c_ref.shape[0] // nf
        return c_ref.at[
            pl.ds(pl.multiple_of(j * deep + core * (deep // 2), 16), deep // 2),
            pl.ds(pl.multiple_of(hi * cols, 128), cols),
        ]

    own = pl.multiple_of(at.x * shard, 16)
    x_copies = {}

    def send_chunk(chunk):
        for k in range(1, nf):
            piece = view(chunk, at.x, at.hi, at.core)
            copy = remote(piece, piece, xs.at[chunk, k], xr.at[chunk, k], at.x_peer(k))
            copy.start()
            x_copies[chunk, k] = copy

    for u in range(3):
        a_ref[u, pl.ds(own, shard), :] = aw_ref[u].astype(BF)
    send_chunk(0)
    normed, _ = normalize(frames_ref[...])
    for copy in vec_copies:
        copy.wait()
    gain = jnp.concatenate([v_ref[j, 0:1, :] for j in range(nf)], axis=1).astype(F32)
    offset = jnp.concatenate([v_ref[j, 1:2, :] for j in range(nf)], axis=1).astype(F32)
    h_ref[pl.ds(pl.multiple_of(at.z * rows, 16), rows), :] = (normed * gain + offset).astype(BF)

    def block(b):
        return h_ref.at[pl.ds(pl.multiple_of(b * rows, 16), rows), :]

    def to_right(b):
        return remote(block(b), block(b), rs.at[b], hr.at[b], {"seq": at.z + 1})

    def to_left(b):
        return remote(block(b), block(b), ls.at[b], hr.at[b], {"seq": at.z - 1})

    @pl.when(at.z < ns - 1)
    def _():
        to_right(at.z).start()

    @pl.when(at.z > 0)
    def _():
        to_left(at.z).start()

    a_ref[3, pl.ds(own, shard), :] = aw_ref[3].astype(BF)
    send_chunk(1)
    e_ref[pl.ds(own, shard), :] = ew_ref[...].astype(BF)
    send_chunk(2)
    deep = cw_ref.shape[0]
    c_ref[pl.ds(pl.multiple_of(at.x * deep, 16), deep), :] = cw_ref[...].astype(BF)
    send_chunk(3)

    pending = []

    def forward(chunk):
        for k in range(1, nf):
            x_copies[chunk, k].wait_recv()
            j = lax.rem(at.x - k + nf, nf)
            piece = view(chunk, j, at.hi, at.core)
            copy = remote(piece, piece, s1s.at[chunk, k], s1r.at[chunk, k], at.sibling())
            copy.start()
            pending.append(copy)
            for m in range(1, nh):
                copy = remote(piece, piece, ys.at[chunk, k, m], yr.at[chunk, k, m], at.y_peer(m))
                copy.start()
                pending.append((copy, chunk, k, m))

    def relay(chunk):
        for k in range(1, nf):
            for m in range(1, nh):
                j = lax.rem(at.x - k + nf, nf)
                hi = lax.rem(at.hi - m + nh, nh)
                piece = view(chunk, j, hi, at.core)
                remote(piece, piece, ys.at[chunk, k, m], yr.at[chunk, k, m], at.y_peer(m)).wait_recv()
                copy = remote(piece, piece, s2s.at[chunk, k, m], s2r.at[chunk, k, m], at.sibling())
                copy.start()
                pending.append(copy)

    def hop(s):
        b = at.z - s

        @pl.when(b >= 0)
        def _():
            to_right(b).wait_recv()

            @pl.when(at.z < ns - 1)
            def _():
                to_right(b).start()

        d = at.z + s

        @pl.when(d < ns)
        def _():
            to_left(d).wait_recv()

            @pl.when(at.z > 0)
            def _():
                to_left(d).start()

    forward(0)
    hop(1)
    forward(1)
    relay(0)
    relay(1)
    for s in range(2, ns - 1):
        hop(s)
    forward(2)
    relay(2)
    if ns > 2:
        hop(ns - 1)
    forward(3)
    relay(3)
    for entry in pending:
        if isinstance(entry, tuple):
            entry[0].wait_send()
        else:
            entry.wait()
    for copy in x_copies.values():
        copy.wait_send()
    for b in range(ns):
        @pl.when(jnp.logical_and(b <= at.z, at.z < ns - 1))
        def _():
            to_right(b).wait_send()

        @pl.when(jnp.logical_and(b >= at.z, at.z > 0))
        def _():
            to_left(b).wait_send()


def gather_all(sizes, frames, aw, ew, cw, vec):
    nd, nf, ns = sizes
    nh = nd // 2
    rows, width = frames.shape
    deep = cw.shape[0] * nf
    dma = pltpu.SemaphoreType.DMA
    return pl.pallas_call(
        functools.partial(gather_kernel, sizes),
        out_shape=(
            jax.ShapeDtypeStruct((4, width, width), BF),
            jax.ShapeDtypeStruct((width, ew.shape[1]), BF),
            jax.ShapeDtypeStruct((deep, width), BF),
            jax.ShapeDtypeStruct((nf, 16, vec.shape[1]), BF),
            jax.ShapeDtypeStruct((rows * ns, width), BF),
        ),
        in_specs=[vmem()] * 5,
        out_specs=(vmem(),) * 5,
        scratch_shapes=[
            dma((4, nf)), dma((4, nf)),
            dma((4, nf, nh)), dma((4, nf, nh)),
            dma((4, nf)), dma((4, nf)),
            dma((4, nf, nh)), dma((4, nf, nh)),
            dma((nf,)), dma((nf,)),
            dma((ns,)), dma((ns,)), dma((ns,)),
        ],
        name="gather",
        compiler_params=pltpu.CompilerParams(
            collective_id=0, has_side_effects=True, vmem_limit_bytes=VMEM_LIMIT
        ),
    )(frames, aw, ew, cw, vec)


def attention_kernel(chunk, q_ref, k_ref, v_ref, ctx_ref, lse_ref):
    rows = q_ref.shape[0]
    lo = lax.broadcasted_iota(jnp.int32, (chunk, 128), 1) < 64

    def pair(p, carry):
        col = pl.ds(pl.multiple_of(p * 128, 128), 128)
        k2 = k_ref[:, col]
        v2 = v_ref[:, col]
        for c in range(rows // chunk):
            part = pl.ds(c * chunk, chunk)
            q2 = q_ref[part, col]
            ctx, lse = [], []
            for h in range(2):
                mask = lo if h == 0 else jnp.logical_not(lo)
                s = nt(jnp.where(mask, q2, jnp.zeros_like(q2)), k2) * score_scale
                largest = jnp.max(s, axis=-1, keepdims=True)
                e = jnp.exp(s - largest)
                total = jnp.sum(e, axis=-1, keepdims=True)
                ctx.append(nn((e * (1.0 / total)).astype(BF), v2))
                lse.append(largest + jnp.log(total))
            ctx_ref[part, col] = jnp.where(lo, ctx[0], ctx[1])
            lse_ref[p, part, :] = jnp.where(lo, lse[0], lse[1])
        return carry

    lax.fori_loop(0, q_ref.shape[1] // 128, pair, 0)


def attention(q, k, v):
    rows, width = q.shape
    return pl.pallas_call(
        functools.partial(attention_kernel, rows),
        out_shape=(
            jax.ShapeDtypeStruct((rows, width), F32),
            jax.ShapeDtypeStruct((width // 128, rows, 128), F32),
        ),
        in_specs=[vmem()] * 3,
        out_specs=(vmem(), vmem()),
        name="attention",
        compiler_params=pltpu.CompilerParams(vmem_limit_bytes=VMEM_LIMIT),
    )(q, k, v)


def attention_back_kernel(chunk, q_ref, k_ref, v_ref, dc_ref, ctx_ref, lse_ref, dq_ref, dk_ref, dv_ref):
    rows = q_ref.shape[0]
    lo = lax.broadcasted_iota(jnp.int32, (chunk, 128), 1) < 64

    def pair(p, carry):
        col = pl.ds(pl.multiple_of(p * 128, 128), 128)
        k2 = k_ref[:, col]
        v2 = v_ref[:, col]
        dk = dv = None
        for c in range(rows // chunk):
            part = pl.ds(c * chunk, chunk)
            q2 = q_ref[part, col]
            dc2 = dc_ref[part, col]
            both = dc2.astype(F32) * ctx_ref[part, col]
            lse2 = lse_ref[p, part, :]
            dq = []
            for h in range(2):
                mask = lo if h == 0 else jnp.logical_not(lo)
                qm = jnp.where(mask, q2, jnp.zeros_like(q2))
                dm = jnp.where(mask, dc2, jnp.zeros_like(q2))
                lse = lse2[:, 0:1] if h == 0 else lse2[:, 64:65]
                dot = jnp.sum(jnp.where(mask, both, 0.0), axis=-1, keepdims=True)
                probs = jnp.exp(nt(qm, k2) * score_scale - lse)
                slopes = nt(dm, v2)
                ds = (probs * (slopes - dot) * score_scale).astype(BF)
                dq.append(nn(ds, k2))
                a = nn(dm.T, probs.astype(BF))
                b = nn(qm.T, ds)
                dv = a if dv is None else dv + a
                dk = b if dk is None else dk + b
            dq_ref[part, col] = jnp.where(lo, dq[0], dq[1])
        dk_ref[col, :] = dk.astype(dk_ref.dtype)
        dv_ref[col, :] = dv.astype(dv_ref.dtype)
        return carry

    lax.fori_loop(0, q_ref.shape[1] // 128, pair, 0)


def attention_back(q, k, v, dc, ctx, lse):
    rows, width = q.shape
    every = k.shape[0]
    return pl.pallas_call(
        functools.partial(attention_back_kernel, rows),
        out_shape=(
            jax.ShapeDtypeStruct((rows, width), F32),
            jax.ShapeDtypeStruct((width, every), F32),
            jax.ShapeDtypeStruct((width, every), F32),
        ),
        in_specs=[vmem()] * 6,
        out_specs=(vmem(),) * 3,
        name="attention_back",
        compiler_params=pltpu.CompilerParams(vmem_limit_bytes=VMEM_LIMIT),
    )(q, k, v, dc, ctx, lse)


def reduce_kernel(
    sizes, ga_ref, ge_ref, gc_ref, gv_ref, dh_ref,
    oa_ref, oe_ref, oc_ref, ov_ref, od_ref,
    ca, ce, cc, xa, xe, xc, ya, ye, yc, za, ze, zc, dr, vb, vx, vy, vz,
    cs, cr, xs, xr, ys, yr, zs, zr, azs, azr, ays, ayr, acs, acr, ds, dm, vs, vr,
):
    at = Place(sizes)
    nf, nh, ns = at.nf, at.nh, at.ns
    half = ga_ref.shape[2] // 2
    width = ga_ref.shape[3]
    cols = width // nh
    wide = ge_ref.shape[2] // nh
    piece = wide // ns
    at.barrier()
    mine = pl.ds(pl.multiple_of(at.core * half, 16), half)
    other = pl.ds(pl.multiple_of((1 - at.core) * half, 16), half)
    sends = []

    def go(copy):
        copy.start()
        sends.append(copy)
        return copy

    held = (cc, ce, ca)
    c_copies = []
    for g, ref in enumerate((gc_ref, ge_ref, ga_ref)):
        src = ref.at[:, other, :] if g == 1 else ref.at[:, :, other, :]
        c_copies.append(go(remote(src, held[g], cs.at[g], cr.at[g], at.sibling())))

    d_copies = []
    for k in range(1, ns):
        d_copies.append(
            go(remote(dh_ref.at[at.z_at(k)], dr.at[k - 1], ds.at[k - 1], dm.at[k - 1], at.z_peer(k)))
        )

    def vector_start():
        return go(remote(gv_ref, vb, vs.at[0], vr.at[0], at.sibling()))

    v_core = vector_start()

    def stage_c(g):
        c_copies[g].wait_recv()
        if g == 0:
            for j in range(nf):
                for u in range(4):
                    cc[j, u] = (cc[j, u].astype(F32) + gc_ref[j, u, mine, :].astype(F32)).astype(BF)
        elif g == 1:
            for j in range(nf):
                ce[j] = (ce[j].astype(F32) + ge_ref[j, mine, :].astype(F32)).astype(BF)
        else:
            for u in range(4):
                for j in range(nf):
                    ca[u, j] = (ca[u, j].astype(F32) + ga_ref[u, j, mine, :].astype(F32)).astype(BF)
        out = []
        for k in range(1, nf):
            j = lax.rem(at.x + k, nf)
            src = ca.at[:, j] if g == 2 else held[g].at[j]
            dst = (xc, xe, xa)[g].at[k - 1]
            out.append(go(remote(src, dst, xs.at[g, k - 1], xr.at[g, k - 1], at.x_peer(k))))
        return out

    def stage_x(g, copies):
        for copy in copies:
            copy.wait_recv()
        got = (xc, xe, xa)[g]

        def mix(u):
            if g == 1:
                total = ce[at.x].astype(F32)
                for k in range(nf - 1):
                    total += got[k].astype(F32)
                got[0] = total.astype(BF)
            else:
                total = (cc[at.x, u] if g == 0 else ca[u, at.x]).astype(F32)
                for k in range(nf - 1):
                    total += got[k, u].astype(F32)
                got[0, u] = total.astype(BF)

        for u in range(1 if g == 1 else 4):
            mix(u)
        out = []
        for m in range(1, nh):
            hi = at.y_hi(m)
            if g == 1:
                src = got.at[0, :, pl.ds(pl.multiple_of(hi * wide, 128), wide)]
            else:
                src = got.at[0, :, :, pl.ds(pl.multiple_of(hi * cols, 128), cols)]
            dst = (yc, ye, ya)[g].at[m - 1]
            out.append(go(remote(src, dst, ys.at[g, m - 1], yr.at[g, m - 1], at.y_peer(m))))
        return out

    def stage_y(g, copies):
        for copy in copies:
            copy.wait_recv()
        kept = (xc, xe, xa)[g]
        got = (yc, ye, ya)[g]
        if g == 1:
            total = kept[0, :, pl.ds(pl.multiple_of(at.hi * wide, 128), wide)].astype(F32)
            for m in range(nh - 1):
                total += got[m].astype(F32)
            got[0] = total.astype(BF)
        else:
            for u in range(4):
                total = kept[0, u, :, pl.ds(pl.multiple_of(at.hi * cols, 128), cols)].astype(F32)
                for m in range(nh - 1):
                    total += got[m, u].astype(F32)
                got[0, u] = total.astype(BF)
        out = []
        for k in range(1, ns):
            b = at.z_at(k)
            if g == 1:
                src = got.at[0, :, pl.ds(pl.multiple_of(b * piece, 128), piece)]
            else:
                src = got.at[0, b]
            dst = (zc, ze, za)[g].at[k - 1]
            out.append(go(remote(src, dst, zs.at[g, k - 1], zr.at[g, k - 1], at.z_peer(k))))
        return out

    def home(g, z, hi):
        if g == 1:
            return oe_ref.at[mine, pl.ds(pl.multiple_of(hi * wide + z * piece, 128), piece)]
        out = oc_ref if g == 0 else oa_ref
        return out.at[z, mine, pl.ds(pl.multiple_of(hi * cols, 128), cols)]

    def stage_z(g, copies):
        for copy in copies:
            copy.wait_recv()
        kept = (yc, ye, ya)[g]
        got = (zc, ze, za)[g]
        if g == 1:
            total = kept[0, :, pl.ds(pl.multiple_of(at.z * piece, 128), piece)].astype(F32)
        else:
            total = kept[0, at.z].astype(F32)
        for k in range(ns - 1):
            total += got[k].astype(F32)
        spot = home(g, at.z, at.hi)
        spot[...] = total.astype(BF)
        out = []
        for k in range(1, ns):
            out.append(go(remote(spot, spot, azs.at[g, k - 1], azr.at[g, k - 1], at.z_peer(k))))
        return out

    def strip(g, hi):
        if g == 1:
            return oe_ref.at[mine, pl.ds(pl.multiple_of(hi * wide, 128), wide)]
        out = oc_ref if g == 0 else oa_ref
        return out.at[:, mine, pl.ds(pl.multiple_of(hi * cols, 128), cols)]

    def gather_y(g, copies):
        for copy in copies:
            copy.wait_recv()
        out = []
        for m in range(1, nh):
            spot = strip(g, at.hi)
            out.append(go(remote(spot, spot, ays.at[g, m - 1], ayr.at[g, m - 1], at.y_peer(m))))
        return out

    def gather_c(g, copies):
        for copy in copies:
            copy.wait_recv()
        if g == 1:
            spot = oe_ref.at[mine, :]
        else:
            spot = (oc_ref if g == 0 else oa_ref).at[:, mine, :]
        return [go(remote(spot, spot, acs.at[g], acr.at[g], at.sibling()))]

    def finish(copies):
        for copy in copies:
            copy.wait_recv()

    x0 = stage_c(0)
    x1 = stage_c(1)
    x2 = stage_c(2)
    v_core.wait_recv()
    vx[at.x] = gv_ref[...] + vb[...]
    v_x = [
        go(remote(vx.at[at.x], vx.at[at.x], vs.at[k], vr.at[k], at.x_peer(k)))
        for k in range(1, nf)
    ]
    y0 = stage_x(0, x0)
    finish(v_x)
    total = vx[0]
    for j in range(1, nf):
        total += vx[j]
    vy[at.hi] = total
    v_y = [
        go(remote(vy.at[at.hi], vy.at[at.hi], vs.at[nf + m], vr.at[nf + m], at.y_peer(m)))
        for m in range(1, nh)
    ]
    z0 = stage_y(0, y0)
    y1 = stage_x(1, x1)
    finish(v_y)
    total = vy[0]
    for j in range(1, nh):
        total += vy[j]
    vz[at.z] = total
    v_z = [
        go(remote(vz.at[at.z], vz.at[at.z], vs.at[nf + nh + k], vr.at[nf + nh + k], at.z_peer(k)))
        for k in range(1, ns)
    ]
    az0 = stage_z(0, z0)
    z1 = stage_y(1, y1)
    ay0 = gather_y(0, az0)
    y2 = stage_x(2, x2)
    az1 = stage_z(1, z1)
    ac0 = gather_c(0, ay0)
    z2 = stage_y(2, y2)
    ay1 = gather_y(1, az1)
    finish(v_z)
    total = vz[0]
    for j in range(1, ns):
        total += vz[j]
    ov_ref[...] = total
    finish(d_copies)
    total = dh_ref[at.z].astype(F32)
    for k in range(ns - 1):
        total += dr[k].astype(F32)
    od_ref[...] = total
    az2 = stage_z(2, z2)
    ac1 = gather_c(1, ay1)
    ay2 = gather_y(2, az2)
    ac2 = gather_c(2, ay2)
    finish(ac0)
    finish(ac1)
    finish(ac2)
    for copy in sends:
        copy.wait_send()


def reduce_all(sizes, ga, ge, gc, gv, dh):
    nd, nf, ns = sizes
    nh = nd // 2
    _, _, shard, width = ga.shape
    half = shard // 2
    full = ge.shape[2]
    cols, wide = width // nh, full // nh
    rows = dh.shape[1]
    dma = pltpu.SemaphoreType.DMA
    xn, yn, zn = max(nf - 1, 1), max(nh - 1, 1), max(ns - 1, 1)
    vec = gv.shape
    return pl.pallas_call(
        functools.partial(reduce_kernel, sizes),
        out_shape=(
            jax.ShapeDtypeStruct((4, shard, width), BF),
            jax.ShapeDtypeStruct((shard, full), BF),
            jax.ShapeDtypeStruct((4, shard, width), BF),
            jax.ShapeDtypeStruct(vec, F32),
            jax.ShapeDtypeStruct((rows, width), F32),
        ),
        in_specs=[vmem()] * 5,
        out_specs=(vmem(),) * 5,
        scratch_shapes=[
            pltpu.VMEM((4, nf, half, width), BF),
            pltpu.VMEM((nf, half, full), BF),
            pltpu.VMEM((nf, 4, half, width), BF),
            pltpu.VMEM((xn, 4, half, width), BF),
            pltpu.VMEM((xn, half, full), BF),
            pltpu.VMEM((xn, 4, half, width), BF),
            pltpu.VMEM((yn, 4, half, cols), BF),
            pltpu.VMEM((yn, half, wide), BF),
            pltpu.VMEM((yn, 4, half, cols), BF),
            pltpu.VMEM((zn, half, cols), BF),
            pltpu.VMEM((zn, half, wide // ns), BF),
            pltpu.VMEM((zn, half, cols), BF),
            pltpu.VMEM((zn, rows, width), BF),
            pltpu.VMEM(vec, F32),
            pltpu.VMEM((nf,) + vec, F32),
            pltpu.VMEM((nh,) + vec, F32),
            pltpu.VMEM((ns,) + vec, F32),
            dma((3,)), dma((3,)),
            dma((3, xn)), dma((3, xn)),
            dma((3, yn)), dma((3, yn)),
            dma((3, zn)), dma((3, zn)),
            dma((3, zn)), dma((3, zn)),
            dma((3, yn)), dma((3, yn)),
            dma((3,)), dma((3,)),
            dma((zn,)), dma((zn,)),
            dma((nf + nh + ns,)), dma((nf + nh + ns,)),
        ],
        name="reduce",
        compiler_params=pltpu.CompilerParams(
            collective_id=1, has_side_effects=True, vmem_limit_bytes=VMEM_LIMIT
        ),
    )(ga, ge, gc, gv, dh)


def on_device(
    sizes,
    frames_in,
    cotangent,
    attention_weight,
    expand_weight,
    contract_weight,
    vectors,
    first_attention,
    first_expand,
    first_contract,
    first_vectors,
    second_attention,
    second_expand,
    second_contract,
    second_vectors,
):
    nd, nf, ns = sizes
    frames = frames_in[0]
    upstream = cotangent[0]
    rows, width = frames.shape
    shard = attention_weight.shape[1]
    full = expand_weight.shape[1]
    vec_pad = jnp.pad(vectors, ((0, 4), (0, 0)))
    aw, ew, cw, vw, h_all = gather_all(
        sizes, frames, attention_weight, expand_weight, contract_weight, vec_pad
    )
    vec = jnp.transpose(vw, (1, 0, 2)).reshape(16, width)[:12].astype(F32)
    bias_expand = vec[8:].reshape(-1)
    normed_one, inverse_one = normalize(frames)
    h_own = lax.dynamic_slice_in_dim(h_all, lax.axis_index("seq") * rows, rows, 0)
    queries = (nn(h_own, aw[0]) + vec[2]).astype(BF)
    key_rows = nn(h_all, aw[1]).astype(BF)
    value_rows = (nn(h_all, aw[2]) + vec[3]).astype(BF)
    context_wide, log_total = attention(queries, key_rows, value_rows)
    context = context_wide.astype(BF)
    middle = frames + nn(context, aw[3]) + vec[4]
    normed_two, inverse_two = normalize(middle)
    hidden_two = (normed_two * vec[5] + vec[6]).astype(BF)
    expanded = nn(hidden_two, ew) + bias_expand
    activated = gelu_exact(expanded).astype(BF)
    frames_out = middle + nn(activated, cw) + vec[7]
    upstream_bf = upstream.astype(BF)
    grad_contract = tn(activated, upstream_bf).astype(BF)
    grad_expanded = nt(upstream_bf, cw) * gelu_slope(expanded)
    grad_expanded_bf = grad_expanded.astype(BF)
    grad_expand = tn(hidden_two, grad_expanded_bf).astype(BF)
    grad_hidden_two = nt(grad_expanded_bf, ew)
    back_two, gain_two_grad, bias_two_grad = norm_back(
        grad_hidden_two, normed_two, inverse_two, vec[5]
    )
    grad_middle = upstream + back_two
    grad_middle_bf = grad_middle.astype(BF)
    grad_output_w = tn(context, grad_middle_bf).astype(BF)
    grad_context = nt(grad_middle_bf, aw[3]).astype(BF)
    dq, dkt, dvt = attention_back(
        queries, key_rows, value_rows, grad_context, context_wide, log_total
    )
    dq_bf = dq.astype(BF)
    dkt_bf = dkt.astype(BF)
    dvt_bf = dvt.astype(BF)
    grad_query_w = tn(h_own, dq_bf).astype(BF)
    grad_key_w = lax.dot_general(
        h_all, dkt_bf, (((0,), (1,)), ((), ())), preferred_element_type=F32
    ).astype(BF)
    grad_value_w = lax.dot_general(
        h_all, dvt_bf, (((0,), (1,)), ((), ())), preferred_element_type=F32
    ).astype(BF)
    spread = (
        lax.dot_general(dkt_bf, aw[1], (((0,), (1,)), ((), ())), preferred_element_type=F32)
        + lax.dot_general(dvt_bf, aw[2], (((0,), (1,)), ((), ())), preferred_element_type=F32)
    ).astype(BF)
    gv = jnp.zeros((16, width), F32)
    small = jnp.stack(
        [
            jnp.sum(dq, axis=0),
            jnp.sum(dvt, axis=1),
            jnp.sum(grad_middle, axis=0),
            gain_two_grad,
            bias_two_grad,
            jnp.sum(upstream, axis=0),
        ]
    )
    gv = jnp.concatenate(
        [jnp.zeros((2, width), F32), small, jnp.sum(grad_expanded, axis=0).reshape(-1, width),
         jnp.zeros((4, width), F32)], axis=0
    )
    ga = jnp.stack([grad_query_w, grad_key_w, grad_value_w, grad_output_w])
    oa, oe, oc, ov, od = reduce_all(
        sizes,
        ga.reshape(4, nf, shard, width),
        grad_expand.reshape(nf, shard, full),
        grad_contract.reshape(nf, 4, shard, width),
        gv,
        spread.reshape(ns, rows, width),
    )
    grad_hidden_one = od + nt(dq_bf, aw[0])
    back_one, gain_one_grad, bias_one_grad = norm_back(
        grad_hidden_one, normed_one, inverse_one, vec[0]
    )
    ends = lax.psum(jnp.stack([gain_one_grad, bias_one_grad]), ("dp", "fsdp", "seq"))
    gv_sum = jnp.concatenate([ends, ov[2:12]], axis=0)
    owned_vec = lax.dynamic_slice_in_dim(
        gv_sum, lax.axis_index("fsdp") * (width // nf), width // nf, 1
    )
    owned = (
        oa.astype(F32),
        oe.astype(F32),
        oc.reshape(4 * shard, width).astype(F32),
        owned_vec,
    )
    new_attention = adam_update(
        attention_weight, owned[0], first_attention, second_attention, rate_matrix, decay_matrix
    )
    new_expand = adam_update(
        expand_weight, owned[1], first_expand, second_expand, rate_matrix, decay_matrix
    )
    new_contract = adam_update(
        contract_weight, owned[2], first_contract, second_contract, rate_matrix, decay_matrix
    )
    new_vectors = adam_update(vectors, owned[3], first_vectors, second_vectors, rate_vector, 0.0)
    return (
        frames_out[None],
        (grad_middle + back_one)[None],
        owned[0],
        owned[1],
        owned[2],
        owned[3],
        new_attention[0],
        new_expand[0],
        new_contract[0],
        new_vectors[0],
        new_attention[1],
        new_expand[1],
        new_contract[1],
        new_vectors[1],
        new_attention[2],
        new_expand[2],
        new_contract[2],
        new_vectors[2],
    )


def solution(mesh):
    sizes = (mesh.shape["dp"], mesh.shape["fsdp"], mesh.shape["seq"])
    data = P(("dp", "fsdp"), "seq", None)
    state = (P(None, "fsdp", None), P("fsdp", None), P("fsdp", None), P(None, "fsdp"))
    return jax.shard_map(
        functools.partial(on_device, sizes),
        mesh=mesh,
        in_specs=(data, data) + state * 3,
        out_specs=(data, data) + state * 4,
        check_vma=False,
    )
```

time: 1290 us -> 499 us (0.39)
  waiting for transfers between devices: 832 us -> 0 us
  Pallas kernels: 0 us -> 314 us
  matrix products: 232 us -> 75.4 us
  local copies, waits for them, and re-layouts: 63.7 us -> 15.9 us
  blocking collectives: 70 us -> 41.1 us
  other arithmetic: 72.3 us -> 45.5 us
  between operations: 14.6 us -> 1.29 us
    reduce_scatter x6 -> x0, waiting for transfers between devices: 455 us -> none  [the longest x1 113 us: on_device(): lax.psum_scatter(summed[2], 'fsdp', scatter_dimension=0, tiled=True)]
    pallas_call x0 -> x4, Pallas kernels: none -> 314 us  [the longest x1 194 us: reduce_all(): pl.pallas_call(functools.partial(reduce_kernel, sizes), out_shape=(jax.Sh...]
    psum x1 -> x0, waiting for transfers between devices: 197 us -> none  [on_device(): summed = lax.psum(current, ('dp', 'seq'))]
    all_gather x5 -> x0, waiting for transfers between devices: 179 us -> none  [the longest x1 58.1 us: on_device(): lax.all_gather(shards[0], 'fsdp', axis=1, tiled=True)]
    dot_general x102 -> x18, matrix products: 232 us -> 75.4 us  [the longest x6 27.7 us: nn(): lax.dot_general(left, right, (((1,), (0,)), ((), ())), preferred_element_...]
    psum x1, blocking collectives: 64.6 us -> 41.1 us  [on_device(): lax.psum(jnp.stack([gain_one_grad, bias_one_grad]), ('dp', 'fsdp', 'seq'))]
    convert_element_type x19 -> x1, other arithmetic: 18.1 us -> 0.89 us  [on_device(): vec = jnp.transpose(vw, (1, 0, 2)).reshape(16, width)[:12].astype(F32)]
    dynamic_update_slice x12 -> x0, local copies, waits for them, and re-layouts: 15.9 us -> none  [on_device(): lax.map(head_forward, (query_heads, key_heads, value_heads))]
  transfers between devices with their start and end apart: 12 -> 0, of which waited for: 11 -> 0; matrix products, arithmetic and copies ran while one was open for 14% -> 0% of each run, Pallas kernels for 0% -> 0%
where the time goes in v1:
time: 499 us; the launch traced here: 493 us
  Pallas kernels  314 us (63%)
  matrix products  75.4 us (15%)
  other arithmetic  45.5 us (9%)
  blocking collectives  41.1 us (8%)
  local copies, waits for them, and re-layouts  15.9 us (3%)
    pallas_call x1, Pallas kernels, reduce_all(): pl.pallas_call(functools.partial(reduce_kernel, sizes), out_shape=(jax.Sh...  194 us
    pallas_call x1, Pallas kernels, gather_all(): pl.pallas_call(functools.partial(gather_kernel, sizes), out_shape=(jax.Sh...  73.4 us
    psum x1, blocking collectives, on_device(): lax.psum(jnp.stack([gain_one_grad, bias_one_grad]), ('dp', 'fsdp', 'seq'))  41.1 us
    sub x4, other arithmetic, adam_update(): weight - rate * (first_hat / (jnp.sqrt(second_hat) + adam_eps) + decay *...  34.6 us
    dot_general x6, matrix products, nn(): lax.dot_general(left, right, (((1,), (0,)), ((), ())), preferred_element_...  27.7 us
    pallas_call x1, Pallas kernels, attention_back(): pl.pallas_call(functools.partial(attention_back_kernel, rows), out_shape=...  25 us
    pallas_call x1, Pallas kernels, attention(): pl.pallas_call(functools.partial(attention_kernel, rows), out_shape=(jax....  21.2 us
    dot_general x4, matrix products, nt(): lax.dot_general(left, right, (((1,), (1,)), ((), ())), preferred_element_...  17.6 us

profile of v1, /device:TPU:0, one launch (start us, length us, event | category | flops | bytes accessed | tf_op | source)
XLA Modules:
  0.0 493.1 jit_solution(15780319023473271416)
XLA Ops:
  0.7 1.4 pad.4.vec_ref
  2.0 73.4 %gather.1 = (bf16[4,768,768]{2,1,0:T(8,128)(2,1)}, bf16[768,3072]{1,0:T(8,128)(2,1)}, bf16[3072,768]{1,0:T(8,128)(2,1)}, bf16[2,16,384]{2,1,0:T(8,128)(2,1)}, bf16[1536,768]{1,0:T(8,128)(2,1)}) custom-call(f32[384,768]{1,0:T(8,128)} %bitcast.84, f32[4,384,768]{2,1,0:T(8,128)} %aw_ref.1, f32[384,3072]{1,0:T(8,128)} %ew_ref.1, f32[1536,768]{1,0:T(8,128)} %cw_ref.1, ...), custom_call_target="tpu_custom_call" | custom-call | tf_op jit(solution)/shard_map/gather/pallas_call | solution.py:295
  75.4 0.9 slice_convert_fusion
  76.3 0.6 slice_reduce_fusion
  77.0 2.9 fusion.11.q_ref
  79.9 4.7 convolution_convert_fusion.2.k_ref
  84.6 4.7 add_convert_fusion.1.v_ref
  89.3 21.2 %attention.1 = (f32[384,768]{1,0:T(8,128)}, f32[6,384,128]{2,1,0:T(8,128)}) custom-call(bf16[384,768]{1,0:T(8,128)(2,1)} %fusion.11.q_ref, bf16[1536,768]{1,0:T(8,128)(2,1)} %convolution_convert_fusion.2.k_ref, bf16[1536,768]{1,0:T(8,128)(2,1)} %add_convert_fusion.1.v_ref), custom_call_target="tpu_custom_call" | custom-call | tf_op jit(solution)/shard_map/attention/pallas_call | solution.py:350
  110.5 2.3 fusion.56
  112.8 0.8 slice.76
  113.7 0.3 multiply_reduce_fusion.5
  114.0 6.9 %multiply_convert_fusion = (bf16[384,3072]{1,0:T(8,128)(2,1)}, f32[384,3072]{1,0:T(8,128)}) fusion(f32[3072]{0:T(1024)S(1)} %add.186, bf16[768,3072]{1,0:T(8,128)(2,1)} %get-tuple-element.37, f32[384,768]{1,0:T(8,128)S(1)} %get-tuple-element.82, f32[768]{0:T(1024)S(1)} %add.183, f32[768]{0:T(1024)S(1)} %mul.264, f32[384]{0:T(512)S(1)} %add_rsqrt_fusion.1, ...), kind=kOutput, calls=%fused_computation.22 | convolution fusion | flops 1820491776 | bytes 12997632 | tf_op jit(solution)/shard_map/dot_general | solution.py:31
  120.8 0.0 copy-start.29
  120.9 6.2 %fusion.10 = f32[1,384,768]{2,1,0:T(8,128)} fusion(f32[384,768]{1,0:T(8,128)S(1)} %get-tuple-element.82, bf16[384,3072]{1,0:T(8,128)(2,1)} %get-tuple-element.83, bf16[3072,768]{1,0:T(8,128)(2,1)} %get-tuple-element.38, f32[768]{0:T(1024)S(1)} %add.191), kind=kOutput, calls=%fused_computation.38 | convolution fusion | flops 1812529152 | bytes 9440256 | tf_op jit(solution)/shard_map/dot_general | solution.py:31
  127.1 5.5 %fusion.57 = (f32[3072]{0:T(1024)}, bf16[384,3072]{1,0:T(8,128)(2,1)S(1)}) fusion(f32[384,3072]{1,0:T(8,128)S(1)} %copy-done.29, bf16[3072,768]{1,0:T(8,128)(2,1)} %get-tuple-element.38, f32[1,384,768]{2,1,0:T(8,128)S(1)} %copy-done.6), kind=kOutput, calls=%fused_computation.115 | convolution fusion | flops 1824912384 | bytes 12988416 | tf_op jit(solution)/shard_map/dot_general | solution.py:27
  132.6 6.1 %multiply_reduce_fusion.2 = (f32[768]{0:T(1024)}, f32[384]{0:T(512)S(1)}, f32[384]{0:T(512)S(1)}, f32[768]{0:T(1024)}, f32[384,768]{1,0:T(8,128)S(1)}) fusion(f32[384,768]{1,0:T(8,128)S(1)} %get-tuple-element.82, f32[384]{0:T(512)S(1)} %add_rsqrt_fusion.1, f32[384]{0:T(512)S(1)} %broadcast_multiply_fusion.5, f32[768]{0:T(1024)S(1)} %mul.264, ...), kind=kOutput, calls=%fused_computation.55 | convolution fusion | flops 1814591232 | bytes 9452544 | tf_op jit(solution)/shard_map/dot_general | solution.py:27
  138.7 0.4 fusion.55
  139.2 0.0 copy-start.2
  139.2 0.1 reduce_sum.157
  139.3 0.3 multiply_reduce_fusion.3
  139.6 0.6 add_rsqrt_fusion
  140.2 0.7 mul.286
  140.9 1.8 convolution_convert_fusion.3
  142.7 2.8 convolution_convert_fusion.7.dc_ref
  145.5 25.0 %attention_back.1 = (f32[384,768]{1,0:T(8,128)}, f32[768,1536]{1,0:T(8,128)}, f32[768,1536]{1,0:T(8,128)}) custom-call(bf16[384,768]{1,0:T(8,128)(2,1)} %fusion.11.q_ref, bf16[1536,768]{1,0:T(8,128)(2,1)} %convolution_convert_fusion.2.k_ref, bf16[1536,768]{1,0:T(8,128)(2,1)} %add_convert_fusion.1.v_ref, bf16[384,768]{1,0:T(8,128)(2,1)} %convolution_convert_fusion.7.dc_ref, ...), custom_call_target="tpu_custom_call" | custom-call | tf_op jit(solution)/shard_map/attention_back/pallas_call | solution.py:404
  170.5 5.2 %convolution_convert_fusion.5 = bf16[768,768]{1,0:T(8,128)(2,1)S(1)} fusion(bf16[1536,768]{1,0:T(8,128)(2,1)} %get-tuple-element.33, f32[768,1536]{1,0:T(8,128)} %get-tuple-element.42), kind=kOutput, calls=%fused_computation.30 | convolution fusion | flops 1813708800 | bytes 8257536 | tf_op jit(solution)/shard_map/dot_general | solution.py:769
  175.8 0.0 copy-start.1
  175.8 2.0 convolution_convert_fusion.6
  177.8 0.0 copy-start.5
  177.9 0.8 convolution_convert_fusion.4
  178.7 0.4 copy-done.5
  179.1 2.7 pad_maximum_fusion.ga_ref
  181.9 1.0 copy-done.28
  182.9 4.6 convolution_convert_fusion.1
  187.5 4.5 fusion.59
  192.0 0.1 reduce_sum.159
  192.1 0.6 stack.47
  192.7 2.6 reduce_sum.160
  195.3 0.6 stack.48
  195.9 0.6 stack.49
  196.5 1.3 stack.50
  197.8 0.6 stack.51
  198.3 1.4 reduce_sum.164
  199.7 0.6 stack.52
  200.3 0.7 reshape.122
  201.0 0.6 broadcast_in_dim.9
  201.6 0.6 broadcast_in_dim.10
  202.2 2.7 concatenate.7.gv_ref
  204.9 4.8 fusion.16
  209.8 6.3 %add_convert_fusion = bf16[1536,768]{1,0:T(8,128)(2,1)} fusion(f32[1536,768]{1,0:T(8,128)S(1)} %fusion.16, f32[768,1536]{1,0:T(8,128)} %get-tuple-element.42, bf16[4,768,768]{2,1,0:T(8,128)(2,1)} %get-tuple-element.34), kind=kOutput, calls=%fused_computation.21 | convolution fusion | flops 1815478272 | bytes 12976128 | tf_op jit(solution)/shard_map/dot_general | solution.py:774
  216.1 194.1 %reduce.17 = (bf16[4,384,768]{2,1,0:T(8,128)(2,1)}, bf16[384,3072]{1,0:T(8,128)(2,1)}, bf16[4,384,768]{2,1,0:T(8,128)(2,1)}, f32[16,768]{1,0:T(8,128)}, f32[384,768]{1,0:T(8,128)}) custom-call(bf16[4,2,384,768]{3,2,1,0:T(8,128)(2,1)} %pad_maximum_fusion.ga_ref, bf16[2,384,3072]{2,1,0:T(8,128)(2,1)} %bitcast.95, bf16[2,4,384,768]{3,2,1,0:T(8,128)(2,1)} %bitcast.96, ...), custom_call_target="tpu_custom_call" | custom-call | tf_op jit(solution)/shard_map/reduce/pallas_call | solution.py:658
  410.3 3.2 multiply_reduce_fusion
  413.5 1.4 add_bitcast_fusion
  414.9 0.7 copy-done.8
  415.6 13.5 %multiply_subtract_fusion.2 = (f32[4,384,768]{2,1,0:T(8,128)}, f32[4,384,768]{2,1,0:T(8,128)}, f32[4,384,768]{2,1,0:T(8,128)}, f32[4,384,768]{2,1,0:T(8,128)}) fusion(f32[4,384,768]{2,1,0:T(8,128)} %aw_ref.1, f32[4,384,768]{2,1,0:T(8,128)} %param.20, f32[4,384,768]{2,1,0:T(8,128)} %param.24, bf16[4,384,768]{2,1,0:T(8,128)(2,1)S(1)} %copy-done.8), kind=kLoop, calls=%fused_computation.19 | loop fusion | flops 18874368 | bytes 35389440 | tf_op jit(solution)/shard_map/sub | solution.py:74
  429.1 0.9 slice-done.6
  430.0 0.2 slice-done.1
  430.2 0.1 slice-done.5
  430.3 0.1 slice-done.7
  430.5 9.6 %multiply_subtract_fusion.1 = (f32[384,3072]{1,0:T(8,128)}, f32[384,3072]{1,0:T(8,128)}, f32[384,3072]{1,0:T(8,128)}, f32[384,3072]{1,0:T(8,128)}) fusion(f32[384,3072]{1,0:T(8,128)S(1)} %bitcast.86, f32[384,3072]{1,0:T(8,128)S(1)} %bitcast.90, f32[384,3072]{1,0:T(8,128)S(1)} %bitcast.92, bf16[384,3072]{1,0:T(8,128)(2,1)} %get-tuple-element.45), kind=kLoop, calls=%fused_computation.17 | loop fusion | flops 18874368 | bytes 35389440 | tf_op jit(solution)/shard_map/sub | solution.py:74
  440.1 0.0 copy-start.19
  440.1 10.8 %multiply_subtract_fusion = (f32[1536,768]{1,0:T(8,128)}, f32[1536,768]{1,0:T(8,128)}, f32[1536,768]{1,0:T(8,128)}, f32[1536,768]{1,0:T(8,128)}) fusion(f32[1536,768]{1,0:T(8,128)S(1)} %bitcast.88, f32[1536,768]{1,0:T(8,128)} %param.22, f32[1536,768]{1,0:T(8,128)} %param.26, bf16[4,384,768]{2,1,0:T(8,128)(2,1)} %get-tuple-element.46), kind=kLoop, calls=%fused_computation.15 | loop fusion | flops 18874368 | bytes 35389440 | tf_op jit(solution)/shard_map/sub | solution.py:74
  451.0 41.1 %psum.7 = f32[2,768]{1,0:T(2,128)S(1)} all-reduce(f32[2,768]{1,0:T(2,128)S(1)} %pad_maximum_fusion.1), channel_id=1, replica_groups=mesh['dp'=4,'fsdp'=2,'seq'=4] {'dp','fsdp','seq'}, use_global_device_ids=true, to_apply=%region_17.18 | all-reduce | flops 1536 | bytes 12288 | tf_op jit(solution)/shard_map/psum | solution.py:804
  492.2 0.7 multiply_subtract_fusion.3
  (86 shorter events, 0.3 us)
Async XLA Ops:
  75.4 4.4 copy-start.9
  76.3 8.2 %copy-start.11 = (f32[12,2,384]{2,0,1:T(8,128)}, f32[12,2,384]{2,0,1:T(8,128)S(1)}, u32[]{:S(2)}) copy-start(f32[12,2,384]{2,0,1:T(8,128)S(1)} %slice_convert_fusion) | copy-start | bytes 110596
  89.3 21.2 %copy-start = (f32[1,384,768]{2,1,0:T(8,128)S(1)}, f32[1,384,768]{2,1,0:T(8,128)}, u32[]{:S(2)}) copy-start(f32[1,384,768]{2,1,0:T(8,128)} %param.14) | copy-start | bytes 3538948
  112.8 25.9 %copy-start.3 = (f32[384,768]{1,0:T(8,128)}, f32[384,768]{1,0:T(8,128)S(1)}, u32[]{:S(2)}) copy-start(f32[384,768]{1,0:T(8,128)S(1)} %get-tuple-element.82) | copy-start | bytes 3538948
  113.7 7.2 %copy-start.22 = (f32[768]{0:T(1024)}, f32[768]{0:T(1024)S(1)}, u32[]{:S(2)}) copy-start(f32[768]{0:T(1024)S(1)} %add.183) | copy-start | bytes 9220
  114.0 24.7 %copy-start.20 = (f32[384]{0:T(512)}, f32[384]{0:T(512)S(1)}, u32[]{:S(2)}) copy-start(f32[384]{0:T(512)S(1)} %add_rsqrt_fusion.1) | copy-start | bytes 4612
  120.8 6.2 %copy-start.6 = (f32[1,384,768]{2,1,0:T(8,128)S(1)}, f32[1,384,768]{2,1,0:T(8,128)}, u32[]{:S(2)}) copy-start(f32[1,384,768]{2,1,0:T(8,128)} %param.15) | copy-start | bytes 3538948
  120.8 6.2 %copy-start.29 = (f32[384,3072]{1,0:T(8,128)S(1)}, f32[384,3072]{1,0:T(8,128)}, u32[]{:S(2)}) copy-start(f32[384,3072]{1,0:T(8,128)} %get-tuple-element.84) | copy-start | bytes 14155780
  132.6 6.1 %copy-start.27 = (bf16[384,3072]{1,0:T(8,128)(2,1)}, bf16[384,3072]{1,0:T(8,128)(2,1)S(1)}, u32[]{:S(2)}) copy-start(bf16[384,3072]{1,0:T(8,128)(2,1)S(1)} %get-tuple-element.87) | copy-start | bytes 7077892
  139.2 1.7 copy-start.2
  139.3 0.9 copy-start.14
  170.5 5.2 %copy-start.10 = (bf16[1536,768]{1,0:T(8,128)(2,1)S(1)}, bf16[1536,768]{1,0:T(8,128)(2,1)}, u32[]{:S(2)}) copy-start(bf16[1536,768]{1,0:T(8,128)(2,1)} %get-tuple-element.33) | copy-start | bytes 7077892
  170.5 5.3 %copy-start.25 = (f32[768,1536]{1,0:T(8,128)S(1)}, f32[768,1536]{1,0:T(8,128)}, u32[]{:S(2)}) copy-start(f32[768,1536]{1,0:T(8,128)} %get-tuple-element.41) | copy-start | bytes 14155780
  175.8 2.1 copy-start.1
  177.8 1.3 copy-start.5
  179.1 2.7 copy-start.4
  179.1 2.7 copy-start.21
  179.1 2.7 copy-start.23
  179.1 3.7 copy-start.28
  182.9 4.6 copy-start.7
  182.9 4.6 copy-start.26
  192.7 5.1 %copy-start.24 = (f32[768]{0:T(1024)S(1)}, f32[768]{0:T(1024)}, u32[]{:S(2)}) copy-start(f32[768]{0:T(1024)} %get-tuple-element.55) | copy-start | bytes 9220
  216.1 194.2 %copy-start.15 = (f32[384]{0:T(512)S(1)}, f32[384]{0:T(512)}, u32[]{:S(2)}) copy-start(f32[384]{0:T(512)} %copy-done.14) | copy-start | bytes 4612
  216.1 194.2 %copy-start.18 = (f32[384]{0:T(512)S(1)}, f32[384]{0:T(512)}, u32[]{:S(2)}) copy-start(f32[384]{0:T(512)} %add_rsqrt_fusion) | copy-start | bytes 4612
  413.5 2.1 copy-start.8
  414.9 14.2 %slice-start = ((s8[4718592]{0:T(1024)(128)(4,1)}), s8[4194304]{0:T(1024)(128)(4,1)S(1)}, s32[]{:S(2)}) async-start(s8[4718592]{0:T(1024)(128)(4,1)} %bitcast.85), calls=%async_computation | async-start | bytes 8388608
  414.9 14.2 %slice-start.4 = ((s8[4718592]{0:T(1024)(128)(4,1)}), s8[4194304]{0:T(1024)(128)(4,1)S(1)}, s32[]{:S(2)}) async-start(s8[4718592]{0:T(1024)(128)(4,1)} %bitcast.89), calls=%async_computation.4 | async-start | bytes 8388608
  414.9 15.1 %slice-start.6 = ((s8[4718592]{0:T(1024)(128)(4,1)}), s8[4194304]{0:T(1024)(128)(4,1)S(1)}, s32[]{:S(2)}) async-start(s8[4718592]{0:T(1024)(128)(4,1)} %bitcast.91), calls=%async_computation.6 | async-start | bytes 8388608
  415.6 14.6 %slice-start.1 = ((s8[4718592]{0:T(1024)(128)(4,1)}), s8[524288]{0:T(1024)(128)(4,1)S(1)}, s32[]{:S(2)}) async-start(s8[4718592]{0:T(1024)(128)(4,1)} %bitcast.85), calls=%async_computation.1 | async-start | bytes 1048576
  415.6 14.7 %slice-start.5 = ((s8[4718592]{0:T(1024)(128)(4,1)}), s8[524288]{0:T(1024)(128)(4,1)S(1)}, s32[]{:S(2)}) async-start(s8[4718592]{0:T(1024)(128)(4,1)} %bitcast.89), calls=%async_computation.5 | async-start | bytes 1048576
  415.6 14.9 %slice-start.7 = ((s8[4718592]{0:T(1024)(128)(4,1)}), s8[524288]{0:T(1024)(128)(4,1)S(1)}, s32[]{:S(2)}) async-start(s8[4718592]{0:T(1024)(128)(4,1)} %bitcast.91), calls=%async_computation.7 | async-start | bytes 1048576
  429.1 11.0 %slice-start.2 = ((s8[4718592]{0:T(1024)(128)(4,1)}), s8[4194304]{0:T(1024)(128)(4,1)S(1)}, s32[]{:S(2)}) async-start(s8[4718592]{0:T(1024)(128)(4,1)} %bitcast.87), calls=%async_computation.2 | async-start | bytes 8388608
  430.5 9.6 %slice-start.3 = ((s8[4718592]{0:T(1024)(128)(4,1)}), s8[524288]{0:T(1024)(128)(4,1)S(1)}, s32[]{:S(2)}) async-start(s8[4718592]{0:T(1024)(128)(4,1)} %bitcast.87), calls=%async_computation.3 | async-start | bytes 1048576
  440.1 10.9 %copy-start.13 = (f32[16,768]{1,0:T(8,128)S(1)}, f32[16,768]{1,0:T(8,128)}, u32[]{:S(2)}) copy-start(f32[16,768]{1,0:T(8,128)} %get-tuple-element.47) | copy-start | bytes 147460
  440.1 10.9 %copy-start.19 = (f32[768]{0:T(1024)S(1)}, f32[768]{0:T(1024)}, u32[]{:S(2)}) copy-start(f32[768]{0:T(1024)} %get-tuple-element.54) | copy-start | bytes 9220
  440.1 52.1 %copy-start.12 = (f32[12,384]{1,0:T(8,128)S(1)}, f32[12,384]{1,0:T(8,128)}, u32[]{:S(2)}) copy-start(f32[12,384]{1,0:T(8,128)} %param.19) | copy-start | bytes 55300
  440.1 52.1 %copy-start.16 = (f32[12,384]{1,0:T(8,128)S(1)}, f32[12,384]{1,0:T(8,128)}, u32[]{:S(2)}) copy-start(f32[12,384]{1,0:T(8,128)} %param.23) | copy-start | bytes 55300
  440.1 52.0 %copy-start.17 = (f32[12,384]{1,0:T(8,128)S(1)}, f32[12,384]{1,0:T(8,128)}, u32[]{:S(2)}) copy-start(f32[12,384]{1,0:T(8,128)} %param.27) | copy-start | bytes 55300

commit v2 on v1

v2 whole, which is shorter than its diff:
```python
import functools

import jax
import jax.numpy as jnp
from jax import lax
from jax.experimental import pallas as pl
from jax.experimental.pallas import tpu as pltpu
from jax.sharding import PartitionSpec as P

HEADS = 12
norm_eps = 1e-05
beta_one = 0.9
beta_two = 0.999
adam_eps = 1e-08
adam_count = 5.0
rate_matrix = 0.02
rate_vector = 0.1
decay_matrix = 0.1
score_scale = 0.125
VMEM_LIMIT = 60 << 20
MESH = pl.DeviceIdType.MESH
BF = jnp.bfloat16
F32 = jnp.float32


def nt(left, right):
    return lax.dot_general(left, right, (((1,), (1,)), ((), ())), preferred_element_type=F32)


def nn(left, right):
    return lax.dot_general(left, right, (((1,), (0,)), ((), ())), preferred_element_type=F32)


def tn(left, right):
    return lax.dot_general(left, right, (((0,), (0,)), ((), ())), preferred_element_type=F32)


def vmem():
    return pl.BlockSpec(memory_space=pltpu.VMEM)


def normalize(values):
    center = values - jnp.mean(values, axis=-1, keepdims=True)
    inverse = lax.rsqrt(jnp.mean(center * center, axis=-1, keepdims=True) + norm_eps)
    return center * inverse, inverse


def norm_back(upstream, normed, inverse, gain):
    scaled = upstream * gain
    inner = (
        scaled
        - jnp.mean(scaled, axis=-1, keepdims=True)
        - normed * jnp.mean(scaled * normed, axis=-1, keepdims=True)
    )
    return (inverse * inner, jnp.sum(upstream * normed, axis=0), jnp.sum(upstream, axis=0))


def gelu_exact(values):
    return 0.5 * values * (1.0 + lax.erf(values * 0.7071067811865476))


def gelu_slope(values):
    return (
        0.5 * (1.0 + lax.erf(values * 0.7071067811865476))
        + values * jnp.exp(-0.5 * values * values) * 0.3989422804014327
    )


def adam_update(weight, gradient, first, second, rate, decay):
    first_new = beta_one * first + (1.0 - beta_one) * gradient
    second_new = beta_two * second + (1.0 - beta_two) * gradient * gradient
    first_hat = first_new / (1.0 - beta_one**adam_count)
    second_hat = second_new / (1.0 - beta_two**adam_count)
    updated = weight - rate * (first_hat / (jnp.sqrt(second_hat) + adam_eps) + decay * weight)
    return (updated, first_new, second_new)


class Place:
    def __init__(self, sizes):
        self.nd, self.nf, self.ns = sizes
        self.nh = self.nd // 2
        self.dp = lax.axis_index("dp")
        self.x = lax.axis_index("fsdp")
        self.z = lax.axis_index("seq")
        self.core = lax.rem(self.dp, 2)
        self.hi = self.dp // 2

    def sibling(self):
        return {"dp": self.hi * 2 + 1 - self.core}

    def x_peer(self, k):
        return {"fsdp": lax.rem(self.x + k, self.nf)}

    def y_hi(self, k):
        return lax.rem(self.hi + k, self.nh)

    def y_peer(self, k):
        return {"dp": self.y_hi(k) * 2 + self.core}

    def z_at(self, k):
        return lax.rem(self.z + k + self.ns, self.ns)

    def z_peer(self, k):
        return {"seq": self.z_at(k)}

    def everyone(self):
        out = [self.sibling()]
        out += [self.x_peer(k) for k in range(1, self.nf)]
        out += [self.y_peer(k) for k in range(1, self.nh)]
        out += [self.z_peer(k) for k in range(1, self.ns)]
        return out

    def barrier(self):
        sem = pltpu.get_barrier_semaphore()
        peers = self.everyone()
        for peer in peers:
            pl.semaphore_signal(sem, inc=1, device_id=peer, device_id_type=MESH)
        pl.semaphore_wait(sem, len(peers))


def remote(src, dst, send, recv, peer):
    return pltpu.make_async_remote_copy(
        src_ref=src, dst_ref=dst, send_sem=send, recv_sem=recv, device_id=peer, device_id_type=MESH
    )


def gather_kernel(
    sizes, frames_ref, aw_ref, ew_ref, cw_ref, vec_ref,
    a_ref, e_ref, c_ref, v_ref, h_ref,
    xs, xr, ys, yr, s1s, s1r, s2s, s2r, vs, vr, rs, ls, hr,
):
    at = Place(sizes)
    nf, nh, ns = at.nf, at.nh, at.ns
    rows, width = frames_ref.shape
    shard = aw_ref.shape[1]
    half = shard // 2
    at.barrier()
    v_ref[at.x] = vec_ref[...].astype(BF)
    vec_copies = []
    for k in range(1, nf):
        copy = remote(v_ref.at[at.x], v_ref.at[at.x], vs.at[k], vr.at[k], at.x_peer(k))
        copy.start()
        vec_copies.append(copy)

    def view(chunk, j, hi, core):
        if chunk < 2:
            first, count = ((0, 3), (3, 1))[chunk]
            cols = width // nh
            return a_ref.at[
                pl.ds(first, count),
                pl.ds(pl.multiple_of(j * shard + core * half, 16), half),
                pl.ds(pl.multiple_of(hi * cols, 128), cols),
            ]
        if chunk == 2:
            cols = e_ref.shape[1] // nh
            return e_ref.at[
                pl.ds(pl.multiple_of(j * shard + core * half, 16), half),
                pl.ds(pl.multiple_of(hi * cols, 128), cols),
            ]
        cols = width // nh
        deep = c_ref.shape[0] // nf
        return c_ref.at[
            pl.ds(pl.multiple_of(j * deep + core * (deep // 2), 16), deep // 2),
            pl.ds(pl.multiple_of(hi * cols, 128), cols),
        ]

    own = pl.multiple_of(at.x * shard, 16)
    x_copies = {}

    def send_chunk(chunk):
        for k in range(1, nf):
            piece = view(chunk, at.x, at.hi, at.core)
            copy = remote(piece, piece, xs.at[chunk, k], xr.at[chunk, k], at.x_peer(k))
            copy.start()
            x_copies[chunk, k] = copy

    for u in range(3):
        a_ref[u, pl.ds(own, shard), :] = aw_ref[u].astype(BF)
    send_chunk(0)
    normed, _ = normalize(frames_ref[...])
    for copy in vec_copies:
        copy.wait()
    gain = jnp.concatenate([v_ref[j, 0:1, :] for j in range(nf)], axis=1).astype(F32)
    offset = jnp.concatenate([v_ref[j, 1:2, :] for j in range(nf)], axis=1).astype(F32)
    h_ref[pl.ds(pl.multiple_of(at.z * rows, 16), rows), :] = (normed * gain + offset).astype(BF)

    def block(b):
        return h_ref.at[pl.ds(pl.multiple_of(b * rows, 16), rows), :]

    def to_right(b):
        return remote(block(b), block(b), rs.at[b], hr.at[b], {"seq": at.z + 1})

    def to_left(b):
        return remote(block(b), block(b), ls.at[b], hr.at[b], {"seq": at.z - 1})

    @pl.when(at.z < ns - 1)
    def _():
        to_right(at.z).start()

    @pl.when(at.z > 0)
    def _():
        to_left(at.z).start()

    a_ref[3, pl.ds(own, shard), :] = aw_ref[3].astype(BF)
    send_chunk(1)
    e_ref[pl.ds(own, shard), :] = ew_ref[...].astype(BF)
    send_chunk(2)
    deep = cw_ref.shape[0]
    c_ref[pl.ds(pl.multiple_of(at.x * deep, 16), deep), :] = cw_ref[...].astype(BF)
    send_chunk(3)

    pending = []

    def forward(chunk):
        for k in range(1, nf):
            x_copies[chunk, k].wait_recv()
            j = lax.rem(at.x - k + nf, nf)
            piece = view(chunk, j, at.hi, at.core)
            copy = remote(piece, piece, s1s.at[chunk, k], s1r.at[chunk, k], at.sibling())
            copy.start()
            pending.append(copy)
            for m in range(1, nh):
                copy = remote(piece, piece, ys.at[chunk, k, m], yr.at[chunk, k, m], at.y_peer(m))
                copy.start()
                pending.append((copy, chunk, k, m))

    def relay(chunk):
        for k in range(1, nf):
            for m in range(1, nh):
                j = lax.rem(at.x - k + nf, nf)
                hi = lax.rem(at.hi - m + nh, nh)
                piece = view(chunk, j, hi, at.core)
                remote(piece, piece, ys.at[chunk, k, m], yr.at[chunk, k, m], at.y_peer(m)).wait_recv()
                copy = remote(piece, piece, s2s.at[chunk, k, m], s2r.at[chunk, k, m], at.sibling())
                copy.start()
                pending.append(copy)

    def hop(s):
        b = at.z - s

        @pl.when(b >= 0)
        def _():
            to_right(b).wait_recv()

            @pl.when(at.z < ns - 1)
            def _():
                to_right(b).start()

        d = at.z + s

        @pl.when(d < ns)
        def _():
            to_left(d).wait_recv()

            @pl.when(at.z > 0)
            def _():
                to_left(d).start()

    forward(0)
    hop(1)
    forward(1)
    relay(0)
    relay(1)
    for s in range(2, ns - 1):
        hop(s)
    forward(2)
    relay(2)
    if ns > 2:
        hop(ns - 1)
    forward(3)
    relay(3)
    for entry in pending:
        if isinstance(entry, tuple):
            entry[0].wait_send()
        else:
            entry.wait()
    for copy in x_copies.values():
        copy.wait_send()
    for b in range(ns):
        @pl.when(jnp.logical_and(b <= at.z, at.z < ns - 1))
        def _():
            to_right(b).wait_send()

        @pl.when(jnp.logical_and(b >= at.z, at.z > 0))
        def _():
            to_left(b).wait_send()


def gather_all(sizes, frames, aw, ew, cw, vec):
    nd, nf, ns = sizes
    nh = nd // 2
    rows, width = frames.shape
    deep = cw.shape[0] * nf
    dma = pltpu.SemaphoreType.DMA
    return pl.pallas_call(
        functools.partial(gather_kernel, sizes),
        out_shape=(
            jax.ShapeDtypeStruct((4, width, width), BF),
            jax.ShapeDtypeStruct((width, ew.shape[1]), BF),
            jax.ShapeDtypeStruct((deep, width), BF),
            jax.ShapeDtypeStruct((nf, 16, vec.shape[1]), BF),
            jax.ShapeDtypeStruct((rows * ns, width), BF),
        ),
        in_specs=[vmem()] * 5,
        out_specs=(vmem(),) * 5,
        scratch_shapes=[
            dma((4, nf)), dma((4, nf)),
            dma((4, nf, nh)), dma((4, nf, nh)),
            dma((4, nf)), dma((4, nf)),
            dma((4, nf, nh)), dma((4, nf, nh)),
            dma((nf,)), dma((nf,)),
            dma((ns,)), dma((ns,)), dma((ns,)),
        ],
        name="gather",
        compiler_params=pltpu.CompilerParams(
            collective_id=0, has_side_effects=True, vmem_limit_bytes=VMEM_LIMIT
        ),
    )(frames, aw, ew, cw, vec)


def attention_kernel(chunk, q_ref, k_ref, v_ref, ctx_ref, lse_ref):
    rows = q_ref.shape[0]
    lo = lax.broadcasted_iota(jnp.int32, (chunk, 128), 1) < 64

    def pair(p, carry):
        col = pl.ds(pl.multiple_of(p * 128, 128), 128)
        k2 = k_ref[:, col]
        v2 = v_ref[:, col]
        for c in range(rows // chunk):
            part = pl.ds(c * chunk, chunk)
            q2 = q_ref[part, col]
            ctx, lse = [], []
            for h in range(2):
                mask = lo if h == 0 else jnp.logical_not(lo)
                s = nt(jnp.where(mask, q2, jnp.zeros_like(q2)), k2) * score_scale
                largest = jnp.max(s, axis=-1, keepdims=True)
                e = jnp.exp(s - largest)
                total = jnp.sum(e, axis=-1, keepdims=True)
                ctx.append(nn((e * (1.0 / total)).astype(BF), v2))
                lse.append(largest + jnp.log(total))
            ctx_ref[part, col] = jnp.where(lo, ctx[0], ctx[1])
            lse_ref[p, part, :] = jnp.where(lo, lse[0], lse[1])
        return carry

    lax.fori_loop(0, q_ref.shape[1] // 128, pair, 0)


def attention(q, k, v):
    rows, width = q.shape
    return pl.pallas_call(
        functools.partial(attention_kernel, rows),
        out_shape=(
            jax.ShapeDtypeStruct((rows, width), F32),
            jax.ShapeDtypeStruct((width // 128, rows, 128), F32),
        ),
        in_specs=[vmem()] * 3,
        out_specs=(vmem(), vmem()),
        name="attention",
        compiler_params=pltpu.CompilerParams(vmem_limit_bytes=VMEM_LIMIT),
    )(q, k, v)


def back_kernel(
    sizes, q_ref, k_ref, v_ref, dc_ref, ctx_ref, lse_ref, ht_ref, w_ref, gm_ref, frames_ref,
    vec_ref, gv_ref, gc_ref, ge_ref, go_ref,
    out_ref, ig_ref, ov_ref,
    ga, own, rc, rx, ry, rz, dkt, dvt, dqt, dhs, dhr, dho, vb, vx, vy, vz,
    os, cs, cr, xs, xr, ys, yr, zs, zr, azs, azr, ays, ayr, acs, acr, ds, dm, vs, vr,
):
    at = Place(sizes)
    nf, nh, ns = at.nf, at.nh, at.ns
    rows, width = q_ref.shape
    half = rc.shape[4]
    cols = width // nh
    chunks = rc.shape[0]
    per = chunks // 3
    at.barrier()
    mine = pl.ds(pl.multiple_of(at.core * half, 16), half)
    other = pl.ds(pl.multiple_of((1 - at.core) * half, 16), half)

    def lanes(s, hi):
        return pl.ds(pl.multiple_of(hi * cols + s * 128, 128), 128)

    for s in range(per):
        for hi in range(nh):
            for part in range(2):
                pltpu.make_async_copy(
                    go_ref.at[:, pl.ds(part * half, half), pl.ds(hi * cols + s * 128, 128)],
                    ga.at[s, hi, :, part, 3],
                    os.at[2],
                ).start()

    def own_whole(slot):
        return pltpu.make_async_copy(own.at[slot], own.at[slot], os.at[slot])

    def c_whole(n):
        return remote(rc.at[n], rc.at[n], cs.at[n], cr.at[n], at.sibling())

    def c_send(n):
        slot = lax.rem(n, 2)

        @pl.when(n < per)
        def _():
            for hi in range(nh):
                block = lanes(n, hi)
                remote(
                    gc_ref.at[:, :, other, block], rc.at[n, hi], cs.at[n], cr.at[n], at.sibling()
                ).start()
                pltpu.make_async_copy(
                    gc_ref.at[:, :, mine, block], own.at[slot, hi], os.at[slot]
                ).start()

        @pl.when(jnp.logical_and(n >= per, n < 2 * per))
        def _():
            for hi in range(nh):
                for u in range(4):
                    block = pl.ds(pl.multiple_of(u * width + hi * cols + (n - per) * 128, 128), 128)
                    remote(
                        ge_ref.at[:, other, block], rc.at[n, hi, :, u], cs.at[n], cr.at[n], at.sibling()
                    ).start()
                    pltpu.make_async_copy(
                        ge_ref.at[:, mine, block], own.at[slot, hi, :, u], os.at[slot]
                    ).start()

        @pl.when(jnp.logical_and(n >= 2 * per, n < chunks))
        def _():
            remote(
                ga.at[n - 2 * per, :, :, 1 - at.core], rc.at[n], cs.at[n], cr.at[n], at.sibling()
            ).start()

    def x_copy(n, k):
        peer = lax.rem(at.x + k, nf)
        return remote(rc.at[n, :, peer], rx.at[n, k - 1], xs.at[n, k - 1], xr.at[n, k - 1], at.x_peer(k))

    def y_copy(n, m):
        return remote(
            rx.at[n, 0, at.y_hi(m)], ry.at[n, m - 1], ys.at[n, m - 1], yr.at[n, m - 1], at.y_peer(m)
        )

    def z_copy(n, k):
        return remote(
            ry.at[n, 0, at.z_at(k)], rz.at[n, k - 1], zs.at[n, k - 1], zr.at[n, k - 1], at.z_peer(k)
        )

    def spot(n):
        return n // per, lax.rem(n, per)

    def az_copy(n, k, z=None):
        g, s = spot(n)
        place = out_ref.at[g, at.z if z is None else z, mine, lanes(s, at.hi)]
        return remote(place, place, azs.at[n, k - 1], azr.at[n, k - 1], at.z_peer(k))

    def ay_copy(n, m):
        g, s = spot(n)
        place = out_ref.at[g, :, mine, lanes(s, at.hi)]
        return remote(place, place, ays.at[n, m - 1], ayr.at[n, m - 1], at.y_peer(m))

    def ac_start(n):
        g, s = spot(n)
        for hi in range(nh):
            place = out_ref.at[g, :, mine, lanes(s, hi)]
            remote(place, place, acs.at[n], acr.at[n], at.sibling()).start()

    def ac_whole(n):
        return remote(rx.at[n, 0], rx.at[n, 0], acs.at[n], acr.at[n], at.sibling())

    def stage_c(n):
        c_whole(n).wait_recv()
        slot = lax.rem(n, 2)

        @pl.when(n < 2 * per)
        def _():
            own_whole(slot).wait()

            def add(i, carry):
                hi, j, u = i // (nf * 4), lax.rem(i // 4, nf), lax.rem(i, 4)
                rc[n, hi, j, u] = (rc[n, hi, j, u].astype(F32) + own[slot, hi, j, u].astype(F32)).astype(BF)
                return carry

            lax.fori_loop(0, nh * nf * 4, add, 0)

        @pl.when(n >= 2 * per)
        def _():
            def add(i, carry):
                hi, j, u = i // (nf * 4), lax.rem(i // 4, nf), lax.rem(i, 4)
                rc[n, hi, j, u] = (
                    rc[n, hi, j, u].astype(F32) + ga[n - 2 * per, hi, j, at.core, u].astype(F32)
                ).astype(BF)
                return carry

            lax.fori_loop(0, nh * nf * 4, add, 0)

        for k in range(1, nf):
            x_copy(n, k).start()

    def stage_x(n):
        for k in range(1, nf):
            x_copy(n, k).wait_recv()

        def add(i, carry):
            hi, u = i // 4, lax.rem(i, 4)
            total = rc[n, hi, at.x, u].astype(F32)
            for k in range(nf - 1):
                total += rx[n, k, hi, u].astype(F32)
            rx[n, 0, hi, u] = total.astype(BF)
            return carry

        lax.fori_loop(0, nh * 4, add, 0)
        for m in range(1, nh):
            y_copy(n, m).start()

    def stage_y(n):
        for m in range(1, nh):
            y_copy(n, m).wait_recv()

        def add(u, carry):
            total = rx[n, 0, at.hi, u].astype(F32)
            for m in range(nh - 1):
                total += ry[n, m, u].astype(F32)
            ry[n, 0, u] = total.astype(BF)
            return carry

        lax.fori_loop(0, 4, add, 0)
        for k in range(1, ns):
            z_copy(n, k).start()

    def stage_z(n):
        for k in range(1, ns):
            z_copy(n, k).wait_recv()
        total = ry[n, 0, at.z].astype(F32)
        for k in range(ns - 1):
            total += rz[n, k].astype(F32)
        g, s = spot(n)
        out_ref[g, at.z, mine, lanes(s, at.hi)] = total.astype(BF)
        for k in range(1, ns):
            az_copy(n, k).start()

    def stage_az(n):
        for k in range(1, ns):
            az_copy(n, k, at.z_at(-k)).wait_recv()
        for m in range(1, nh):
            ay_copy(n, m).start()

    def stage_ay(n):
        for m in range(1, nh):
            ay_copy(n, m).wait_recv()
        ac_start(n)

    lo = lax.broadcasted_iota(jnp.int32, (rows, 128), 1) < 64

    def pair(step):
        s, hi = step // nh, lax.rem(step, nh)
        p = hi * per + s
        col = pl.ds(pl.multiple_of(p * 128, 128), 128)
        k2 = k_ref[:, col]
        v2 = v_ref[:, col]
        q2 = q_ref[:, col]
        dc2 = dc_ref[:, col]
        both = dc2.astype(F32) * ctx_ref[:, col]
        lse2 = lse_ref[p]
        dq, dk, dv = [], None, None
        for h in range(2):
            mask = lo if h == 0 else jnp.logical_not(lo)
            qm = jnp.where(mask, q2, jnp.zeros_like(q2))
            dmask = jnp.where(mask, dc2, jnp.zeros_like(q2))
            lse = lse2[:, 0:1] if h == 0 else lse2[:, 64:65]
            dot = jnp.sum(jnp.where(mask, both, 0.0), axis=-1, keepdims=True)
            probs = jnp.exp(nt(qm, k2) * score_scale - lse)
            slopes = nt(dmask, v2)
            dscore = (probs * (slopes - dot) * score_scale).astype(BF)
            dq.append(nn(dscore, k2))
            a = nn(dmask.T, probs.astype(BF))
            b = nn(qm.T, dscore)
            dv = a if dv is None else dv + a
            dk = b if dk is None else dk + b
        dq2 = jnp.where(lo, dq[0], dq[1])
        gv_ref_row = jnp.sum(dq2, axis=0, keepdims=True)
        vb[2, 0:1, col] = gv_ref_row
        dq2 = dq2.astype(BF)
        dqt[col, :] = dq2.T
        dkb = dk.astype(BF)
        dvb = dv.astype(BF)
        dkt[col, :] = dkb
        dvt[col, :] = dvb
        shard = 2 * half
        for j in range(nf):
            for part in range(2):
                here = pl.ds(j * shard + part * half, half)
                ga[s, hi, j, part, 0] = nn(
                    ht_ref[here, pl.ds(pl.multiple_of(at.z * rows, 128), rows)], dq2
                ).astype(BF)
                ga[s, hi, j, part, 1] = nt(ht_ref[here, :], dkb).astype(BF)
                ga[s, hi, j, part, 2] = nt(ht_ref[here, :], dvb).astype(BF)

    def spread():
        def block(b):
            part = pl.ds(pl.multiple_of(b * rows, 128), rows)
            return nn(w_ref[1], dkt[:, part]) + nn(w_ref[2], dvt[:, part])

        for k in range(1, ns):
            dhs[k - 1] = block(at.z_at(k)).astype(BF)
            d_copy(k).start()
        dho[...] = block(at.z) + nn(w_ref[0], dqt[...])

    def d_copy(k):
        return remote(dhs.at[k - 1], dhr.at[k - 1], ds.at[k - 1], dm.at[k - 1], at.z_peer(k))

    def first_norm():
        for k in range(1, ns):
            d_copy(k).wait_recv()
        total = dho[...]
        for k in range(ns - 1):
            total += dhr[k].astype(F32)
        total = total.T
        normed, inverse = normalize(frames_ref[...])
        scaled = total * vec_ref[0:1, :]
        inner = (
            scaled
            - jnp.mean(scaled, axis=-1, keepdims=True)
            - normed * jnp.mean(scaled * normed, axis=-1, keepdims=True)
        )
        ig_ref[...] = gm_ref[...] + inverse * inner
        vb[1] = gv_ref[...]
        vb[1, 0:1, :] = jnp.sum(total * normed, axis=0, keepdims=True)
        vb[1, 1:2, :] = jnp.sum(total, axis=0, keepdims=True)
        vb[1, 2:3, :] = vb[2, 0:1, :]

    def v_core():
        return remote(vb.at[1], vb.at[0], vs.at[0], vr.at[0], at.sibling())

    def v_x(k):
        return remote(vx.at[at.x], vx.at[at.x], vs.at[k], vr.at[k], at.x_peer(k))

    def v_y(m):
        return remote(vy.at[at.hi], vy.at[at.hi], vs.at[nf + m], vr.at[nf + m], at.y_peer(m))

    def v_z(k):
        return remote(
            vz.at[at.z], vz.at[at.z], vs.at[nf + nh + k], vr.at[nf + nh + k], at.z_peer(k)
        )

    def v_step(i):
        if i == 0:
            v_core().start()
        elif i == 1:
            v_core().wait_recv()
            vx[at.x] = vb[0] + vb[1]
            for k in range(1, nf):
                v_x(k).start()
        elif i == 2:
            for k in range(1, nf):
                v_x(k).wait_recv()
            total = vx[0]
            for j in range(1, nf):
                total += vx[j]
            vy[at.hi] = total
            for m in range(1, nh):
                v_y(m).start()
        elif i == 3:
            for m in range(1, nh):
                v_y(m).wait_recv()
            total = vy[0]
            for j in range(1, nh):
                total += vy[j]
            vz[at.z] = total
            for k in range(1, ns):
                v_z(k).start()
        else:
            for k in range(1, ns):
                v_z(k).wait_recv()
            total = vz[0]
            for j in range(1, ns):
                total += vz[j]
            ov_ref[...] = total

    c_send(0)
    c_send(1)
    pairs = width // 128

    def step(n, carry):
        @pl.when(n < chunks)
        def _():
            stage_c(n)

        @pl.when(n < pairs)
        def _():
            pair(n)

        @pl.when(n == 2 * per - 2)
        def _():
            pltpu.make_async_copy(ga.at[:, :, :, :, 3], ga.at[:, :, :, :, 3], os.at[2]).wait()

        @pl.when(n + 2 < chunks)
        def _():
            c_send(n + 2)

        @pl.when(n == pairs)
        def _():
            spread()

        for lag, stage in ((1, stage_x), (2, stage_y), (3, stage_z), (4, stage_az), (5, stage_ay)):
            @pl.when(jnp.logical_and(n >= lag, n < chunks + lag))
            def _(lag=lag, stage=stage):
                stage(n - lag)

        @pl.when(n == chunks + 2)
        def _():
            first_norm()
            v_step(0)

        @pl.when(n == chunks + 3)
        def _():
            v_step(1)

        @pl.when(n == chunks + 4)
        def _():
            v_step(2)

        return carry

    lax.fori_loop(0, chunks + 5, step, 0)
    v_step(3)
    for n in range(chunks):
        ac_whole(n).wait()
    v_step(4)

    def drain(n, carry):
        c_whole(n).wait_send()
        for k in range(1, nf):
            x_copy(n, k).wait_send()
        for m in range(1, nh):
            y_copy(n, m).wait_send()
            ay_copy(n, m).wait_send()
        for k in range(1, ns):
            z_copy(n, k).wait_send()
            az_copy(n, k).wait_send()
        return carry

    lax.fori_loop(0, chunks, drain, 0)
    for k in range(1, ns):
        d_copy(k).wait_send()
        v_z(k).wait_send()
    for k in range(1, nf):
        v_x(k).wait_send()
    for m in range(1, nh):
        v_y(m).wait_send()
    v_core().wait_send()


def back_all(sizes, q, k, v, dc, ctx, lse, ht, w, gm, frames, vec, gv, gc, ge, go):
    nd, nf, ns = sizes
    nh = nd // 2
    rows, width = q.shape
    shard = go.shape[1]
    half = shard // 2
    every = k.shape[0]
    per = width // nh // 128
    chunks = 3 * per
    xn, yn, zn = max(nf - 1, 1), max(nh - 1, 1), max(ns - 1, 1)
    dma = pltpu.SemaphoreType.DMA
    anywhere = pl.BlockSpec(memory_space=pl.ANY)
    return pl.pallas_call(
        functools.partial(back_kernel, sizes),
        out_shape=(
            jax.ShapeDtypeStruct((3, 4, shard, width), BF),
            jax.ShapeDtypeStruct((rows, width), F32),
            jax.ShapeDtypeStruct((16, width), F32),
        ),
        in_specs=[vmem()] * 12 + [anywhere] * 3,
        out_specs=(vmem(),) * 3,
        scratch_shapes=[
            pltpu.VMEM((per, nh, nf, 2, 4, half, 128), BF),
            pltpu.VMEM((2, nh, nf, 4, half, 128), BF),
            pltpu.VMEM((chunks, nh, nf, 4, half, 128), BF),
            pltpu.VMEM((chunks, xn, nh, 4, half, 128), BF),
            pltpu.VMEM((chunks, yn, 4, half, 128), BF),
            pltpu.VMEM((chunks, zn, half, 128), BF),
            pltpu.VMEM((width, every), BF),
            pltpu.VMEM((width, every), BF),
            pltpu.VMEM((width, rows), BF),
            pltpu.VMEM((zn, width, rows), BF),
            pltpu.VMEM((zn, width, rows), BF),
            pltpu.VMEM((width, rows), F32),
            pltpu.VMEM((3, 16, width), F32),
            pltpu.VMEM((nf, 16, width), F32),
            pltpu.VMEM((nh, 16, width), F32),
            pltpu.VMEM((ns, 16, width), F32),
            dma((3,)),
            dma((chunks,)), dma((chunks,)),
            dma((chunks, xn)), dma((chunks, xn)),
            dma((chunks, yn)), dma((chunks, yn)),
            dma((chunks, zn)), dma((chunks, zn)),
            dma((chunks, zn)), dma((chunks, zn)),
            dma((chunks, yn)), dma((chunks, yn)),
            dma((chunks,)), dma((chunks,)),
            dma((zn,)), dma((zn,)),
            dma((nf + nh + ns,)), dma((nf + nh + ns,)),
        ],
        name="back",
        compiler_params=pltpu.CompilerParams(
            collective_id=1, has_side_effects=True, vmem_limit_bytes=67043328
        ),
    )(q, k, v, dc, ctx, lse, ht, w, gm, frames, vec, gv, gc, ge, go)


def adam_kernel(g_ref, w_ref, m_ref, v_ref, go_ref, wo_ref, mo_ref, vo_ref):
    gradient = g_ref[...].reshape(w_ref.shape).astype(F32)
    go_ref[...] = gradient
    wo_ref[...], mo_ref[...], vo_ref[...] = adam_update(
        w_ref[...], gradient, m_ref[...], v_ref[...], rate_matrix, decay_matrix
    )


def adam(group, out, weight, first, second, name):
    shard, width = out.shape[2:]
    rows = min(192, shard)
    parts = shard // rows
    if group == 1:
        grid_map = lambda u, r: (r, u)
    else:
        grid_map = lambda u, r: (u * parts + r, 0)
    spec = pl.BlockSpec((rows, width), grid_map)
    shape = jax.ShapeDtypeStruct(weight.shape, F32)
    return pl.pallas_call(
        adam_kernel,
        grid=(4, parts),
        out_shape=(shape,) * 4,
        in_specs=[pl.BlockSpec((None, None, rows, width), lambda u, r: (group, u, r, 0))] + [spec] * 3,
        out_specs=(spec,) * 4,
        name=name,
        compiler_params=pltpu.CompilerParams(vmem_limit_bytes=67043328),
    )(out, weight, first, second)


def on_device(
    sizes,
    frames_in,
    cotangent,
    attention_weight,
    expand_weight,
    contract_weight,
    vectors,
    first_attention,
    first_expand,
    first_contract,
    first_vectors,
    second_attention,
    second_expand,
    second_contract,
    second_vectors,
):
    nd, nf, ns = sizes
    frames = frames_in[0]
    upstream = cotangent[0]
    rows, width = frames.shape
    shard = attention_weight.shape[1]
    full = expand_weight.shape[1]
    vec_pad = jnp.pad(vectors, ((0, 4), (0, 0)))
    aw, ew, cw, vw, h_all = gather_all(
        sizes, frames, attention_weight, expand_weight, contract_weight, vec_pad
    )
    vec = jnp.transpose(vw, (1, 0, 2)).reshape(16, width)[:12].astype(F32)
    bias_expand = vec[8:].reshape(-1)
    h_own = lax.dynamic_slice_in_dim(h_all, lax.axis_index("seq") * rows, rows, 0)
    queries = (nn(h_own, aw[0]) + vec[2]).astype(BF)
    key_rows = nn(h_all, aw[1]).astype(BF)
    value_rows = (nn(h_all, aw[2]) + vec[3]).astype(BF)
    context_wide, log_total = attention(queries, key_rows, value_rows)
    context = context_wide.astype(BF)
    middle = frames + nn(context, aw[3]) + vec[4]
    normed_two, inverse_two = normalize(middle)
    hidden_two = (normed_two * vec[5] + vec[6]).astype(BF)
    expanded = nn(hidden_two, ew) + bias_expand
    activated = gelu_exact(expanded).astype(BF)
    frames_out = middle + nn(activated, cw) + vec[7]
    upstream_bf = upstream.astype(BF)
    grad_contract = tn(activated, upstream_bf).astype(BF)
    grad_expanded = nt(upstream_bf, cw) * gelu_slope(expanded)
    grad_expanded_bf = grad_expanded.astype(BF)
    grad_expand = tn(hidden_two, grad_expanded_bf).astype(BF)
    grad_hidden_two = nt(grad_expanded_bf, ew)
    back_two, gain_two_grad, bias_two_grad = norm_back(
        grad_hidden_two, normed_two, inverse_two, vec[5]
    )
    grad_middle = upstream + back_two
    grad_middle_bf = grad_middle.astype(BF)
    grad_output_w = tn(context, grad_middle_bf).astype(BF)
    grad_context = nt(grad_middle_bf, aw[3]).astype(BF)
    small = jnp.stack(
        [
            jnp.sum(grad_context.astype(F32), axis=0),
            jnp.sum(grad_middle, axis=0),
            gain_two_grad,
            bias_two_grad,
            jnp.sum(upstream, axis=0),
        ]
    )
    gv = jnp.concatenate(
        [jnp.zeros((3, width), F32), small, jnp.sum(grad_expanded, axis=0).reshape(-1, width),
         jnp.zeros((4, width), F32)], axis=0
    )
    out, input_gradient, gv_sum = back_all(
        sizes,
        queries,
        key_rows,
        value_rows,
        grad_context,
        context_wide,
        log_total,
        h_all.T,
        aw,
        grad_middle,
        frames,
        vec[:8],
        gv,
        grad_contract.reshape(nf, 4, shard, width),
        grad_expand.reshape(nf, shard, full),
        grad_output_w.reshape(nf, shard, width),
    )
    owned_vec = lax.dynamic_slice_in_dim(
        gv_sum[:12], lax.axis_index("fsdp") * (width // nf), width // nf, 1
    )
    flat = (4 * shard, width)
    contract_out = adam(0, out, contract_weight, first_contract, second_contract, "adam_contract")
    expand_out = adam(1, out, expand_weight, first_expand, second_expand, "adam_expand")
    attention_out = adam(
        2, out, attention_weight.reshape(flat), first_attention.reshape(flat),
        second_attention.reshape(flat), "adam_attention"
    )
    attention_out = [each.reshape(attention_weight.shape) for each in attention_out]
    vector_out = (owned_vec,) + adam_update(
        vectors, owned_vec, first_vectors, second_vectors, rate_vector, 0.0
    )
    result = [frames_out[None], input_gradient[None]]
    for i in range(4):
        result += [attention_out[i], expand_out[i], contract_out[i], vector_out[i]]
    return tuple(result)


def solution(mesh):
    sizes = (mesh.shape["dp"], mesh.shape["fsdp"], mesh.shape["seq"])
    data = P(("dp", "fsdp"), "seq", None)
    state = (P(None, "fsdp", None), P("fsdp", None), P("fsdp", None), P(None, "fsdp"))
    return jax.shard_map(
        functools.partial(on_device, sizes),
        mesh=mesh,
        in_specs=(data, data) + state * 3,
        out_specs=(data, data) + state * 4,
        check_vma=False,
    )
```

time: 499 us -> 402 us (0.81)
  other arithmetic: 45.5 us -> 3.14 us
  blocking collectives: 41.1 us -> 0 us
  matrix products: 75.4 us -> 56.3 us
  Pallas kernels: 314 us -> 322 us
    psum x1 -> x0, blocking collectives: 41.1 us -> none  [on_device(): lax.psum(jnp.stack([gain_one_grad, bias_one_grad]), ('dp', 'fsdp', 'seq'))]
    sub x4 -> x1, other arithmetic: 34.6 us -> 1.43 us  [adam_update(): weight - rate * (first_hat / (jnp.sqrt(second_hat) + adam_eps) + decay *...]
    dot_general x4 -> x0, matrix products: 18.4 us -> none  [the longest x1 6.33 us: on_device(): lax.dot_general(dvt_bf, aw[2], (((0,), (1,)), ((), ())), preferred_elemen...]
    pallas_call x2 -> x4, Pallas kernels: 219 us -> 228 us  [the longest x1 182 us: back_all(): pl.pallas_call(functools.partial(back_kernel, sizes), out_shape=(jax.Shap...]
    dot_general x4 -> x3, matrix products: 17.6 us -> 15.5 us  [nt(): lax.dot_general(left, right, (((1,), (1,)), ((), ())), preferred_element_...]
    dot_general x4 -> x3, matrix products: 11.8 us -> 13.1 us  [tn(): lax.dot_general(left, right, (((0,), (0,)), ((), ())), preferred_element_...]
where the time goes in v2:
time: 402 us; the launch traced here: 401 us
  Pallas kernels  322 us (80%)
  matrix products  56.3 us (14%)
  local copies, waits for them, and re-layouts  17.8 us (4%)
    pallas_call x1, Pallas kernels, back_all(): pl.pallas_call(functools.partial(back_kernel, sizes), out_shape=(jax.Shap...  182 us
    pallas_call x1, Pallas kernels, gather_all(): pl.pallas_call(functools.partial(gather_kernel, sizes), out_shape=(jax.Sh...  73.5 us
    pallas_call x3, Pallas kernels, adam(): pl.pallas_call(adam_kernel, grid=(4, parts), out_shape=(shape,) * 4, in_s...  46.7 us
    dot_general x6, matrix products, nn(): lax.dot_general(left, right, (((1,), (0,)), ((), ())), preferred_element_...  27.7 us
    pallas_call x1, Pallas kernels, attention(): pl.pallas_call(functools.partial(attention_kernel, rows), out_shape=(jax....  20.8 us
    dot_general x3, matrix products, nt(): lax.dot_general(left, right, (((1,), (1,)), ((), ())), preferred_element_...  15.5 us
    dot_general x3, matrix products, tn(): lax.dot_general(left, right, (((0,), (0,)), ((), ())), preferred_element_...  13.1 us

profile of v2, /device:TPU:0, one launch (start us, length us, event | category | flops | bytes accessed | tf_op | source)
XLA Modules:
  0.0 400.6 jit_solution(14753287404991469074)
XLA Ops:
  0.7 1.4 pad.4.vec_ref
  2.0 73.5 %gather.1 = (bf16[4,768,768]{2,1,0:T(8,128)(2,1)}, bf16[768,3072]{1,0:T(8,128)(2,1)}, bf16[3072,768]{1,0:T(8,128)(2,1)}, bf16[2,16,384]{2,1,0:T(8,128)(2,1)}, bf16[1536,768]{1,0:T(8,128)(2,1)}) custom-call(f32[384,768]{1,0:T(8,128)} %bitcast.74, f32[4,384,768]{2,1,0:T(8,128)} %aw_ref.1, f32[384,3072]{1,0:T(8,128)} %w_ref.2, f32[1536,768]{1,0:T(8,128)} %w_ref.3, ...), custom_call_target="tpu_custom_call" | custom-call | tf_op jit(solution)/shard_map/gather/pallas_call | solution.py:295
  75.5 0.0 copy-start.4
  75.5 0.9 slice_convert_fusion
  76.4 0.0 copy-start.5
  76.4 0.1 slice_reduce_fusion
  76.5 2.9 fusion.8.q_ref
  79.4 0.0 copy-done.4
  79.4 4.7 %convolution_convert_fusion.2.k_ref = bf16[1536,768]{1,0:T(8,128)(2,1)} fusion(bf16[1536,768]{1,0:T(8,128)(2,1)S(1)} %copy-done.4, bf16[4,768,768]{2,1,0:T(8,128)(2,1)} %get-tuple-element.41.w_ref), kind=kOutput, calls=%fused_computation.12 | convolution fusion | flops 1813118976 | bytes 5898240 | tf_op jit(solution)/shard_map/dot_general | solution.py:31
  84.1 4.7 %add_convert_fusion.v_ref = bf16[1536,768]{1,0:T(8,128)(2,1)} fusion(bf16[1536,768]{1,0:T(8,128)(2,1)S(1)} %copy-done.4, f32[768]{0:T(1024)S(1)} %add.114, bf16[4,768,768]{2,1,0:T(8,128)(2,1)} %get-tuple-element.41.w_ref), kind=kOutput, calls=%fused_computation.10 | convolution fusion | flops 1814298624 | bytes 5901312 | tf_op jit(solution)/shard_map/dot_general | solution.py:31
  88.8 0.0 copy-start
  88.8 20.8 %attention.1 = (f32[384,768]{1,0:T(8,128)}, f32[6,384,128]{2,1,0:T(8,128)}) custom-call(bf16[384,768]{1,0:T(8,128)(2,1)} %fusion.8.q_ref, bf16[1536,768]{1,0:T(8,128)(2,1)} %convolution_convert_fusion.2.k_ref, bf16[1536,768]{1,0:T(8,128)(2,1)} %add_convert_fusion.v_ref), custom_call_target="tpu_custom_call" | custom-call | tf_op jit(solution)/shard_map/attention/pallas_call | solution.py:350
  109.6 0.0 copy-done
  109.6 2.3 fusion.33
  111.9 0.0 copy-done.5
  112.0 0.0 copy-start.10
  112.0 0.0 copy-start.6
  112.0 0.3 multiply_reduce_fusion.2
  112.3 0.0 copy-start.8
  112.3 6.9 %multiply_convert_fusion = (bf16[384,3072]{1,0:T(8,128)(2,1)}, f32[384,3072]{1,0:T(8,128)}) fusion(f32[3072]{0:T(1024)S(1)} %add.126, bf16[768,3072]{1,0:T(8,128)(2,1)} %get-tuple-element.44, f32[384,768]{1,0:T(8,128)S(1)} %get-tuple-element.79, f32[768]{0:T(1024)S(1)} %add.123, f32[768]{0:T(1024)S(1)} %mul.124, f32[384]{0:T(512)S(1)} %add_rsqrt_fusion, ...), kind=kOutput, calls=%fused_computation.8 | convolution fusion | flops 1820491776 | bytes 12997632 | tf_op jit(solution)/shard_map/dot_general | solution.py:31
  119.2 0.0 copy-done.10
  119.2 0.0 copy-start.3
  119.2 0.0 copy-start.16
  119.2 6.2 %fusion.7 = f32[1,384,768]{2,1,0:T(8,128)} fusion(f32[384,768]{1,0:T(8,128)S(1)} %get-tuple-element.79, bf16[384,3072]{1,0:T(8,128)(2,1)} %get-tuple-element.80, bf16[3072,768]{1,0:T(8,128)(2,1)} %get-tuple-element.45, f32[768]{0:T(1024)S(1)} %add.131), kind=kOutput, calls=%fused_computation.19 | convolution fusion | flops 1812529152 | bytes 9440256 | tf_op jit(solution)/shard_map/dot_general | solution.py:31
  125.4 0.0 copy-done.3
  125.4 0.0 copy-done.16
  125.4 5.5 %fusion.34 = (f32[3072]{0:T(1024)}, bf16[384,3072]{1,0:T(8,128)(2,1)S(1)}) fusion(f32[384,3072]{1,0:T(8,128)S(1)} %copy-done.16, bf16[3072,768]{1,0:T(8,128)(2,1)} %get-tuple-element.45, f32[1,384,768]{2,1,0:T(8,128)S(1)} %copy-done.3), kind=kOutput, calls=%fused_computation.68 | convolution fusion | flops 1824912384 | bytes 12988416 | tf_op jit(solution)/shard_map/dot_general | solution.py:27
  130.9 6.2 %multiply_reduce_fusion = (f32[768]{0:T(1024)}, f32[384]{0:T(512)S(1)}, f32[384]{0:T(512)S(1)}, f32[768]{0:T(1024)}, f32[384,768]{1,0:T(8,128)S(1)}) fusion(f32[384,768]{1,0:T(8,128)S(1)} %get-tuple-element.79, f32[384]{0:T(512)S(1)} %add_rsqrt_fusion, f32[384]{0:T(512)S(1)} %broadcast_multiply_fusion.2, f32[768]{0:T(1024)S(1)} %mul.124, ...), kind=kOutput, calls=%fused_computation.29 | convolution fusion | flops 1814591232 | bytes 9452544 | tf_op jit(solution)/shard_map/dot_general | solution.py:27
  137.1 0.0 copy-done.14
  137.1 0.0 copy-done.6
  137.1 0.0 copy-done.8
  137.1 0.4 fusion.32
  137.6 0.0 copy-start.2
  137.6 3.8 convert_reduce_fusion
  141.4 4.3 %copy.34 = bf16[1536,768]{0,1:T(8,128)(2,1)} copy(bf16[1536,768]{1,0:T(8,128)(2,1)} %get-tuple-element.40) | data formatting | bytes 4718592 | tf_op jit(solution)/shard_map/gather/pallas_call | solution.py:295
  145.7 1.3 slice.78
  147.0 1.3 stack.15
  148.3 0.6 stack.16
  148.9 0.0 copy-done.13
  148.9 0.6 stack.17
  149.4 0.0 copy-done.12
  149.5 0.6 stack.18
  150.0 0.1 reduce_sum.98
  150.1 0.6 stack.19
  150.7 0.7 reshape.108
  151.4 0.6 broadcast_in_dim.17
  152.0 0.6 broadcast_in_dim.18
  152.6 2.7 concatenate.3.gv_ref
  155.3 6.7 %fusion.36 = bf16[3072,768]{1,0:T(8,128)(2,1)} fusion(bf16[384,3072]{1,0:T(8,128)(2,1)} %get-tuple-element.80, f32[1,384,768]{2,1,0:T(8,128)S(1)} %copy-done.3), kind=kOutput, calls=%fused_computation.70 | convolution fusion | flops 1811939328 | bytes 8257536 | tf_op jit(solution)/shard_map/dot_general | solution.py:35
  162.0 0.0 copy-done.7
  162.0 0.0 copy-done.9
  162.0 0.0 copy-done.11
  162.0 0.0 copy-done.15
  162.0 0.0 copy-start.1
  162.0 4.7 %convolution_convert_fusion = bf16[768,3072]{1,0:T(8,128)(2,1)} fusion(bf16[384,3072]{1,0:T(8,128)(2,1)S(1)} %copy-done.15, f32[384,768]{1,0:T(8,128)S(1)} %get-tuple-element.79, f32[768]{0:T(1024)S(1)} %copy-done.11, f32[768]{0:T(1024)S(1)} %copy-done.7, f32[384]{0:T(512)S(1)} %copy-done.9, f32[384]{0:T(512)S(1)} %broadcast_multiply_fusion.2), kind=kOutput, calls=%fused_computation.1 | convolution fusion | flops 1815773184 | bytes 8266752 | tf_op jit(solution)/shard_map/dot_general | solution.py:35
  166.7 0.0 copy-done.2
  166.7 0.0 copy-done.1
  166.7 1.8 convolution_convert_fusion.3
  168.5 181.5 %back.1 = (bf16[3,4,384,768]{3,2,1,0:T(8,128)(2,1)}, f32[384,768]{1,0:T(8,128)}, f32[16,768]{1,0:T(8,128)}) custom-call(bf16[384,768]{1,0:T(8,128)(2,1)} %fusion.8.q_ref, bf16[1536,768]{1,0:T(8,128)(2,1)} %convolution_convert_fusion.2.k_ref, bf16[1536,768]{1,0:T(8,128)(2,1)} %add_convert_fusion.v_ref, bf16[384,768]{1,0:T(8,128)(2,1)} %get-tuple-element.84.dc_ref, ...), custom_call_target="tpu_custom_call" | custom-call | tf_op jit(solution)/shard_map/back/pallas_call | solution.py:762
  350.1 15.6 %adam_attention.1 = (f32[1536,768]{1,0:T(8,128)}, f32[1536,768]{1,0:T(8,128)}, f32[1536,768]{1,0:T(8,128)}, f32[1536,768]{1,0:T(8,128)}) custom-call(bf16[3,4,384,768]{3,2,1,0:T(8,128)(2,1)} %get-tuple-element.48.g_ref, f32[1536,768]{1,0:T(8,128)} %bitcast.73, f32[1536,768]{1,0:T(8,128)} %bitcast.77, f32[1536,768]{1,0:T(8,128)} %bitcast.78), custom_call_target="tpu_custom_call" | custom-call | tf_op jit(solution)/shard_map/adam_attention/pallas_call | solution.py:824
  365.6 15.6 %adam_expand.1 = (f32[384,3072]{1,0:T(8,128)}, f32[384,3072]{1,0:T(8,128)}, f32[384,3072]{1,0:T(8,128)}, f32[384,3072]{1,0:T(8,128)}) custom-call(bf16[3,4,384,768]{3,2,1,0:T(8,128)(2,1)} %get-tuple-element.48.g_ref, f32[384,3072]{1,0:T(8,128)} %w_ref.2, f32[384,3072]{1,0:T(8,128)} %m_ref.2, f32[384,3072]{1,0:T(8,128)} %v_ref.2), custom_call_target="tpu_custom_call" | custom-call | tf_op jit(solution)/shard_map/adam_expand/pallas_call | solution.py:824
  381.2 15.6 %adam_contract.1 = (f32[1536,768]{1,0:T(8,128)}, f32[1536,768]{1,0:T(8,128)}, f32[1536,768]{1,0:T(8,128)}, f32[1536,768]{1,0:T(8,128)}) custom-call(bf16[3,4,384,768]{3,2,1,0:T(8,128)(2,1)} %get-tuple-element.48.g_ref, f32[1536,768]{1,0:T(8,128)} %w_ref.3, f32[1536,768]{1,0:T(8,128)} %m_ref.3, f32[1536,768]{1,0:T(8,128)} %v_ref.3), custom_call_target="tpu_custom_call" | custom-call | tf_op jit(solution)/shard_map/adam_contract/pallas_call | solution.py:824
  396.8 1.4 multiply_subtract_fusion
  398.2 2.4 copy.36
  (19 shorter events, 0.1 us)
Async XLA Ops:
  75.5 3.9 copy-start.4
  76.4 35.5 %copy-start.5 = (f32[12,2,384]{2,0,1:T(8,128)}, f32[12,2,384]{2,0,1:T(8,128)S(1)}, u32[]{:S(2)}) copy-start(f32[12,2,384]{2,0,1:T(8,128)S(1)} %slice_convert_fusion) | copy-start | bytes 110596
  88.8 20.8 %copy-start = (f32[1,384,768]{2,1,0:T(8,128)S(1)}, f32[1,384,768]{2,1,0:T(8,128)}, u32[]{:S(2)}) copy-start(f32[1,384,768]{2,1,0:T(8,128)} %param.14) | copy-start | bytes 3538948
  112.0 7.2 %copy-start.10 = (f32[768]{0:T(1024)}, f32[768]{0:T(1024)S(1)}, u32[]{:S(2)}) copy-start(f32[768]{0:T(1024)S(1)} %add.123) | copy-start | bytes 9220
  112.0 25.1 %copy-start.6 = (f32[768]{0:T(1024)}, f32[768]{0:T(1024)S(1)}, u32[]{:S(2)}) copy-start(f32[768]{0:T(1024)S(1)} %mul.124) | copy-start | bytes 9220
  112.3 24.8 %copy-start.8 = (f32[384]{0:T(512)}, f32[384]{0:T(512)S(1)}, u32[]{:S(2)}) copy-start(f32[384]{0:T(512)S(1)} %add_rsqrt_fusion) | copy-start | bytes 4612
  119.2 6.2 %copy-start.3 = (f32[1,384,768]{2,1,0:T(8,128)S(1)}, f32[1,384,768]{2,1,0:T(8,128)}, u32[]{:S(2)}) copy-start(f32[1,384,768]{2,1,0:T(8,128)} %param.15) | copy-start | bytes 3538948
  119.2 6.2 %copy-start.16 = (f32[384,3072]{1,0:T(8,128)S(1)}, f32[384,3072]{1,0:T(8,128)}, u32[]{:S(2)}) copy-start(f32[384,3072]{1,0:T(8,128)} %get-tuple-element.81) | copy-start | bytes 14155780
  130.9 6.2 %copy-start.14 = (bf16[384,3072]{1,0:T(8,128)(2,1)}, bf16[384,3072]{1,0:T(8,128)(2,1)S(1)}, u32[]{:S(2)}) copy-start(bf16[384,3072]{1,0:T(8,128)(2,1)S(1)} %get-tuple-element.86) | copy-start | bytes 7077892
  137.6 29.1 %copy-start.2 = (f32[384,768]{1,0:T(8,128)}, f32[384,768]{1,0:T(8,128)S(1)}, u32[]{:S(2)}) copy-start(f32[384,768]{1,0:T(8,128)S(1)} %get-tuple-element.77.gm_ref) | copy-start | bytes 3538948
  141.4 7.5 %copy-start.13 = (f32[768]{0:T(1024)S(1)}, f32[768]{0:T(1024)}, u32[]{:S(2)}) copy-start(f32[768]{0:T(1024)} %get-tuple-element.62) | copy-start | bytes 9220
  141.4 8.1 %copy-start.12 = (f32[768]{0:T(1024)S(1)}, f32[768]{0:T(1024)}, u32[]{:S(2)}) copy-start(f32[768]{0:T(1024)} %get-tuple-element.65) | copy-start | bytes 9220
  155.3 6.7 %copy-start.7 = (f32[768]{0:T(1024)S(1)}, f32[768]{0:T(1024)}, u32[]{:S(2)}) copy-start(f32[768]{0:T(1024)} %copy-done.6) | copy-start | bytes 9220
  155.3 6.7 %copy-start.9 = (f32[384]{0:T(512)S(1)}, f32[384]{0:T(512)}, u32[]{:S(2)}) copy-start(f32[384]{0:T(512)} %copy-done.8) | copy-start | bytes 4612
  155.3 6.7 %copy-start.11 = (f32[768]{0:T(1024)S(1)}, f32[768]{0:T(1024)}, u32[]{:S(2)}) copy-start(f32[768]{0:T(1024)} %copy-done.10) | copy-start | bytes 9220
  155.3 6.7 %copy-start.15 = (bf16[384,3072]{1,0:T(8,128)(2,1)S(1)}, bf16[384,3072]{1,0:T(8,128)(2,1)}, u32[]{:S(2)}) copy-start(bf16[384,3072]{1,0:T(8,128)(2,1)} %copy-done.14) | copy-start | bytes 7077892
  162.0 4.7 %copy-start.1 = (f32[384,768]{1,0:T(8,128)S(1)}, f32[384,768]{1,0:T(8,128)}, u32[]{:S(2)}) copy-start(f32[384,768]{1,0:T(8,128)} %get-tuple-element.43.ctx_ref) | copy-start | bytes 3538948

commit v3 on v2

--- a/solution.py
+++ b/solution.py
@@ -364,31 +364,42 @@
     sizes, q_ref, k_ref, v_ref, dc_ref, ctx_ref, lse_ref, ht_ref, w_ref, gm_ref, frames_ref,
     vec_ref, gv_ref, gc_ref, ge_ref, go_ref,
     out_ref, ig_ref, ov_ref,
-    ga, own, rc, rx, ry, rz, dkt, dvt, dqt, dhs, dhr, dho, vb, vx, vy, vz,
-    os, cs, cr, xs, xr, ys, yr, zs, zr, azs, azr, ays, ayr, acs, acr, ds, dm, vs, vr,
+    ga, own, rc, rx, ry, rza, rzb, dkt, dvt, dqa, dhs, dhr, vb, vx, vy, vz,
+    os, cs, cr, xs, xr, ys, yr, zas, zar, zbs, zbr, gbs, gbr, gas, gar, ays, ayr, acs, acr,
+    das, dar, vs, vr,
 ):
     at = Place(sizes)
     nf, nh, ns = at.nf, at.nh, at.ns
     rows, width = q_ref.shape
-    half = rc.shape[4]
+    q = rc.shape[5]
     cols = width // nh
+    per = cols // 128
     chunks = rc.shape[0]
-    per = chunks // 3
+    split = chunks // (3 * per)
+    half = q * split
+    group = per * split
+    b0 = lax.rem(at.z, 2)
+    b1 = at.z // 2
     at.barrier()
-    mine = pl.ds(pl.multiple_of(at.core * half, 16), half)
-    other = pl.ds(pl.multiple_of((1 - at.core) * half, 16), half)
+
+    def strip(core, r):
+        return pl.ds(pl.multiple_of(core * half + r * q, 16), q)
 
     def lanes(s, hi):
         return pl.ds(pl.multiple_of(hi * cols + s * 128, 128), 128)
+
+    def place_of(n):
+        return n // group, lax.rem(n, group) // split, lax.rem(n, split)
 
     for s in range(per):
         for hi in range(nh):
             for part in range(2):
-                pltpu.make_async_copy(
-                    go_ref.at[:, pl.ds(part * half, half), pl.ds(hi * cols + s * 128, 128)],
-                    ga.at[s, hi, :, part, 3],
-                    os.at[2],
-                ).start()
+                for r in range(split):
+                    pltpu.make_async_copy(
+                        go_ref.at[:, pl.ds(part * half + r * q, q), pl.ds(hi * cols + s * 128, 128)],
+                        ga.at[s, r, hi, :, part, 1, 1],
+                        os.at[4],
+                    ).start()
 
     def own_whole(slot):
         return pltpu.make_async_copy(own.at[slot], own.at[slot], os.at[slot])
@@ -397,35 +408,41 @@
         return remote(rc.at[n], rc.at[n], cs.at[n], cr.at[n], at.sibling())
 
     def c_send(n):
-        slot = lax.rem(n, 2)
-
-        @pl.when(n < per)
-        def _():
-            for hi in range(nh):
-                block = lanes(n, hi)
-                remote(
-                    gc_ref.at[:, :, other, block], rc.at[n, hi], cs.at[n], cr.at[n], at.sibling()
-                ).start()
-                pltpu.make_async_copy(
-                    gc_ref.at[:, :, mine, block], own.at[slot, hi], os.at[slot]
-                ).start()
-
-        @pl.when(jnp.logical_and(n >= per, n < 2 * per))
+        slot = lax.rem(n, 4)
+        g, s, r = place_of(n)
+
+        @pl.when(n < group)
         def _():
             for hi in range(nh):
                 for u in range(4):
-                    block = pl.ds(pl.multiple_of(u * width + hi * cols + (n - per) * 128, 128), 128)
+                    block = lanes(s, hi)
                     remote(
-                        ge_ref.at[:, other, block], rc.at[n, hi, :, u], cs.at[n], cr.at[n], at.sibling()
+                        gc_ref.at[:, u, strip(1 - at.core, r), block],
+                        rc.at[n, hi, :, u // 2, u % 2], cs.at[n], cr.at[n], at.sibling(),
                     ).start()
                     pltpu.make_async_copy(
-                        ge_ref.at[:, mine, block], own.at[slot, hi, :, u], os.at[slot]
+                        gc_ref.at[:, u, strip(at.core, r), block],
+                        own.at[slot, hi, :, u // 2, u % 2], os.at[slot],
                     ).start()
 
-        @pl.when(jnp.logical_and(n >= 2 * per, n < chunks))
+        @pl.when(jnp.logical_and(n >= group, n < 2 * group))
+        def _():
+            for hi in range(nh):
+                for u in range(4):
+                    block = pl.ds(pl.multiple_of(u * width + hi * cols + s * 128, 128), 128)
+                    remote(
+                        ge_ref.at[:, strip(1 - at.core, r), block],
+                        rc.at[n, hi, :, u // 2, u % 2], cs.at[n], cr.at[n], at.sibling(),
+                    ).start()
+                    pltpu.make_async_copy(
+                        ge_ref.at[:, strip(at.core, r), block],
+                        own.at[slot, hi, :, u // 2, u % 2], os.at[slot],
+                    ).start()
+
+        @pl.when(jnp.logical_and(n >= 2 * group, n < chunks))
         def _():
             remote(
-                ga.at[n - 2 * per, :, :, 1 - at.core], rc.at[n], cs.at[n], cr.at[n], at.sibling()
+                ga.at[s, r, :, :, 1 - at.core], rc.at[n], cs.at[n], cr.at[n], at.sibling()
             ).start()
 
     def x_copy(n, k):
@@ -437,54 +454,66 @@
             rx.at[n, 0, at.y_hi(m)], ry.at[n, m - 1], ys.at[n, m - 1], yr.at[n, m - 1], at.y_peer(m)
         )
 
-    def z_copy(n, k):
-        return remote(
-            ry.at[n, 0, at.z_at(k)], rz.at[n, k - 1], zs.at[n, k - 1], zr.at[n, k - 1], at.z_peer(k)
-        )
-
-    def spot(n):
-        return n // per, lax.rem(n, per)
-
-    def az_copy(n, k, z=None):
-        g, s = spot(n)
-        place = out_ref.at[g, at.z if z is None else z, mine, lanes(s, at.hi)]
-        return remote(place, place, azs.at[n, k - 1], azr.at[n, k - 1], at.z_peer(k))
+    near = {"seq": at.z + 1 - 2 * b0}
+    far = {"seq": at.z + 2 - 4 * b1}
+
+    def za_copy(n):
+        return remote(ry.at[n, 0, :, 1 - b0], rza.at[n], zas.at[n], zar.at[n], near)
+
+    def zb_copy(n):
+        return remote(rza.at[n, 1 - b1], rzb.at[n], zbs.at[n], zbr.at[n], far)
+
+    def gb_copy(n):
+        g, s, r = place_of(n)
+        place = out_ref.at[g, b1, b0, strip(at.core, r), lanes(s, at.hi)]
+        return remote(place, place, gbs.at[n], gbr.at[n], far)
+
+    def ga_copy(n):
+        g, s, r = place_of(n)
+        place = out_ref.at[g, :, b0, strip(at.core, r), lanes(s, at.hi)]
+        return remote(place, place, gas.at[n], gar.at[n], near)
 
     def ay_copy(n, m):
-        g, s = spot(n)
-        place = out_ref.at[g, :, mine, lanes(s, at.hi)]
+        g, s, r = place_of(n)
+        place = out_ref.at[g, :, :, strip(at.core, r), lanes(s, at.hi)]
         return remote(place, place, ays.at[n, m - 1], ayr.at[n, m - 1], at.y_peer(m))
 
     def ac_start(n):
-        g, s = spot(n)
+        g, s, r = place_of(n)
         for hi in range(nh):
-            place = out_ref.at[g, :, mine, lanes(s, hi)]
+            place = out_ref.at[g, :, :, strip(at.core, r), lanes(s, hi)]
             remote(place, place, acs.at[n], acr.at[n], at.sibling()).start()
 
     def ac_whole(n):
         return remote(rx.at[n, 0], rx.at[n, 0], acs.at[n], acr.at[n], at.sibling())
 
+    def split_index(i):
+        return i // (nf * 4), lax.rem(i // 4, nf), lax.rem(i, 4) // 2, lax.rem(i, 2)
+
     def stage_c(n):
         c_whole(n).wait_recv()
-        slot = lax.rem(n, 2)
-
-        @pl.when(n < 2 * per)
+        slot = lax.rem(n, 4)
+        _, s, r = place_of(n)
+
+        @pl.when(n < 2 * group)
         def _():
             own_whole(slot).wait()
 
             def add(i, carry):
-                hi, j, u = i // (nf * 4), lax.rem(i // 4, nf), lax.rem(i, 4)
-                rc[n, hi, j, u] = (rc[n, hi, j, u].astype(F32) + own[slot, hi, j, u].astype(F32)).astype(BF)
+                at_i = split_index(i)
+                rc[(n,) + at_i] = (
+                    rc[(n,) + at_i].astype(F32) + own[(slot,) + at_i].astype(F32)
+                ).astype(BF)
                 return carry
 
             lax.fori_loop(0, nh * nf * 4, add, 0)
 
-        @pl.when(n >= 2 * per)
+        @pl.when(n >= 2 * group)
         def _():
             def add(i, carry):
-                hi, j, u = i // (nf * 4), lax.rem(i // 4, nf), lax.rem(i, 4)
-                rc[n, hi, j, u] = (
-                    rc[n, hi, j, u].astype(F32) + ga[n - 2 * per, hi, j, at.core, u].astype(F32)
+                hi, j, ua, ub = split_index(i)
+                rc[n, hi, j, ua, ub] = (
+                    rc[n, hi, j, ua, ub].astype(F32) + ga[s, r, hi, j, at.core, ua, ub].astype(F32)
                 ).astype(BF)
                 return carry
 
@@ -498,11 +527,11 @@
             x_copy(n, k).wait_recv()
 
         def add(i, carry):
-            hi, u = i // 4, lax.rem(i, 4)
-            total = rc[n, hi, at.x, u].astype(F32)
+            hi, ua, ub = i // 4, lax.rem(i, 4) // 2, lax.rem(i, 2)
+            total = rc[n, hi, at.x, ua, ub].astype(F32)
             for k in range(nf - 1):
-                total += rx[n, k, hi, u].astype(F32)
-            rx[n, 0, hi, u] = total.astype(BF)
+                total += rx[n, k, hi, ua, ub].astype(F32)
+            rx[n, 0, hi, ua, ub] = total.astype(BF)
             return carry
 
         lax.fori_loop(0, nh * 4, add, 0)
@@ -513,31 +542,37 @@
         for m in range(1, nh):
             y_copy(n, m).wait_recv()
 
-        def add(u, carry):
-            total = rx[n, 0, at.hi, u].astype(F32)
+        def add(i, carry):
+            ua, ub = i // 2, lax.rem(i, 2)
+            total = rx[n, 0, at.hi, ua, ub].astype(F32)
             for m in range(nh - 1):
-                total += ry[n, m, u].astype(F32)
-            ry[n, 0, u] = total.astype(BF)
+                total += ry[n, m, ua, ub].astype(F32)
+            ry[n, 0, ua, ub] = total.astype(BF)
             return carry
 
         lax.fori_loop(0, 4, add, 0)
-        for k in range(1, ns):
-            z_copy(n, k).start()
-
-    def stage_z(n):
-        for k in range(1, ns):
-            z_copy(n, k).wait_recv()
-        total = ry[n, 0, at.z].astype(F32)
-        for k in range(ns - 1):
-            total += rz[n, k].astype(F32)
-        g, s = spot(n)
-        out_ref[g, at.z, mine, lanes(s, at.hi)] = total.astype(BF)
-        for k in range(1, ns):
-            az_copy(n, k).start()
-
-    def stage_az(n):
-        for k in range(1, ns):
-            az_copy(n, k, at.z_at(-k)).wait_recv()
+        za_copy(n).start()
+
+    def stage_za(n):
+        za_copy(n).wait_recv()
+        for ua in range(2):
+            rza[n, ua] = (ry[n, 0, ua, b0].astype(F32) + rza[n, ua].astype(F32)).astype(BF)
+        zb_copy(n).start()
+
+    def stage_zb(n):
+        zb_copy(n).wait_recv()
+        g, s, r = place_of(n)
+        out_ref[g, b1, b0, strip(at.core, r), lanes(s, at.hi)] = (
+            rza[n, b1].astype(F32) + rzb[n].astype(F32)
+        ).astype(BF)
+        gb_copy(n).start()
+
+    def stage_gb(n):
+        gb_copy(n).wait_recv()
+        ga_copy(n).start()
+
+    def stage_ga(n):
+        ga_copy(n).wait_recv()
         for m in range(1, nh):
             ay_copy(n, m).start()
 
@@ -547,13 +582,18 @@
         ac_start(n)
 
     lo = lax.broadcasted_iota(jnp.int32, (rows, 128), 1) < 64
-
-    def pair(step):
-        s, hi = step // nh, lax.rem(step, nh)
-        p = hi * per + s
+    pairs = width // 128
+
+    def block_of(i):
+        return lax.rem(at.z + 1 + i, ns)
+
+    def unit(index):
+        i, p = index // pairs, lax.rem(index, pairs)
+        there = block_of(i)
+        keys = pl.ds(pl.multiple_of(there * rows, 128), rows)
         col = pl.ds(pl.multiple_of(p * 128, 128), 128)
-        k2 = k_ref[:, col]
-        v2 = v_ref[:, col]
+        k2 = k_ref[keys, col]
+        v2 = v_ref[keys, col]
         q2 = q_ref[:, col]
         dc2 = dc_ref[:, col]
         both = dc2.astype(F32) * ctx_ref[:, col]
@@ -574,43 +614,56 @@
             dv = a if dv is None else dv + a
             dk = b if dk is None else dk + b
         dq2 = jnp.where(lo, dq[0], dq[1])
-        gv_ref_row = jnp.sum(dq2, axis=0, keepdims=True)
-        vb[2, 0:1, col] = gv_ref_row
-        dq2 = dq2.astype(BF)
-        dqt[col, :] = dq2.T
-        dkb = dk.astype(BF)
-        dvb = dv.astype(BF)
-        dkt[col, :] = dkb
-        dvt[col, :] = dvb
-        shard = 2 * half
-        for j in range(nf):
-            for part in range(2):
-                here = pl.ds(j * shard + part * half, half)
-                ga[s, hi, j, part, 0] = nn(
-                    ht_ref[here, pl.ds(pl.multiple_of(at.z * rows, 128), rows)], dq2
-                ).astype(BF)
-                ga[s, hi, j, part, 1] = nt(ht_ref[here, :], dkb).astype(BF)
-                ga[s, hi, j, part, 2] = nt(ht_ref[here, :], dvb).astype(BF)
-
-    def spread():
-        def block(b):
-            part = pl.ds(pl.multiple_of(b * rows, 128), rows)
-            return nn(w_ref[1], dkt[:, part]) + nn(w_ref[2], dvt[:, part])
-
-        for k in range(1, ns):
-            dhs[k - 1] = block(at.z_at(k)).astype(BF)
-            d_copy(k).start()
-        dho[...] = block(at.z) + nn(w_ref[0], dqt[...])
-
-    def d_copy(k):
-        return remote(dhs.at[k - 1], dhr.at[k - 1], ds.at[k - 1], dm.at[k - 1], at.z_peer(k))
+
+        @pl.when(i == 0)
+        def _():
+            dqa[:, col] = dq2
+
+        @pl.when(i > 0)
+        def _():
+            dqa[:, col] += dq2
+
+        dkt[col, keys] = dk.astype(BF)
+        dvt[col, keys] = dv.astype(BF)
+
+    def weights(s):
+        frames = pl.ds(pl.multiple_of(at.z * rows, 128), rows)
+        for hi in range(nh):
+            col = pl.ds(hi * cols + s * 128, 128)
+            dq2 = dqa[:, col]
+            vb[2, 0:1, col] = jnp.sum(dq2, axis=0, keepdims=True)
+            dq2 = dq2.astype(BF)
+            dk2 = dkt[col, :]
+            dv2 = dvt[col, :]
+            for j in range(nf):
+                for part in range(2):
+                    for r in range(split):
+                        here = pl.ds((2 * j + part) * half + r * q, q)
+                        ga[s, r, hi, j, part, 0, 0] = nn(ht_ref[here, frames], dq2).astype(BF)
+                        ga[s, r, hi, j, part, 0, 1] = nt(ht_ref[here, :], dk2).astype(BF)
+                        ga[s, r, hi, j, part, 1, 0] = nt(ht_ref[here, :], dv2).astype(BF)
+
+    pieces = 8
+
+    def d_copy(i, t):
+        part = pl.ds(t * (width // pieces), width // pieces)
+        return remote(dhs.at[i, part], dhr.at[i, part], das.at[i], dar.at[i], at.z_peer(i + 1))
+
+    def d_whole(i):
+        return remote(dhs.at[i], dhr.at[i], das.at[i], dar.at[i], at.z_peer(i + 1))
+
+    def spread(i):
+        part = pl.ds(pl.multiple_of(block_of(i) * rows, 128), rows)
+        total = nn(w_ref[1], dkt[:, part]) + nn(w_ref[2], dvt[:, part])
+        if i == ns - 1:
+            total += nt(w_ref[0], dqa[...].astype(BF))
+        dhs[i] = total.astype(BF)
 
     def first_norm():
-        for k in range(1, ns):
-            d_copy(k).wait_recv()
-        total = dho[...]
-        for k in range(ns - 1):
-            total += dhr[k].astype(F32)
+        total = dhs[ns - 1].astype(F32)
+        for i in range(ns - 1):
+            d_whole(i).wait_recv()
+            total += dhr[i].astype(F32)
         total = total.T
         normed, inverse = normalize(frames_ref[...])
         scaled = total * vec_ref[0:1, :]
@@ -673,72 +726,101 @@
                 total += vz[j]
             ov_ref[...] = total
 
-    c_send(0)
-    c_send(1)
-    pairs = width // 128
+    ready = group + 2
+    each = -(-ns * pairs // ready)
+    done = [-(-pairs * (i + 1) // each) - 1 for i in range(ns)]
+    norm = done[ns - 1] + 6
+    stages = (stage_x, stage_y, stage_za, stage_zb, stage_gb, stage_ga, stage_ay)
+    last = max(chunks + len(stages), norm + 6)
+    for n in range(4):
+        c_send(n)
 
     def step(n, carry):
-        @pl.when(n < chunks)
-        def _():
-            stage_c(n)
-
-        @pl.when(n < pairs)
-        def _():
-            pair(n)
-
-        @pl.when(n == 2 * per - 2)
-        def _():
-            pltpu.make_async_copy(ga.at[:, :, :, :, 3], ga.at[:, :, :, :, 3], os.at[2]).wait()
-
-        @pl.when(n + 2 < chunks)
-        def _():
-            c_send(n + 2)
-
-        @pl.when(n == pairs)
-        def _():
-            spread()
-
-        for lag, stage in ((1, stage_x), (2, stage_y), (3, stage_z), (4, stage_az), (5, stage_ay)):
+        for k in range(2):
+            @pl.when(2 * n + k < 2 * group)
+            def _(k=k):
+                stage_c(2 * n + k)
+
+                @pl.when(2 * n + k + 4 < 2 * group)
+                def _():
+                    c_send(2 * n + k + 4)
+
+        for s in range(per):
+            @pl.when(n == ready + s + 1)
+            def _(s=s):
+                for r in range(split):
+                    stage_c(2 * group + s * split + r)
+
+        @pl.when(n < ready)
+        def _():
+            def one(k, carry):
+                @pl.when(n * each + k < ns * pairs)
+                def _():
+                    unit(n * each + k)
+
+                return carry
+
+            lax.fori_loop(0, each, one, 0)
+
+        for i in range(ns):
+            @pl.when(n == done[i])
+            def _(i=i):
+                spread(i)
+
+            if i < ns - 1:
+                for late in range(2):
+                    @pl.when(n == done[i] + late)
+                    def _(i=i, late=late):
+                        for t in range(pieces // 2):
+                            d_copy(i, late * (pieces // 2) + t).start()
+
+        @pl.when(n == norm)
+        def _():
+            first_norm()
+
+        for s in range(per):
+            @pl.when(n == ready + s)
+            def _(s=s):
+                weights(s)
+                if s == 0:
+                    whole = ga.at[:, :, :, :, :, 1, 1]
+                    pltpu.make_async_copy(whole, whole, os.at[4]).wait()
+                for r in range(split):
+                    c_send(2 * group + s * split + r)
+
+        for lag, stage in enumerate(stages):
             @pl.when(jnp.logical_and(n >= lag, n < chunks + lag))
             def _(lag=lag, stage=stage):
                 stage(n - lag)
 
-        @pl.when(n == chunks + 2)
-        def _():
-            first_norm()
-            v_step(0)
-
-        @pl.when(n == chunks + 3)
-        def _():
-            v_step(1)
-
-        @pl.when(n == chunks + 4)
-        def _():
-            v_step(2)
+        for i in range(5):
+            @pl.when(n == norm + i)
+            def _(i=i):
+                v_step(i)
 
         return carry
 
-    lax.fori_loop(0, chunks + 5, step, 0)
-    v_step(3)
+    lax.fori_loop(0, last, step, 0)
     for n in range(chunks):
         ac_whole(n).wait()
-    v_step(4)
 
     def drain(n, carry):
         c_whole(n).wait_send()
+        za_copy(n).wait_send()
+        zb_copy(n).wait_send()
+        gb_copy(n).wait_send()
+        ga_copy(n).wait_send()
         for k in range(1, nf):
             x_copy(n, k).wait_send()
         for m in range(1, nh):
             y_copy(n, m).wait_send()
             ay_copy(n, m).wait_send()
-        for k in range(1, ns):
-            z_copy(n, k).wait_send()
-            az_copy(n, k).wait_send()
         return carry
 
     lax.fori_loop(0, chunks, drain, 0)
+    for i in range(ns - 1):
+        d_whole(i).wait_send()
     for k in range(1, ns):
-        d_copy(k).wait_send()
         v_z(k).wait_send()
     for k in range(1, nf):
         v_x(k).wait_send()
@@ -754,46 +836,50 @@
     shard = go.shape[1]
     half = shard // 2
     every = k.shape[0]
+    split = 2 if half % 32 == 0 else 1
+    strip = half // split
     per = width // nh // 128
-    chunks = 3 * per
-    xn, yn, zn = max(nf - 1, 1), max(nh - 1, 1), max(ns - 1, 1)
+    chunks = 3 * per * split
+    xn, yn = max(nf - 1, 1), max(nh - 1, 1)
     dma = pltpu.SemaphoreType.DMA
     anywhere = pl.BlockSpec(memory_space=pl.ANY)
     return pl.pallas_call(
         functools.partial(back_kernel, sizes),
         out_shape=(
-            jax.ShapeDtypeStruct((3, 4, shard, width), BF),
+            jax.ShapeDtypeStruct((3, 2, 2, shard, width), BF),
             jax.ShapeDtypeStruct((rows, width), F32),
             jax.ShapeDtypeStruct((16, width), F32),
         ),
         in_specs=[vmem()] * 12 + [anywhere] * 3,
         out_specs=(vmem(),) * 3,
         scratch_shapes=[
-            pltpu.VMEM((per, nh, nf, 2, 4, half, 128), BF),
-            pltpu.VMEM((2, nh, nf, 4, half, 128), BF),
-            pltpu.VMEM((chunks, nh, nf, 4, half, 128), BF),
-            pltpu.VMEM((chunks, xn, nh, 4, half, 128), BF),
-            pltpu.VMEM((chunks, yn, 4, half, 128), BF),
-            pltpu.VMEM((chunks, zn, half, 128), BF),
+            pltpu.VMEM((per, split, nh, nf, 2, 2, 2, strip, 128), BF),
+            pltpu.VMEM((4, nh, nf, 2, 2, strip, 128), BF),
+            pltpu.VMEM((chunks, nh, nf, 2, 2, strip, 128), BF),
+            pltpu.VMEM((chunks, xn, nh, 2, 2, strip, 128), BF),
+            pltpu.VMEM((chunks, yn, 2, 2, strip, 128), BF),
+            pltpu.VMEM((chunks, 2, strip, 128), BF),
+            pltpu.VMEM((chunks, strip, 128), BF),
             pltpu.VMEM((width, every), BF),
             pltpu.VMEM((width, every), BF),
-            pltpu.VMEM((width, rows), BF),
-            pltpu.VMEM((zn, width, rows), BF),
-            pltpu.VMEM((zn, width, rows), BF),
-            pltpu.VMEM((width, rows), F32),
+            pltpu.VMEM((rows, width), F32),
+            pltpu.VMEM((ns, width, rows), BF),
+            pltpu.VMEM((ns - 1, width, rows), BF),
             pltpu.VMEM((3, 16, width), F32),
             pltpu.VMEM((nf, 16, width), F32),
             pltpu.VMEM((nh, 16, width), F32),
             pltpu.VMEM((ns, 16, width), F32),
-            dma((3,)),
+            dma((5,)),
             dma((chunks,)), dma((chunks,)),
             dma((chunks, xn)), dma((chunks, xn)),
             dma((chunks, yn)), dma((chunks, yn)),
-            dma((chunks, zn)), dma((chunks, zn)),
-            dma((chunks, zn)), dma((chunks, zn)),
+            dma((chunks,)), dma((chunks,)),
+            dma((chunks,)), dma((chunks,)),
+            dma((chunks,)), dma((chunks,)),
+            dma((chunks,)), dma((chunks,)),
             dma((chunks, yn)), dma((chunks, yn)),
             dma((chunks,)), dma((chunks,)),
-            dma((zn,)), dma((zn,)),
+            dma((ns,)), dma((ns,)),
             dma((nf + nh + ns,)), dma((nf + nh + ns,)),
         ],
         name="back",
@@ -803,33 +889,157 @@
     )(q, k, v, dc, ctx, lse, ht, w, gm, frames, vec, gv, gc, ge, go)
 
 
-def adam_kernel(g_ref, w_ref, m_ref, v_ref, go_ref, wo_ref, mo_ref, vo_ref):
-    gradient = g_ref[...].reshape(w_ref.shape).astype(F32)
-    go_ref[...] = gradient
-    wo_ref[...], mo_ref[...], vo_ref[...] = adam_update(
-        w_ref[...], gradient, m_ref[...], v_ref[...], rate_matrix, decay_matrix
-    )
-
-
-def adam(group, out, weight, first, second, name):
-    shard, width = out.shape[2:]
-    rows = min(192, shard)
-    parts = shard // rows
-    if group == 1:
-        grid_map = lambda u, r: (r, u)
-    else:
-        grid_map = lambda u, r: (u * parts + r, 0)
-    spec = pl.BlockSpec((rows, width), grid_map)
-    shape = jax.ShapeDtypeStruct(weight.shape, F32)
+def feed_kernel(
+    ctx_ref, frames_ref, cot_ref, vec_ref, wo_ref, win_ref, wout_ref,
+    fo_ref, gm_ref, dc_ref, gi_ref, gout_ref, go_ref, gv_ref,
+    mid, h2, h2t, dyb, acc, dh2,
+):
+    b = pl.program_id(0)
+
+    @pl.when(b == 0)
+    def _():
+        middle = frames_ref[...] + nn(ctx_ref[...].astype(BF), wo_ref[...]) + vec_ref[4:5, :]
+        mid[...] = middle
+        normed, _ = normalize(middle)
+        hidden = (normed * vec_ref[5:6, :] + vec_ref[6:7, :]).astype(BF)
+        h2[...] = hidden
+        h2t[...] = hidden.T
+        dyb[...] = cot_ref[...].astype(BF)
+        acc[...] = middle + vec_ref[7:8, :]
+        dh2[...] = jnp.zeros_like(dh2)
+        gv_ref[...] = jnp.zeros_like(gv_ref)
+
+    up = dyb[...]
+    u = nn(h2[...], win_ref[...]) + vec_ref[pl.ds(8 + b, 1), :]
+    phi = 0.5 * (1.0 + lax.erf(u * 0.7071067811865476))
+    activated = (u * phi).astype(BF)
+    acc[...] += nn(activated, wout_ref[...])
+    gout_ref[...] = tn(activated, up).astype(BF)
+    du = nt(up, wout_ref[...]) * (phi + u * jnp.exp(-0.5 * u * u) * 0.3989422804014327)
+    gv_ref[pl.ds(8 + b, 1), :] = jnp.sum(du, axis=0, keepdims=True)
+    dub = du.astype(BF)
+    gi_ref[...] = nn(h2t[...], dub).astype(BF)
+    dh2[...] += nt(dub, win_ref[...])
+
+    @pl.when(b == pl.num_programs(0) - 1)
+    def _():
+        fo_ref[...] = acc[...]
+        normed, inverse = normalize(mid[...])
+        back, gain, offset = norm_back(dh2[...], normed, inverse, vec_ref[5:6, :])
+        upstream = cot_ref[...]
+        middle = upstream + back
+        gm_ref[...] = middle
+        dab = middle.astype(BF)
+        go_ref[...] = tn(ctx_ref[...].astype(BF), dab).astype(BF)
+        dctx = nt(dab, wo_ref[...]).astype(BF)
+        dc_ref[...] = dctx
+        gv_ref[3:4, :] = jnp.sum(dctx.astype(F32), axis=0, keepdims=True)
+        gv_ref[4:5, :] = jnp.sum(middle, axis=0, keepdims=True)
+        gv_ref[5:6, :] = gain[None]
+        gv_ref[6:7, :] = offset[None]
+        gv_ref[7:8, :] = jnp.sum(upstream, axis=0, keepdims=True)
+
+
+def feed_all(ctx, frames, cot, vec, aw, ew, cw):
+    rows, width = frames.shape
+    full = ew.shape[1]
+    whole = lambda shape: pl.BlockSpec(shape, lambda b: (0,) * len(shape))
+    blocks = full // width
     return pl.pallas_call(
-        adam_kernel,
-        grid=(4, parts),
-        out_shape=(shape,) * 4,
-        in_specs=[pl.BlockSpec((None, None, rows, width), lambda u, r: (group, u, r, 0))] + [spec] * 3,
-        out_specs=(spec,) * 4,
-        name=name,
+        feed_kernel,
+        grid=(blocks,),
+        out_shape=(
+            jax.ShapeDtypeStruct((rows, width), F32),
+            jax.ShapeDtypeStruct((rows, width), F32),
+            jax.ShapeDtypeStruct((rows, width), BF),
+            jax.ShapeDtypeStruct((width, full), BF),
+            jax.ShapeDtypeStruct((full, width), BF),
+            jax.ShapeDtypeStruct((width, width), BF),
+            jax.ShapeDtypeStruct((16, width), F32),
+        ),
+        in_specs=[
+            whole((rows, width)), whole((rows, width)), whole((rows, width)), whole((16, width)),
+            pl.BlockSpec((None, width, width), lambda b: (3, 0, 0)),
+            pl.BlockSpec((width, width), lambda b: (0, b)),
+            pl.BlockSpec((width, width), lambda b: (b, 0)),
+        ],
+        out_specs=(
+            whole((rows, width)), whole((rows, width)), whole((rows, width)),
+            pl.BlockSpec((width, width), lambda b: (0, b)),
+            pl.BlockSpec((width, width), lambda b: (b, 0)),
+            whole((width, width)), whole((16, width)),
+        ),
+        scratch_shapes=[
+            pltpu.VMEM((rows, width), F32),
+            pltpu.VMEM((rows, width), BF),
+            pltpu.VMEM((width, rows), BF),
+            pltpu.VMEM((rows, width), BF),
+            pltpu.VMEM((rows, width), F32),
+            pltpu.VMEM((rows, width), F32),
+        ],
+        name="feed",
         compiler_params=pltpu.CompilerParams(vmem_limit_bytes=67043328),
-    )(out, weight, first, second)
+    )(ctx, frames, cot, vec, aw, ew, cw)
+
+
+def adam_kernel(parts, g_ref, *refs):
+    step = pl.program_id(0)
+    for i, group in enumerate((2, 1, 0)):
+        w_ref, m_ref, v_ref = refs[3 * i : 3 * i + 3]
+        go_ref, wo_ref, mo_ref, vo_ref = refs[9 + 4 * i : 13 + 4 * i]
+
+        @pl.when(step // parts == i)
+        def _():
+            gradient = g_ref[...].astype(F32)
+            go_ref[...] = gradient
+            wo_ref[...], mo_ref[...], vo_ref[...] = adam_update(
+                w_ref[...], gradient, m_ref[...], v_ref[...], rate_matrix, decay_matrix
+            )
+
+
+def adam_all(out, arrays):
+    shard, width = out.shape[3:]
+    rows = 96 if shard % 96 == 0 else shard
+    deep = shard // rows
+    parts = 4 * deep
+
+    def local(step, i):
+        t = jnp.clip(step - i * parts, 0, parts - 1)
+        return t // deep, lax.rem(t, deep)
+
+    def g_map(step):
+        i = step // parts
+        t = step - i * parts
+        u = t // deep
+        return 2 - i, u // 2, lax.rem(u, 2), lax.rem(t, deep), 0
+
+    def map_of(i):
+        def rows_map(step):
+            u, r = local(step, i)
+            return u * deep + r, 0
+
+        def cols_map(step):
+            u, r = local(step, i)
+            return r, u
+
+        return cols_map if i == 1 else rows_map
+
+    in_specs = [pl.BlockSpec((None, None, None, rows, width), g_map)]
+    out_specs, shapes = [], []
+    for i in range(3):
+        spec = pl.BlockSpec((rows, width), map_of(i))
+        in_specs += [spec] * 3
+        out_specs += [spec] * 4
+        shapes += [jax.ShapeDtypeStruct(arrays[i][0].shape, F32)] * 4
+    return pl.pallas_call(
+        functools.partial(adam_kernel, parts),
+        grid=(3 * parts,),
+        out_shape=tuple(shapes),
+        in_specs=in_specs,
+        out_specs=tuple(out_specs),
+        name="adam",
+        compiler_params=pltpu.CompilerParams(vmem_limit_bytes=67043328),
+    )(out, *[each for group in arrays for each in group])
 
 
 def on_device(
@@ -859,45 +1069,14 @@
     aw, ew, cw, vw, h_all = gather_all(
         sizes, frames, attention_weight, expand_weight, contract_weight, vec_pad
     )
-    vec = jnp.transpose(vw, (1, 0, 2)).reshape(16, width)[:12].astype(F32)
-    bias_expand = vec[8:].reshape(-1)
+    vec = jnp.transpose(vw, (1, 0, 2)).reshape(16, width).astype(F32)
     h_own = lax.dynamic_slice_in_dim(h_all, lax.axis_index("seq") * rows, rows, 0)
     queries = (nn(h_own, aw[0]) + vec[2]).astype(BF)
     key_rows = nn(h_all, aw[1]).astype(BF)
     value_rows = (nn(h_all, aw[2]) + vec[3]).astype(BF)
     context_wide, log_total = attention(queries, key_rows, value_rows)
-    context = context_wide.astype(BF)
-    middle = frames + nn(context, aw[3]) + vec[4]
-    normed_two, inverse_two = normalize(middle)
-    hidden_two = (normed_two * vec[5] + vec[6]).astype(BF)
-    expanded = nn(hidden_two, ew) + bias_expand
-    activated = gelu_exact(expanded).astype(BF)
-    frames_out = middle + nn(activated, cw) + vec[7]
-    upstream_bf = upstream.astype(BF)
-    grad_contract = tn(activated, upstream_bf).astype(BF)
-    grad_expanded = nt(upstream_bf, cw) * gelu_slope(expanded)
-    grad_expanded_bf = grad_expanded.astype(BF)
-    grad_expand = tn(hidden_two, grad_expanded_bf).astype(BF)
-    grad_hidden_two = nt(grad_expanded_bf, ew)
-    back_two, gain_two_grad, bias_two_grad = norm_back(
-        grad_hidden_two, normed_two, inverse_two, vec[5]
-    )
-    grad_middle = upstream + back_two
-    grad_middle_bf = grad_middle.astype(BF)
-    grad_output_w = tn(context, grad_middle_bf).astype(BF)
-    grad_context = nt(grad_middle_bf, aw[3]).astype(BF)
-    small = jnp.stack(
-        [
-            jnp.sum(grad_context.astype(F32), axis=0),
-            jnp.sum(grad_middle, axis=0),
-            gain_two_grad,
-            bias_two_grad,
-            jnp.sum(upstream, axis=0),
-        ]
-    )
-    gv = jnp.concatenate(
-        [jnp.zeros((3, width), F32), small, jnp.sum(grad_expanded, axis=0).reshape(-1, width),
-         jnp.zeros((4, width), F32)], axis=0
+    frames_out, grad_middle, grad_context, grad_expand, grad_contract, grad_output_w, gv = feed_all(
+        context_wide, frames, upstream, vec, aw, ew, cw
     )
     out, input_gradient, gv_sum = back_all(
         sizes,
@@ -911,7 +1090,7 @@
         aw,
         grad_middle,
         frames,
-        vec[:8],
+        vec,
         gv,
         grad_contract.reshape(nf, 4, shard, width),
         grad_expand.reshape(nf, shard, full),
@@ -921,13 +1100,16 @@
         gv_sum[:12], lax.axis_index("fsdp") * (width // nf), width // nf, 1
     )
     flat = (4 * shard, width)
-    contract_out = adam(0, out, contract_weight, first_contract, second_contract, "adam_contract")
-    expand_out = adam(1, out, expand_weight, first_expand, second_expand, "adam_expand")
-    attention_out = adam(
-        2, out, attention_weight.reshape(flat), first_attention.reshape(flat),
-        second_attention.reshape(flat), "adam_attention"
+    done = adam_all(
+        out,
+        (
+            [x.reshape(flat) for x in (attention_weight, first_attention, second_attention)],
+            [expand_weight, first_expand, second_expand],
+            [contract_weight, first_contract, second_contract],
+        ),
     )
-    attention_out = [each.reshape(attention_weight.shape) for each in attention_out]
+    attention_out = [each.reshape(attention_weight.shape) for each in done[:4]]
+    expand_out, contract_out = done[4:8], done[8:]
     vector_out = (owned_vec,) + adam_update(
         vectors, owned_vec, first_vectors, second_vectors, rate_vector, 0.0
     )

time: 402 us -> 364 us (0.905)
  matrix products: 56.3 us -> 13.1 us
  Pallas kernels: 322 us -> 337 us
  local copies, waits for them, and re-layouts: 17.8 us -> 8.66 us
    pallas_call x3 -> x2, Pallas kernels: 46.7 us -> 76.2 us  [the longest x1 52.7 us: adam_all(): pl.pallas_call(functools.partial(adam_kernel, parts), grid=(3 * parts,),...]
    dot_general x6 -> x0, matrix products: 28.6 us -> none  [the longest x3 15.5 us: nt(): lax.dot_general(left, right, (((1,), (1,)), ((), ())), preferred_element_...]
    pallas_call x1, Pallas kernels: 182 us -> 167 us  [back_all(): pl.pallas_call(functools.partial(back_kernel, sizes), out_shape=(jax.Shap...]
    dot_general x6 -> x3, matrix products: 27.7 us -> 13.1 us  [nn(): lax.dot_general(left, right, (((1,), (0,)), ((), ())), preferred_element_...]
where the time goes in v3:
time: 364 us; the launch traced here: 362 us
  Pallas kernels  337 us (93%)
  matrix products  13.1 us (4%)
  local copies, waits for them, and re-layouts  8.66 us (2%)
    pallas_call x1, Pallas kernels, back_all(): pl.pallas_call(functools.partial(back_kernel, sizes), out_shape=(jax.Shap...  167 us
    pallas_call x1, Pallas kernels, gather_all(): pl.pallas_call(functools.partial(gather_kernel, sizes), out_shape=(jax.Sh...  73.4 us
    pallas_call x1, Pallas kernels, adam_all(): pl.pallas_call(functools.partial(adam_kernel, parts), grid=(3 * parts,),...  52.7 us
    pallas_call x1, Pallas kernels, feed_all(): pl.pallas_call(feed_kernel, grid=(blocks,), out_shape=(jax.ShapeDtypeStru...  23.5 us
    pallas_call x1, Pallas kernels, attention(): pl.pallas_call(functools.partial(attention_kernel, rows), out_shape=(jax....  20.7 us
    dot_general x3, matrix products, nn(): lax.dot_general(left, right, (((1,), (0,)), ((), ())), preferred_element_...  13.1 us

profile of v3, /device:TPU:0, one launch (start us, length us, event | category | flops | bytes accessed | tf_op | source)
XLA Modules:
  0.0 361.8 jit_solution(95720758477668586)
XLA Ops:
  0.7 1.4 pad.4.vec_ref
  2.0 73.4 %gather.1 = (bf16[4,768,768]{2,1,0:T(8,128)(2,1)}, bf16[768,3072]{1,0:T(8,128)(2,1)}, bf16[3072,768]{1,0:T(8,128)(2,1)}, bf16[2,16,384]{2,1,0:T(8,128)(2,1)}, bf16[1536,768]{1,0:T(8,128)(2,1)}) custom-call(f32[384,768]{1,0:T(8,128)} %bitcast.33, f32[4,384,768]{2,1,0:T(8,128)} %aw_ref.1, f32[384,3072]{1,0:T(8,128)} %refs_3_.1, f32[1536,768]{1,0:T(8,128)} %refs_6_.1, ...), custom_call_target="tpu_custom_call" | custom-call | tf_op jit(solution)/shard_map/gather/pallas_call | solution.py:295
  75.5 0.7 convert_bitcast_fusion
  76.3 2.9 fusion.q_ref
  79.2 0.0 copy-start
  79.2 5.5 %convolution_convert_fusion.k_ref = bf16[1536,768]{1,0:T(8,128)(2,1)} fusion(bf16[1536,768]{1,0:T(8,128)(2,1)} %get-tuple-element.47, bf16[4,768,768]{2,1,0:T(8,128)(2,1)} %get-tuple-element.48.wo_ref.w_ref), kind=kOutput, calls=%fused_computation.1 | convolution fusion | flops 1813118976 | bytes 5898240 | tf_op jit(solution)/shard_map/dot_general | solution.py:31
  84.7 0.0 copy-done
  84.7 4.7 %add_convert_fusion.v_ref = bf16[1536,768]{1,0:T(8,128)(2,1)} fusion(bf16[1536,768]{1,0:T(8,128)(2,1)S(1)} %copy-done, f32[768]{0:T(1024)S(1)} %add.47, bf16[4,768,768]{2,1,0:T(8,128)(2,1)} %get-tuple-element.48.wo_ref.w_ref), kind=kOutput, calls=%fused_computation | convolution fusion | flops 1814298624 | bytes 5901312 | tf_op jit(solution)/shard_map/dot_general | solution.py:31
  89.4 20.7 %attention.1 = (f32[384,768]{1,0:T(8,128)}, f32[6,384,128]{2,1,0:T(8,128)}) custom-call(bf16[384,768]{1,0:T(8,128)(2,1)} %fusion.q_ref, bf16[1536,768]{1,0:T(8,128)(2,1)} %convolution_convert_fusion.k_ref, bf16[1536,768]{1,0:T(8,128)(2,1)} %add_convert_fusion.v_ref), custom_call_target="tpu_custom_call" | custom-call | tf_op jit(solution)/shard_map/attention/pallas_call | solution.py:350
  110.1 0.6 copy.34
  110.7 23.5 %feed.1 = (f32[384,768]{1,0:T(8,128)}, f32[384,768]{1,0:T(8,128)}, bf16[384,768]{1,0:T(8,128)(2,1)}, bf16[768,3072]{1,0:T(8,128)(2,1)}, bf16[3072,768]{1,0:T(8,1...) custom-call(f32[384,768]{1,0:T(8,128)} %get-tuple-element.50.ctx_ref, f32[384,768]{1,0:T(8,128)} %bitcast.34, ...), custom_call_target="tpu_custom_call" | custom-call | tf_op jit(solution)/shard_map/feed/pallas_call | solution.py:948
  134.2 4.3 %copy.33 = bf16[1536,768]{0,1:T(8,128)(2,1)} copy(bf16[1536,768]{1,0:T(8,128)(2,1)} %get-tuple-element.47) | data formatting | bytes 4718592 | tf_op jit(solution)/shard_map/gather/pallas_call | solution.py:295
  138.5 166.8 %back.1 = (bf16[3,2,2,384,768]{4,3,2,1,0:T(8,128)(2,1)}, f32[384,768]{1,0:T(8,128)}, f32[16,768]{1,0:T(8,128)}) custom-call(bf16[384,768]{1,0:T(8,128)(2,1)} %fusion.q_ref, bf16[1536,768]{1,0:T(8,128)(2,1)} %convolution_convert_fusion.k_ref, bf16[1536,768]{1,0:T(8,128)(2,1)} %add_convert_fusion.v_ref, bf16[384,768]{1,0:T(8,128)(2,1)} %get-tuple-element.54.dc_ref, ...), custom_call_target="tpu_custom_call" | custom-call | tf_op jit(solution)/shard_map/back/pallas_call | solution.py:846
  305.3 52.7 %adam.1 = (f32[1536,768]{1,0:T(8,128)}, f32[1536,768]{1,0:T(8,128)}, f32[1536,768]{1,0:T(8,128)}, f32[1536,768]{1,0:T(8,128)}, f32[384,3072]{1,0:T(8,128)}, /*in...) custom-call(bf16[3,2,2,384,768]{4,3,2,1,0:T(8,128)(2,1)} %get-tuple-, ...), custom_call_target="tpu_custom_call" | custom-call | tf_op jit(solution)/shard_map/adam/pallas_call | solution.py:1034
  358.0 1.4 multiply_subtract_fusion
  359.4 2.4 copy.36
  (3 shorter events, 0.1 us)
Async XLA Ops:
  79.2 5.6 %copy-start = (bf16[1536,768]{1,0:T(8,128)(2,1)S(1)}, bf16[1536,768]{1,0:T(8,128)(2,1)}, u32[]{:S(2)}) copy-start(bf16[1536,768]{1,0:T(8,128)(2,1)} %get-tuple-element.47) | copy-start | bytes 7077892

commit v4 on v3

--- a/solution.py
+++ b/solution.py
@@ -55,17 +55,6 @@
     return (inverse * inner, jnp.sum(upstream * normed, axis=0), jnp.sum(upstream, axis=0))
 
 
-def gelu_exact(values):
-    return 0.5 * values * (1.0 + lax.erf(values * 0.7071067811865476))
-
-
-def gelu_slope(values):
-    return (
-        0.5 * (1.0 + lax.erf(values * 0.7071067811865476))
-        + values * jnp.exp(-0.5 * values * values) * 0.3989422804014327
-    )
-
-
 def adam_update(weight, gradient, first, second, rate, decay):
     first_new = beta_one * first + (1.0 - beta_one) * gradient
     second_new = beta_two * second + (1.0 - beta_two) * gradient * gradient
@@ -124,25 +113,40 @@
     )
 
 
-def gather_kernel(
-    sizes, frames_ref, aw_ref, ew_ref, cw_ref, vec_ref,
-    a_ref, e_ref, c_ref, v_ref, h_ref,
-    xs, xr, ys, yr, s1s, s1r, s2s, s2r, vs, vr, rs, ls, hr,
+def front_kernel(
+    sizes, frames_ref, vec_ref, aw_ref, ew_ref, cw_ref,
+    a_out, e_ref, c_ref, vec_out, ht_out, q_out, k_out, v_out, ctx_out, lse_ref,
+    a_ref, v_buf, h_ref, ht, q_buf, k_buf, v_buf2, ctx_buf, af, ef, cf, eb, cb,
+    ls, xs, xr, ys, yr, s1s, s1r, s2s, s2r, vs, vr, rs, hs, hr,
 ):
     at = Place(sizes)
     nf, nh, ns = at.nf, at.nh, at.ns
     rows, width = frames_ref.shape
     shard = aw_ref.shape[1]
     half = shard // 2
+    deep = cw_ref.shape[0]
+
+    def load(i, src, dst):
+        return pltpu.make_async_copy(src, dst, ls.at[i])
+
+    loads = [
+        load(0, aw_ref.at[pl.ds(0, 3)], af.at[pl.ds(0, 3)]),
+        load(1, aw_ref.at[pl.ds(3, 1)], af.at[pl.ds(3, 1)]),
+        load(2, ew_ref, ef),
+        load(3, cw_ref, cf),
+    ]
+    for copy in loads:
+        copy.start()
     at.barrier()
-    v_ref[at.x] = vec_ref[...].astype(BF)
+    v_buf[at.x] = jnp.zeros(v_buf.shape[1:], BF)
+    v_buf[at.x, 0 : vec_ref.shape[0], :] = vec_ref[...].astype(BF)
     vec_copies = []
     for k in range(1, nf):
-        copy = remote(v_ref.at[at.x], v_ref.at[at.x], vs.at[k], vr.at[k], at.x_peer(k))
+        copy = remote(v_buf.at[at.x], v_buf.at[at.x], vs.at[k], vr.at[k], at.x_peer(k))
         copy.start()
         vec_copies.append(copy)
 
-    def view(chunk, j, hi, core):
+    def view(chunk, j, hi, core, own=False):
         if chunk < 2:
             first, count = ((0, 3), (3, 1))[chunk]
             cols = width // nh
@@ -151,16 +155,15 @@
                 pl.ds(pl.multiple_of(j * shard + core * half, 16), half),
                 pl.ds(pl.multiple_of(hi * cols, 128), cols),
             ]
-        if chunk == 2:
-            cols = e_ref.shape[1] // nh
-            return e_ref.at[
-                pl.ds(pl.multiple_of(j * shard + core * half, 16), half),
-                pl.ds(pl.multiple_of(hi * cols, 128), cols),
-            ]
-        cols = width // nh
-        deep = c_ref.shape[0] // nf
-        return c_ref.at[
-            pl.ds(pl.multiple_of(j * deep + core * (deep // 2), 16), deep // 2),
+        ref, stage, size = ((e_ref, eb, shard), (c_ref, cb, deep))[chunk - 2]
+        cols = ref.shape[1] // nh
+        start = core * (size // 2)
+        if own:
+            ref = stage
+        else:
+            start = j * size + start
+        return ref.at[
+            pl.ds(pl.multiple_of(start, 16), size // 2),
             pl.ds(pl.multiple_of(hi * cols, 128), cols),
         ]
 
@@ -169,29 +172,34 @@
 
     def send_chunk(chunk):
         for k in range(1, nf):
-            piece = view(chunk, at.x, at.hi, at.core)
-            copy = remote(piece, piece, xs.at[chunk, k], xr.at[chunk, k], at.x_peer(k))
+            copy = remote(
+                view(chunk, at.x, at.hi, at.core, True), view(chunk, at.x, at.hi, at.core),
+                xs.at[chunk, k], xr.at[chunk, k], at.x_peer(k),
+            )
             copy.start()
             x_copies[chunk, k] = copy
 
+    loads[0].wait()
     for u in range(3):
-        a_ref[u, pl.ds(own, shard), :] = aw_ref[u].astype(BF)
+        a_ref[u, pl.ds(own, shard), :] = af[u].astype(BF)
     send_chunk(0)
     normed, _ = normalize(frames_ref[...])
     for copy in vec_copies:
         copy.wait()
-    gain = jnp.concatenate([v_ref[j, 0:1, :] for j in range(nf)], axis=1).astype(F32)
-    offset = jnp.concatenate([v_ref[j, 1:2, :] for j in range(nf)], axis=1).astype(F32)
-    h_ref[pl.ds(pl.multiple_of(at.z * rows, 16), rows), :] = (normed * gain + offset).astype(BF)
+    vec = jnp.concatenate([v_buf[j] for j in range(nf)], axis=1).astype(F32)
+    vec_out[...] = vec
+    mine = pl.ds(pl.multiple_of(at.z * rows, 128), rows)
+    hidden = (normed * vec[0:1] + vec[1:2]).astype(BF)
+    h_ref[mine, :] = hidden
 
     def block(b):
-        return h_ref.at[pl.ds(pl.multiple_of(b * rows, 16), rows), :]
+        return h_ref.at[pl.ds(pl.multiple_of(b * rows, 128), rows), :]
 
     def to_right(b):
         return remote(block(b), block(b), rs.at[b], hr.at[b], {"seq": at.z + 1})
 
     def to_left(b):
-        return remote(block(b), block(b), ls.at[b], hr.at[b], {"seq": at.z - 1})
+        return remote(block(b), block(b), hs.at[b], hr.at[b], {"seq": at.z - 1})
 
     @pl.when(at.z < ns - 1)
     def _():
@@ -201,42 +209,69 @@
     def _():
         to_left(at.z).start()
 
-    a_ref[3, pl.ds(own, shard), :] = aw_ref[3].astype(BF)
+    loads[1].wait()
+    a_ref[3, pl.ds(own, shard), :] = af[3].astype(BF)
     send_chunk(1)
-    e_ref[pl.ds(own, shard), :] = ew_ref[...].astype(BF)
+    loads[2].wait()
+    eb[...] = ef[...].astype(BF)
     send_chunk(2)
-    deep = cw_ref.shape[0]
-    c_ref[pl.ds(pl.multiple_of(at.x * deep, 16), deep), :] = cw_ref[...].astype(BF)
+    loads[3].wait()
+    cb[...] = cf[...].astype(BF)
     send_chunk(3)
-
-    pending = []
+    stores = [
+        load(4, eb, e_ref.at[pl.ds(own, shard), :]),
+        load(5, cb, c_ref.at[pl.ds(pl.multiple_of(at.x * deep, 16), deep), :]),
+    ]
+    for copy in stores:
+        copy.start()
+    ht[:, mine] = hidden.T
+
+    def first_copy(chunk, k):
+        j = lax.rem(at.x - k + nf, nf)
+        piece = view(chunk, j, at.hi, at.core)
+        return remote(piece, piece, s1s.at[chunk, k], s1r.at[chunk, k], at.sibling())
+
+    def y_copy(chunk, k, m):
+        j = lax.rem(at.x - k + nf, nf)
+        piece = view(chunk, j, at.hi, at.core)
+        return remote(piece, piece, ys.at[chunk, k, m], yr.at[chunk, k, m], at.y_peer(m))
+
+    def second_copy(chunk, k, m):
+        j = lax.rem(at.x - k + nf, nf)
+        piece = view(chunk, j, lax.rem(at.hi - m + nh, nh), at.core)
+        return remote(piece, piece, s2s.at[chunk, k, m], s2r.at[chunk, k, m], at.sibling())
 
     def forward(chunk):
         for k in range(1, nf):
             x_copies[chunk, k].wait_recv()
-            j = lax.rem(at.x - k + nf, nf)
-            piece = view(chunk, j, at.hi, at.core)
-            copy = remote(piece, piece, s1s.at[chunk, k], s1r.at[chunk, k], at.sibling())
-            copy.start()
-            pending.append(copy)
+            first_copy(chunk, k).start()
             for m in range(1, nh):
-                copy = remote(piece, piece, ys.at[chunk, k, m], yr.at[chunk, k, m], at.y_peer(m))
-                copy.start()
-                pending.append((copy, chunk, k, m))
+                y_copy(chunk, k, m).start()
 
     def relay(chunk):
         for k in range(1, nf):
             for m in range(1, nh):
-                j = lax.rem(at.x - k + nf, nf)
-                hi = lax.rem(at.hi - m + nh, nh)
-                piece = view(chunk, j, hi, at.core)
-                remote(piece, piece, ys.at[chunk, k, m], yr.at[chunk, k, m], at.y_peer(m)).wait_recv()
-                copy = remote(piece, piece, s2s.at[chunk, k, m], s2r.at[chunk, k, m], at.sibling())
-                copy.start()
-                pending.append(copy)
+                y_copy(chunk, k, m).wait_recv()
+                second_copy(chunk, k, m).start()
+
+    def arrived(chunk):
+        for k in range(1, nf):
+            first_copy(chunk, k).wait_recv()
+            for m in range(1, nh):
+                second_copy(chunk, k, m).wait_recv()
+
+    def rows_of(b):
+        part = pl.ds(pl.multiple_of(b * rows, 128), rows)
+        k_buf[part, :] = nn(h_ref[part, :], a_ref[1]).astype(BF)
+        v_buf2[part, :] = (nn(h_ref[part, :], a_ref[2]) + vec[3:4]).astype(BF)
+
+    def turn(b):
+        part = pl.ds(pl.multiple_of(b * rows, 128), rows)
+        ht[:, part] = h_ref[part, :].T
 
     def hop(s):
         b = at.z - s
+        d = at.z + s
 
         @pl.when(b >= 0)
         def _():
@@ -246,8 +281,6 @@
             def _():
                 to_right(b).start()
 
-        d = at.z + s
-
         @pl.when(d < ns)
         def _():
             to_left(d).wait_recv()
@@ -255,27 +288,82 @@
             @pl.when(at.z > 0)
             def _():
                 to_left(d).start()
+
+    def use(s):
+        b = at.z - s
+        d = at.z + s
+
+        @pl.when(b >= 0)
+        def _():
+            rows_of(b)
+            turn(b)
+
+        @pl.when(d < ns)
+        def _():
+            rows_of(d)
+            turn(d)
 
     forward(0)
     hop(1)
     forward(1)
     relay(0)
+    arrived(0)
+    q_buf[...] = (nn(h_ref[mine, :], a_ref[0]) + vec[2:3]).astype(BF)
+    stores.append(load(6, q_buf, q_out))
+    stores[-1].start()
+    rows_of(at.z)
+    use(1)
     relay(1)
-    for s in range(2, ns - 1):
+    forward(2)
+    for s in range(2, ns):
         hop(s)
-    forward(2)
+        use(s)
+    arrived(1)
+    for i, (src, dst) in enumerate(((a_ref, a_out), (ht, ht_out), (k_buf, k_out), (v_buf2, v_out))):
+        stores.append(load(7 + i, src, dst))
+        stores[-1].start()
+    forward(3)
     relay(2)
-    if ns > 2:
-        hop(ns - 1)
-    forward(3)
-    relay(3)
-    for entry in pending:
-        if isinstance(entry, tuple):
-            entry[0].wait_send()
-        else:
-            entry.wait()
+    lo = lax.broadcasted_iota(jnp.int32, (rows, 128), 1) < 64
+
+    def pair(p, carry):
+        col = pl.ds(pl.multiple_of(p * 128, 128), 128)
+        k2 = k_buf[:, col]
+        v2 = v_buf2[:, col]
+        q2 = q_buf[:, col]
+        ctx, lse = [], []
+        for h in range(2):
+            mask = lo if h == 0 else jnp.logical_not(lo)
+            s = nt(jnp.where(mask, q2, jnp.zeros_like(q2)), k2) * score_scale
+            largest = jnp.max(s, axis=-1, keepdims=True)
+            e = jnp.exp(s - largest)
+            total = jnp.sum(e, axis=-1, keepdims=True)
+            ctx.append(nn((e * (1.0 / total)).astype(BF), v2))
+            lse.append(largest + jnp.log(total))
+        ctx_buf[:, col] = jnp.where(lo, ctx[0], ctx[1])
+        lse_ref[p] = jnp.where(lo, lse[0], lse[1])
+
+        @pl.when(p == 1)
+        def _():
+            relay(3)
+
+        return carry
+
+    lax.fori_loop(0, width // 128, pair, 0)
+    stores.append(load(11, ctx_buf, ctx_out))
+    stores[-1].start()
+    arrived(2)
+    arrived(3)
+    for copy in stores:
+        copy.wait()
     for copy in x_copies.values():
         copy.wait_send()
+    for chunk in range(4):
+        for k in range(1, nf):
+            first_copy(chunk, k).wait_send()
+            for m in range(1, nh):
+                y_copy(chunk, k, m).wait_send()
+                second_copy(chunk, k, m).wait_send()
     for b in range(ns):
         @pl.when(jnp.logical_and(b <= at.z, at.z < ns - 1))
         def _():
@@ -286,24 +374,46 @@
             to_left(b).wait_send()
 
 
-def gather_all(sizes, frames, aw, ew, cw, vec):
+def front_all(sizes, frames, vec, aw, ew, cw):
     nd, nf, ns = sizes
     nh = nd // 2
     rows, width = frames.shape
-    deep = cw.shape[0] * nf
+    shard, full = ew.shape
+    deep = cw.shape[0]
+    every = rows * ns
     dma = pltpu.SemaphoreType.DMA
+    anywhere = pl.BlockSpec(memory_space=pl.ANY)
     return pl.pallas_call(
-        functools.partial(gather_kernel, sizes),
+        functools.partial(front_kernel, sizes),
         out_shape=(
             jax.ShapeDtypeStruct((4, width, width), BF),
-            jax.ShapeDtypeStruct((width, ew.shape[1]), BF),
-            jax.ShapeDtypeStruct((deep, width), BF),
-            jax.ShapeDtypeStruct((nf, 16, vec.shape[1]), BF),
-            jax.ShapeDtypeStruct((rows * ns, width), BF),
+            jax.ShapeDtypeStruct((width, full), BF),
+            jax.ShapeDtypeStruct((deep * nf, width), BF),
+            jax.ShapeDtypeStruct((16, width), F32),
+            jax.ShapeDtypeStruct((width, every), BF),
+            jax.ShapeDtypeStruct((rows, width), BF),
+            jax.ShapeDtypeStruct((every, width), BF),
+            jax.ShapeDtypeStruct((every, width), BF),
+            jax.ShapeDtypeStruct((rows, width), F32),
+            jax.ShapeDtypeStruct((width // 128, rows, 128), F32),
         ),
-        in_specs=[vmem()] * 5,
-        out_specs=(vmem(),) * 5,
+        in_specs=[vmem(), vmem(), anywhere, anywhere, anywhere],
+        out_specs=(anywhere, anywhere, anywhere, vmem()) + (anywhere,) * 5 + (vmem(),),
         scratch_shapes=[
+            pltpu.VMEM((4, width, width), BF),
+            pltpu.VMEM((nf, 16, vec.shape[1]), BF),
+            pltpu.VMEM((every, width), BF),
+            pltpu.VMEM((width, every), BF),
+            pltpu.VMEM((rows, width), BF),
+            pltpu.VMEM((every, width), BF),
+            pltpu.VMEM((every, width), BF),
+            pltpu.VMEM((rows, width), F32),
+            pltpu.VMEM((4, shard, width), F32),
+            pltpu.VMEM((shard, full), F32),
+            pltpu.VMEM((deep, width), F32),
+            pltpu.VMEM((shard, full), BF),
+            pltpu.VMEM((deep, width), BF),
+            dma((12,)),
             dma((4, nf)), dma((4, nf)),
             dma((4, nf, nh)), dma((4, nf, nh)),
             dma((4, nf)), dma((4, nf)),
@@ -311,53 +421,11 @@
             dma((nf,)), dma((nf,)),
             dma((ns,)), dma((ns,)), dma((ns,)),
         ],
-        name="gather",
+        name="front",
         compiler_params=pltpu.CompilerParams(
-            collective_id=0, has_side_effects=True, vmem_limit_bytes=VMEM_LIMIT
+            collective_id=0, has_side_effects=True, vmem_limit_bytes=67043328
         ),
-    )(frames, aw, ew, cw, vec)
-
-
-def attention_kernel(chunk, q_ref, k_ref, v_ref, ctx_ref, lse_ref):
-    rows = q_ref.shape[0]
-    lo = lax.broadcasted_iota(jnp.int32, (chunk, 128), 1) < 64
-
-    def pair(p, carry):
-        col = pl.ds(pl.multiple_of(p * 128, 128), 128)
-        k2 = k_ref[:, col]
-        v2 = v_ref[:, col]
-        for c in range(rows // chunk):
-            part = pl.ds(c * chunk, chunk)
-            q2 = q_ref[part, col]
-            ctx, lse = [], []
-            for h in range(2):
-                mask = lo if h == 0 else jnp.logical_not(lo)
-                s = nt(jnp.where(mask, q2, jnp.zeros_like(q2)), k2) * score_scale
-                largest = jnp.max(s, axis=-1, keepdims=True)
-                e = jnp.exp(s - largest)
-                total = jnp.sum(e, axis=-1, keepdims=True)
-                ctx.append(nn((e * (1.0 / total)).astype(BF), v2))
-                lse.append(largest + jnp.log(total))
-            ctx_ref[part, col] = jnp.where(lo, ctx[0], ctx[1])
-            lse_ref[p, part, :] = jnp.where(lo, lse[0], lse[1])
-        return carry
-
-    lax.fori_loop(0, q_ref.shape[1] // 128, pair, 0)
-
-
-def attention(q, k, v):
-    rows, width = q.shape
-    return pl.pallas_call(
-        functools.partial(attention_kernel, rows),
-        out_shape=(
-            jax.ShapeDtypeStruct((rows, width), F32),
-            jax.ShapeDtypeStruct((width // 128, rows, 128), F32),
-        ),
-        in_specs=[vmem()] * 3,
-        out_specs=(vmem(), vmem()),
-        name="attention",
-        compiler_params=pltpu.CompilerParams(vmem_limit_bytes=VMEM_LIMIT),
-    )(q, k, v)
+    )(frames, vec, aw, ew, cw)
 
 
 def back_kernel(
@@ -982,66 +1050,6 @@
     )(ctx, frames, cot, vec, aw, ew, cw)
 
 
-def adam_kernel(parts, g_ref, *refs):
-    step = pl.program_id(0)
-    for i, group in enumerate((2, 1, 0)):
-        w_ref, m_ref, v_ref = refs[3 * i : 3 * i + 3]
-        go_ref, wo_ref, mo_ref, vo_ref = refs[9 + 4 * i : 13 + 4 * i]
-
-        @pl.when(step // parts == i)
-        def _():
-            gradient = g_ref[...].astype(F32)
-            go_ref[...] = gradient
-            wo_ref[...], mo_ref[...], vo_ref[...] = adam_update(
-                w_ref[...], gradient, m_ref[...], v_ref[...], rate_matrix, decay_matrix
-            )
-
-
-def adam_all(out, arrays):
-    shard, width = out.shape[3:]
-    rows = 96 if shard % 96 == 0 else shard
-    deep = shard // rows
-    parts = 4 * deep
-
-    def local(step, i):
-        t = jnp.clip(step - i * parts, 0, parts - 1)
-        return t // deep, lax.rem(t, deep)
-
-    def g_map(step):
-        i = step // parts
-        t = step - i * parts
-        u = t // deep
-        return 2 - i, u // 2, lax.rem(u, 2), lax.rem(t, deep), 0
-
-    def map_of(i):
-        def rows_map(step):
-            u, r = local(step, i)
-            return u * deep + r, 0
-
-        def cols_map(step):
-            u, r = local(step, i)
-            return r, u
-
-        return cols_map if i == 1 else rows_map
-
-    in_specs = [pl.BlockSpec((None, None, None, rows, width), g_map)]
-    out_specs, shapes = [], []
-    for i in range(3):
-        spec = pl.BlockSpec((rows, width), map_of(i))
-        in_specs += [spec] * 3
-        out_specs += [spec] * 4
-        shapes += [jax.ShapeDtypeStruct(arrays[i][0].shape, F32)] * 4
-    return pl.pallas_call(
-        functools.partial(adam_kernel, parts),
-        grid=(3 * parts,),
-        out_shape=tuple(shapes),
-        in_specs=in_specs,
-        out_specs=tuple(out_specs),
-        name="adam",
-        compiler_params=pltpu.CompilerParams(vmem_limit_bytes=67043328),
-    )(out, *[each for group in arrays for each in group])
-
-
 def on_device(
     sizes,
     frames_in,
@@ -1065,16 +1073,9 @@
     rows, width = frames.shape
     shard = attention_weight.shape[1]
     full = expand_weight.shape[1]
-    vec_pad = jnp.pad(vectors, ((0, 4), (0, 0)))
-    aw, ew, cw, vw, h_all = gather_all(
-        sizes, frames, attention_weight, expand_weight, contract_weight, vec_pad
+    aw, ew, cw, vec, h_turned, queries, key_rows, value_rows, context_wide, log_total = front_all(
+        sizes, frames, vectors, attention_weight, expand_weight, contract_weight
     )
-    vec = jnp.transpose(vw, (1, 0, 2)).reshape(16, width).astype(F32)
-    h_own = lax.dynamic_slice_in_dim(h_all, lax.axis_index("seq") * rows, rows, 0)
-    queries = (nn(h_own, aw[0]) + vec[2]).astype(BF)
-    key_rows = nn(h_all, aw[1]).astype(BF)
-    value_rows = (nn(h_all, aw[2]) + vec[3]).astype(BF)
-    context_wide, log_total = attention(queries, key_rows, value_rows)
     frames_out, grad_middle, grad_context, grad_expand, grad_contract, grad_output_w, gv = feed_all(
         context_wide, frames, upstream, vec, aw, ew, cw
     )
@@ -1086,7 +1087,7 @@
         grad_context,
         context_wide,
         log_total,
-        h_all.T,
+        h_turned,
         aw,
         grad_middle,
         frames,
@@ -1099,17 +1100,20 @@
     owned_vec = lax.dynamic_slice_in_dim(
         gv_sum[:12], lax.axis_index("fsdp") * (width // nf), width // nf, 1
     )
-    flat = (4 * shard, width)
-    done = adam_all(
-        out,
-        (
-            [x.reshape(flat) for x in (attention_weight, first_attention, second_attention)],
-            [expand_weight, first_expand, second_expand],
-            [contract_weight, first_contract, second_contract],
-        ),
+    owned = (
+        out[2].reshape(4, shard, width).astype(F32),
+        jnp.transpose(out[1].reshape(4, shard, width), (1, 0, 2)).reshape(shard, full).astype(F32),
+        out[0].reshape(4 * shard, width).astype(F32),
     )
-    attention_out = [each.reshape(attention_weight.shape) for each in done[:4]]
-    expand_out, contract_out = done[4:8], done[8:]
+    attention_out = (owned[0],) + adam_update(
+        attention_weight, owned[0], first_attention, second_attention, rate_matrix, decay_matrix
+    )
+    expand_out = (owned[1],) + adam_update(
+        expand_weight, owned[1], first_expand, second_expand, rate_matrix, decay_matrix
+    )
+    contract_out = (owned[2],) + adam_update(
+        contract_weight, owned[2], first_contract, second_contract, rate_matrix, decay_matrix
+    )
     vector_out = (owned_vec,) + adam_update(
         vectors, owned_vec, first_vectors, second_vectors, rate_vector, 0.0
     )

time: 364 us -> 321 us (0.88); the launches traced: 362 us -> 315 us
  Pallas kernels: 337 us -> 271 us
  other arithmetic: 2.19 us -> 32.3 us
  matrix products: 13.1 us -> 0 us
    pallas_call x3 -> x1, Pallas kernels: 147 us -> 79.6 us  [front_all(): pl.pallas_call(functools.partial(front_kernel, sizes), out_shape=(jax.Sha...]
    sub x1 -> x4, other arithmetic: 1.44 us -> 31.7 us  [adam_update(): weight - rate * (first_hat / (jnp.sqrt(second_hat) + adam_eps) + decay *...]
    dot_general x3 -> x0, matrix products: 13.1 us -> none  [nn(): lax.dot_general(left, right, (((1,), (0,)), ((), ())), preferred_element_...]
    pallas_call x1 -> x0, local copies, waits for them, and re-layouts: 4.27 us -> none  [gather_all(): pl.pallas_call(functools.partial(gather_kernel, sizes), out_shape=(jax.Sh...]
    slice x1, local copies, waits for them, and re-layouts: 0.03 us -> 3.71 us  [on_device(): out[0].reshape(4 * shard, width).astype(F32)]
where the time goes in v4:
time: 321 us; the launch traced here: 315 us
  Pallas kernels  271 us (84%)
  other arithmetic  32.3 us (10%)
  local copies, waits for them, and re-layouts  9.66 us (3%)
    pallas_call x1, Pallas kernels, back_all(): pl.pallas_call(functools.partial(back_kernel, sizes), out_shape=(jax.Shap...  168 us
    pallas_call x1, Pallas kernels, front_all(): pl.pallas_call(functools.partial(front_kernel, sizes), out_shape=(jax.Sha...  79.6 us
    sub x4, other arithmetic, adam_update(): weight - rate * (first_hat / (jnp.sqrt(second_hat) + adam_eps) + decay *...  31.7 us
    pallas_call x1, Pallas kernels, feed_all(): pl.pallas_call(feed_kernel, grid=(blocks,), out_shape=(jax.ShapeDtypeStru...  23.5 us

profile of v4, /device:TPU:0, one launch (start us, length us, event | category | flops | bytes accessed | tf_op | source)
XLA Modules:
  0.0 314.5 jit_solution(1105440150264901012)
XLA Ops:
  0.7 79.6 %front.1 = (bf16[4,768,768]{2,1,0:T(8,128)(2,1)}, bf16[768,3072]{1,0:T(8,128)(2,1)}, bf16[3072,768]{1,0:T(8,128)(2,1)}, f32[16,768]{1,0:T(8,128)}, bf16[768,1536...) custom-call(f32[384,768]{1,0:T(8,128)} %bitcast.27, ...), custom_call_target="tpu_custom_call" | custom-call | tf_op jit(solution)/shard_map/front/pallas_call | solution.py:386
  80.2 23.5 %feed.1 = (f32[384,768]{1,0:T(8,128)}, f32[384,768]{1,0:T(8,128)}, bf16[384,768]{1,0:T(8,128)(2,1)}, bf16[768,3072]{1,0:T(8,128)(2,1)}, bf16[3072,768]{1,0:T(8,1...) custom-call(f32[384,768]{1,0:T(8,128)} %get-tuple-element.38.ctx_ref, f32[384,768]{1,0:T(8,128)} %bitcast.28, ...), custom_call_target="tpu_custom_call" | custom-call | tf_op jit(solution)/shard_map/feed/pallas_call | solution.py:1016
  103.8 168.2 %back.1 = (bf16[3,2,2,384,768]{4,3,2,1,0:T(8,128)(2,1)}, f32[384,768]{1,0:T(8,128)}, f32[16,768]{1,0:T(8,128)}) custom-call(bf16[384,768]{1,0:T(8,128)(2,1)} %get-tuple-element.44.q_ref, bf16[1536,768]{1,0:T(8,128)(2,1)} %get-tuple-element.45.k_ref, bf16[1536,768]{1,0:T(8,128)(2,1)} %get-tuple-element.46.v_ref, bf16[384,768]{1,0:T(8,128)(2,1)} %get-tuple-element.47.dc_ref, ...), custom_call_target="tpu_custom_call" | custom-call | tf_op jit(solution)/shard_map/back/pallas_call | solution.py:914
  272.0 0.0 slice-start.4
  272.0 3.7 %fusion.8 = (bf16[1,2,2,384,768]{4,3,2,1,0:T(8,128)(2,1)S(1)}, bf16[1,2,2,384,768]{4,3,2,1,0:T(8,128)(2,1)S(1)}, bf16[1,2,2,384,768]{4,3,2,1,0:T(8,128)(2,1)S(1)}) fusion(bf16[3,2,2,384,768]{4,3,2,1,0:T(8,128)(2,1)} %get-tuple-element.56), kind=kLoop, calls=%fused_computation.20 | loop fusion | bytes 14155776 | tf_op jit(solution)/shard_map/slice | solution.py:1106
  275.8 0.0 slice-start.5
  275.8 10.4 %multiply_subtract_fusion.2 = (f32[4,384,768]{2,1,0:T(8,128)}, f32[4,384,768]{2,1,0:T(8,128)}, f32[4,384,768]{2,1,0:T(8,128)}, f32[4,384,768]{2,1,0:T(8,128)}) fusion(f32[4,384,768]{2,1,0:T(8,128)} %aw_ref.1, f32[4,384,768]{2,1,0:T(8,128)} %param.20, f32[4,384,768]{2,1,0:T(8,128)} %param.24, bf16[1,2,2,384,768]{4,3,2,1,0:T(8,128)(2,1)S(1)} %get-tuple-element.75), kind=kLoop, calls=%fused_computation.11 | loop fusion | flops 18874368 | bytes 35389440 | tf_op jit(solution)/shard_map/sub | solution.py:63
  286.2 0.0 slice-start
  286.2 0.0 slice-start.2
  286.2 0.5 convert_bitcast_fusion
  286.7 0.0 slice-start.1
  286.8 0.0 slice-start.3
  286.8 3.1 copy.33
  289.8 0.0 slice-done.4
  289.8 0.0 slice-done.5
  289.9 0.0 slice-done
  289.9 1.5 slice-done.2
  291.3 0.2 slice-done.1
  291.5 0.2 slice-done.3
  291.7 0.0 copy-start.1
  291.7 0.0 copy-start.2
  291.7 0.0 copy-start.3
  291.7 0.0 copy-start.4
  291.7 8.1 %multiply_subtract_fusion = (f32[1536,768]{1,0:T(8,128)}, f32[1536,768]{1,0:T(8,128)}, f32[1536,768]{1,0:T(8,128)}, f32[1536,768]{1,0:T(8,128)}) fusion(f32[1536,768]{1,0:T(8,128)S(1)} %bitcast.24, f32[1536,768]{1,0:T(8,128)S(1)} %bitcast.31, f32[1536,768]{1,0:T(8,128)S(1)} %bitcast.33, bf16[1,2,2,384,768]{4,3,2,1,0:T(8,128)(2,1)S(1)} %get-tuple-element.73), kind=kLoop, calls=%fused_computation.7 | loop fusion | flops 18874368 | bytes 35389440 | tf_op jit(solution)/shard_map/sub | solution.py:63
  299.8 0.0 copy-done.1
  299.8 0.0 copy-done.2
  299.8 0.0 copy-done.3
  299.8 0.0 copy-done.4
  299.9 0.6 multiply_subtract_fusion.3
  300.5 0.0 copy-start
  300.5 12.6 %multiply_subtract_fusion.1 = (f32[384,3072]{1,0:T(8,128)}, f32[384,3072]{1,0:T(8,128)}, f32[384,3072]{1,0:T(8,128)}) fusion(f32[384,3072]{1,0:T(8,128)} %ew_ref.1, f32[384,3072]{1,0:T(8,128)} %bitcast.25, f32[384,3072]{1,0:T(8,128)} %param.21, f32[384,3072]{1,0:T(8,128)} %param.25), kind=kLoop, calls=%fused_computation.9 | loop fusion | flops 17694720 | bytes 33030144 | tf_op jit(solution)/shard_map/sub | solution.py:63
  313.1 0.0 copy-done
  313.1 1.0 copy.35
  (3 shorter events, 0.0 us)
Async XLA Ops:
  272.0 17.8 %slice-start.4 = ((s8[4718592]{0:T(1024)(128)(4,1)}), s8[4194304]{0:T(1024)(128)(4,1)S(1)}, s32[]{:S(2)}) async-start(s8[4718592]{0:T(1024)(128)(4,1)} %bitcast.32), calls=%async_computation.4 | async-start | bytes 8388608
  275.8 14.1 %slice-start.5 = ((s8[4718592]{0:T(1024)(128)(4,1)}), s8[524288]{0:T(1024)(128)(4,1)S(1)}, s32[]{:S(2)}) async-start(s8[4718592]{0:T(1024)(128)(4,1)} %bitcast.32), calls=%async_computation.5 | async-start | bytes 1048576
  286.2 3.7 %slice-start = ((s8[4718592]{0:T(1024)(128)(4,1)}), s8[4194304]{0:T(1024)(128)(4,1)S(1)}, s32[]{:S(2)}) async-start(s8[4718592]{0:T(1024)(128)(4,1)} %bitcast.23), calls=%async_computation | async-start | bytes 8388608
  286.2 5.2 %slice-start.2 = ((s8[4718592]{0:T(1024)(128)(4,1)}), s8[4194304]{0:T(1024)(128)(4,1)S(1)}, s32[]{:S(2)}) async-start(s8[4718592]{0:T(1024)(128)(4,1)} %bitcast.30), calls=%async_computation.2 | async-start | bytes 8388608
  286.7 4.8 %slice-start.1 = ((s8[4718592]{0:T(1024)(128)(4,1)}), s8[524288]{0:T(1024)(128)(4,1)S(1)}, s32[]{:S(2)}) async-start(s8[4718592]{0:T(1024)(128)(4,1)} %bitcast.23), calls=%async_computation.1 | async-start | bytes 1048576
  286.8 4.9 %slice-start.3 = ((s8[4718592]{0:T(1024)(128)(4,1)}), s8[524288]{0:T(1024)(128)(4,1)S(1)}, s32[]{:S(2)}) async-start(s8[4718592]{0:T(1024)(128)(4,1)} %bitcast.30), calls=%async_computation.3 | async-start | bytes 1048576
  291.7 8.2 %copy-start.1 = (f32[12,384]{1,0:T(8,128)S(1)}, f32[12,384]{1,0:T(8,128)}, u32[]{:S(2)}) copy-start(f32[12,384]{1,0:T(8,128)} %vec_ref.1) | copy-start | bytes 55300
  291.7 8.2 %copy-start.2 = (f32[12,384]{1,0:T(8,128)S(1)}, f32[12,384]{1,0:T(8,128)}, u32[]{:S(2)}) copy-start(f32[12,384]{1,0:T(8,128)} %param.23) | copy-start | bytes 55300
  291.7 8.2 %copy-start.3 = (f32[12,384]{1,0:T(8,128)S(1)}, f32[12,384]{1,0:T(8,128)}, u32[]{:S(2)}) copy-start(f32[12,384]{1,0:T(8,128)} %param.27) | copy-start | bytes 55300
  291.7 8.2 %copy-start.4 = (f32[16,768]{1,0:T(8,128)S(1)}, f32[16,768]{1,0:T(8,128)}, u32[]{:S(2)}) copy-start(f32[16,768]{1,0:T(8,128)} %get-tuple-element.57) | copy-start | bytes 147460
  300.5 12.6 %copy-start = (f32[384,768]{1,0:T(8,128)S(1)}, f32[384,768]{1,0:T(8,128)}, u32[]{:S(2)}) copy-start(f32[384,768]{1,0:T(8,128)} %get-tuple-element.55) | copy-start | bytes 3538948
